TPU v7x, 256 devices: a whole 4x4x8 slice. The times are simulated.
256 devices in a mesh: expert: 8 (over z), neuron: 32 (over y, x, core).
Axes of the slice: x: 4, y: 4, z: 8, core: 2. Of those that a mesh axis runs over, the one named last changes fastest.
Arguments:
- tokens: bfloat16 [1024, 4096], P('neuron'), may hold values from -6 to 6
- route_logits: float32 [1024, 2], replicated, may hold values from -6 to 6
- expert_ids: int32 [1024, 2], replicated, may hold values from 0 to 7, all different within a row; in each aligned block of 1024 rows (0 to 1023, 1024 to 2047, ...) at most 512 rows name the same one
- block_live: int32 [8, 224], P('expert', 'neuron'), may hold values 0 or 1
- w_gate: bfloat16 [8, 4096, 14336], P('expert', None, 'neuron'), may hold values from -0.09375 to 0.09375
- w_up: bfloat16 [8, 4096, 14336], P('expert', None, 'neuron'), may hold values from -0.09375 to 0.09375
- w_down: bfloat16 [8, 14336, 4096], P('expert', 'neuron'), may hold values from -0.046875 to 0.046875
Outputs:
- mixed: bfloat16 [1024, 4096], P('neuron')
Inputs may be any that keep to these rules, and one draw needn't show every extreme that they name: `expert_ids`: each token names two different experts; no expert is named by more than 512 tokens, a bound that some block reaches; every expert is named.
All inputs are finite; a program needn't handle non-finite values. No bound on the sum of `block_live` on one device may be relied on, other than what follows from the above.
Results may differ from a plain program's by a relative error of at most 0.0049.
Values may be sent and summed in bfloat16 or wider, within the bound.
No kernel may reach another device: no remote copies, remote signals or barrier semaphores. Data moves between devices by JAX's collectives and lax.ppermute only.
A program may use at most 128 MiB of HBM per device.

v0:
```python
import jax
import jax.numpy as jnp
from jax import lax
from jax.experimental import pallas as pl
from jax.experimental.pallas import tpu as pltpu
from jax.sharding import PartitionSpec as P


BLK = 64
RING = 4


def device(y, x, c):
    return ((y % RING) * RING + x % RING) * 2 + c


PLACES = [(y, x, c) for y in range(RING) for x in range(RING) for c in range(2)]
PARTNER = [(device(y, x, c), device(y, x, 1 - c)) for y, x, c in PLACES]


def from_x(d):
    return [(device(y, x + d, c), device(y, x, c)) for y, x, c in PLACES]


def from_y(d):
    return [(device(y + d, x, c), device(y, x, c)) for y, x, c in PLACES]


def to_x(d):
    return [(device(y, x, c), device(y, x + d, c)) for y, x, c in PLACES]


def to_y(d):
    return [(device(y, x, c), device(y + d, x, c)) for y, x, c in PLACES]


def ring_steps(by_x, by_y, perm_x, perm_y):
    got_x, got_y = {0: by_x[0]}, {0: by_y[0]}
    for d in STEPS:
        got_x[d] = lax.ppermute(by_x[d], "neuron", perm_x(d))
        got_y[d] = lax.ppermute(by_y[d], "neuron", perm_y(d))
    return [got_x[k] for k in range(RING)], [got_y[k] for k in range(RING)]


def ring_gather(by_x, by_y):
    return ring_steps([by_x] * RING, [by_y] * RING, from_x, from_y)


def ring_scatter(by_x, by_y):
    return ring_steps(by_x, by_y, to_x, to_y)


STEPS = (2, 1, 3)


def mm(a, b):
    return jnp.dot(a, b, preferred_element_type=jnp.float32)


def mm_t(a, b):
    return lax.dot_general(a, b, (((1,), (1,)), ((), ())), preferred_element_type=jnp.float32)


LIMIT = pltpu.CompilerParams(vmem_limit_bytes=20 * 2**20)


def whole(*arrays):
    return [pl.BlockSpec(a.shape, lambda i, s, n=len(a.shape): (0,) * n) for a in arrays]


def call(body, place, ins, specs, outs, scratch=(), flops=10**9, steps=1):
    return pl.pallas_call(
        body,
        grid_spec=pltpu.PrefetchScalarGridSpec(
            num_scalar_prefetch=1, grid=(steps,), in_specs=specs, out_specs=whole(*outs), scratch_shapes=list(scratch)
        ),
        out_shape=outs,
        compiler_params=LIMIT,
        cost_estimate=pl.CostEstimate(flops=flops, bytes_accessed=4 * 2**20, transcendentals=0),
    )(place, *ins)


def rows_kernel(place, mine, theirs, to_x_rows, to_y_rows):
    rows, span = mine.shape[0], to_x_rows.shape[1]
    for source, core in ((mine, place[0]), (theirs, 1 - place[0])):
        at = pl.ds(pl.multiple_of(core * rows, rows), rows)
        to_x_rows[at, :] = source[:, :span]
        to_y_rows[at, :] = source[:, span:]


def lines_kernel(place, *refs):
    for refs_in, out, start in ((refs[:RING], refs[-2], place[1]), (refs[RING:-2], refs[-1], place[2])):
        rows = refs_in[0].shape[0]
        for k in range(RING):
            out[pl.ds(pl.multiple_of((start + k) % RING * rows, rows), rows), :] = refs_in[k][...]


def routing_kernel(place, ids, logits, slots, slots_t, weight, spread):
    total_tokens, capacity = spread.shape
    lanes = 128
    first, second = (jnp.where(ids[k : k + 1, :] == place[3], 1.0, 0.0) for k in range(2))
    lead = 1.0 / (1.0 + jnp.exp(logits[1:2, :] - logits[0:1, :]))
    share = first * lead + second * (1.0 - lead)
    chosen = first + second
    chunks = [chosen[:, k : k + lanes] for k in range(0, total_tokens, lanes)]
    grid = jnp.concatenate(chunks, axis=0)
    earlier = lax.broadcasted_iota(jnp.int32, (lanes, lanes), 0) < lax.broadcasted_iota(jnp.int32, (lanes, lanes), 1)
    before = mm(grid.astype(jnp.bfloat16), jnp.where(earlier, 1.0, 0.0).astype(jnp.bfloat16))
    offset = jnp.zeros((1, 1), jnp.float32)
    out = []
    for k, chunk in enumerate(chunks):
        out.append(jnp.where(chunk > 0.0, before[k : k + 1, :] + offset, float(capacity)))
        offset = offset + jnp.sum(chunk, axis=1, keepdims=True)
    slot = jnp.concatenate(out, axis=1).astype(jnp.int32)
    slots[...] = slot
    per_chip = total_tokens // RING // RING
    slots_t[...] = jnp.concatenate(
        [slot[:, (y * RING + x) * per_chip : (y * RING + x + 1) * per_chip] for x in range(RING) for y in range(RING)], axis=1
    )
    hit = slot == lax.broadcasted_iota(jnp.int32, (capacity, total_tokens), 0)
    weight[...] = jnp.sum(jnp.where(hit, share, 0.0), axis=1, keepdims=True)
    planes, own = place_counts(total_tokens)
    each, part = own // planes, total_tokens // planes
    step = 256
    for top in range(0, total_tokens, step):
        row = lax.broadcasted_iota(jnp.int32, (step, total_tokens), 0) + top
        token = row % part // each * own + row // part * each + row % each
        column = lax.broadcasted_iota(jnp.int32, (step, total_tokens), 1)
        mine = jnp.sum(jnp.where(token == column, slot.astype(jnp.float32), 0.0), axis=1, keepdims=True)
        index = lax.broadcasted_iota(jnp.int32, (step, capacity), 1)
        spread[top : top + step, :] = jnp.where(mine.astype(jnp.int32) == index, 1.0, 0.0).astype(jnp.bfloat16)


def place_counts(total_tokens):
    return 8, total_tokens // len(PLACES)


def dispatch_kernel(place, slots, slots_t, *refs):
    blocks, out = refs[:-1], refs[-1]
    rows, span = blocks[0].shape
    capacity = out.shape[0]
    index = lax.broadcasted_iota(jnp.int32, (capacity, rows), 0)
    for side, (lines, start) in enumerate(((slots, place[2]), (slots_t, place[1]))):
        hot = []
        for k in range(RING):
            line = lines[:, pl.ds(pl.multiple_of((start + k) % RING * rows, rows), rows)]
            hot.append(jnp.where(line == index, 1.0, 0.0).astype(jnp.bfloat16))
        for n in range(0, span, 256):
            acc = mm(hot[0], blocks[side * RING][:, n : n + 256])
            for k in range(1, RING):
                acc = acc + mm(hot[k], blocks[side * RING + k][:, n : n + 256])
            out[:, side * span + n : side * span + n + 256] = acc.astype(jnp.bfloat16)


def near_kernel(place, rows, gate, up, gate_out, up_out):
    @pl.when(pl.program_id(0) == 0)
    def _():
        gate_out[...] = mm_t(rows[...], gate[...])
        up_out[...] = mm_t(rows[...], up[...])

    @pl.when(pl.program_id(0) > 0)
    def _():
        gate_out[...] += mm_t(rows[...], gate[...])
        up_out[...] += mm_t(rows[...], up[...])


def far_kernel(place, rows, gate, up, gate_near, up_near, live, out, gate_sum, up_sum):
    @pl.when(pl.program_id(0) == 0)
    def _():
        gate_sum[...] = gate_near[...] + mm_t(rows[...], gate[...])
        up_sum[...] = up_near[...] + mm_t(rows[...], up[...])

    @pl.when(pl.program_id(0) > 0)
    def _():
        gate_sum[...] += mm_t(rows[...], gate[...])
        up_sum[...] += mm_t(rows[...], up[...])

    @pl.when(pl.program_id(0) == pl.num_programs(0) - 1)
    def _():
        gate_val = gate_sum[...]
        block = lax.broadcasted_iota(jnp.int32, (1, out.shape[1]), 1) // BLK
        kept = jnp.zeros((1, out.shape[1]), jnp.float32)
        for k in range(out.shape[1] // BLK):
            kept = jnp.where(block == k, live[0, k].astype(jnp.float32), kept)
        out[...] = (gate_val / (1.0 + jnp.exp(-gate_val)) * up_sum[...] * kept).astype(jnp.bfloat16)


def down_kernel(place, near, far, w_near, w_far, weight, *refs):
    to_x_refs, to_y_refs, part = refs[:RING], refs[RING : 2 * RING], refs[-1]
    x, y = place[1], place[2]
    rows, span = to_x_refs[0].shape
    col = span // RING
    for e in range(RING):
        at = (y + e) % RING
        cols = pl.ds(pl.multiple_of(at * span, span), span)
        value = mm(near[...], w_near[:, cols]) + mm(far[...], w_far[:, cols])
        value = (value * weight[...]).astype(jnp.bfloat16)
        to_y_refs[e][...] = value[rows:]
        part[...] = value[:rows]
        for d in range(RING):
            block = part[:, pl.ds(pl.multiple_of((x + d) % RING * col, col), col)]
            to_x_refs[d][:, pl.ds(pl.multiple_of(at * col, col), col)] = block


def total(refs):
    value = refs[0][...].astype(jnp.float32)
    for r in refs[1:]:
        value = value + r[...].astype(jnp.float32)
    return value


def middle_kernel(place, *refs):
    got_x, got_y = refs[:RING], refs[RING : 2 * RING]
    to_y_refs, to_x_refs, part = refs[2 * RING : 3 * RING], refs[3 * RING : 4 * RING], refs[-1]
    col = to_y_refs[0].shape[1]
    for got, outs, start in ((got_x, to_y_refs, place[2]), (got_y, to_x_refs, place[1])):
        part[...] = total(got).astype(jnp.bfloat16)
        for k in range(RING):
            outs[k][...] = part[:, pl.ds(pl.multiple_of((start + k) % RING * col, col), col)]


def last_kernel(place, spread, *refs):
    got_y, got_x, out = refs[:RING], refs[RING : 2 * RING], refs[-1]
    rows = got_y[0].shape[0]
    value = mm(spread[:, :rows], total(got_y).astype(jnp.bfloat16))
    value = value + mm(spread[:, rows:], total(got_x).astype(jnp.bfloat16))
    out[...] = value.astype(jnp.bfloat16)


def per_device(planes, tokens, route_logits, expert_ids, block_live, w_gate, w_up, w_down):
    total_tokens = expert_ids.shape[0]
    own_tokens, width = tokens.shape
    capacity = total_tokens // 2
    sites = RING * RING
    members = 2 * sites
    share = own_tokens // planes
    half = width // 2
    col = half // sites
    place = lax.axis_index("neuron")
    core, x, y = place % 2, place // 2 % RING, place // (2 * RING)
    where = jnp.stack([core, x, y, lax.axis_index("expert")]).astype(jnp.int32)
    where, tokens = lax.optimization_barrier((where, tokens))
    shape = jax.ShapeDtypeStruct
    quarter = half // 2
    units = w_gate.shape[2]
    bf16 = jnp.bfloat16

    theirs = lax.ppermute(tokens, "neuron", PARTNER)
    own_half = pl.BlockSpec((own_tokens, half), lambda i, s: (0, s[0]))
    chip_rows = call(
        rows_kernel, where, (tokens, theirs), [own_half, own_half], [shape((2 * own_tokens, quarter), bf16)] * 2
    )
    *chip_rows, w_down, expert_ids, route_logits = lax.optimization_barrier((*chip_rows, w_down, expert_ids, route_logits))
    first_x, first_y = ring_gather(*chip_rows)
    down_far = lax.ppermute(w_down[0], "neuron", PARTNER)
    ins = (expert_ids.T, route_logits.T)
    routed = call(
        routing_kernel, where, ins, whole(*ins),
        [shape((1, total_tokens), jnp.int32)] * 2
        + [shape((capacity, 1), jnp.float32), shape((total_tokens, capacity), bf16)],
    )
    ins = (*first_x, *first_y)
    lines = call(lines_kernel, where, ins, whole(*ins), [shape((2 * RING * own_tokens, quarter), bf16)] * 2)
    line_x, line_y, *routed = lax.optimization_barrier((*lines, *routed))
    second_x, second_y = ring_gather(line_y, line_x)
    slots, slots_t, slot_weight, spread = routed

    ins = (slots, slots_t, *second_y, *second_x)
    near_in = call(
        dispatch_kernel, where, ins, whole(*ins), [shape((capacity, half), bf16)], flops=2 * capacity * total_tokens * half
    )[0]
    far_in = lax.ppermute(near_in, "neuron", PARTNER)
    gate, up = w_gate[0].T, w_up[0].T
    steps = 4
    cut = half // steps
    slab = pl.BlockSpec((capacity, cut), lambda i, s: (0, i))
    near_cut = pl.BlockSpec((units, cut), lambda i, s: (0, s[0] * steps + i))
    far_cut = pl.BlockSpec((units, cut), lambda i, s: (0, (1 - s[0]) * steps + i))
    down_half = pl.BlockSpec((units, half), lambda i, s: (0, s[0]))
    sums = call(
        near_kernel, where, (near_in, gate, up), [slab, near_cut, near_cut],
        [shape((capacity, units), jnp.float32)] * 2, flops=4 * capacity * half * units, steps=steps,
    )
    hidden = call(
        far_kernel, where, (far_in, gate, up, *sums, block_live), [slab, far_cut, far_cut, *whole(*sums), pl.BlockSpec(memory_space=pltpu.SMEM)],
        [shape((capacity, units), jnp.bfloat16)], [pltpu.VMEM((capacity, units), jnp.float32)] * 2,
        flops=4 * capacity * half * units, steps=steps,
    )[0]
    hidden_far = lax.ppermute(hidden, "neuron", PARTNER)
    rows = capacity // 2
    span = RING * col
    ins = (hidden, hidden_far, w_down[0], down_far, slot_weight)
    outs = call(
        down_kernel, where, ins,
        [*whole(hidden, hidden_far), down_half, down_half, *whole(slot_weight)],
        [shape((rows, span), jnp.bfloat16)] * (2 * RING), [pltpu.VMEM((rows, span), jnp.bfloat16)],
        flops=4 * capacity * half * units,
    )
    got_x, got_y = ring_scatter(outs[:RING], outs[RING:])
    ins = (*got_x, *got_y)
    outs = call(
        middle_kernel, where, ins, whole(*ins),
        [shape((rows, col), jnp.bfloat16)] * (2 * RING), [pltpu.VMEM((rows, span), jnp.bfloat16)],
    )
    got_x, got_y = ring_scatter(outs[RING:], outs[:RING])
    ins = (spread, *got_y, *got_x)
    placed = call(last_kernel, where, ins, whole(*ins), [shape((total_tokens, col), jnp.bfloat16)])[0]
    over = lax.all_to_all(placed.reshape(planes, members * share, col), "expert", 0, 0, tiled=True)
    mixed = jnp.sum(over.astype(jnp.float32), axis=0).astype(jnp.bfloat16)
    owned = lax.all_to_all(mixed.reshape(members, share, col), "neuron", 0, 0, tiled=True)
    copies = jnp.broadcast_to(owned.reshape(1, members * share, col), (planes, members * share, col))
    every = lax.all_to_all(copies, "expert", 0, 0, tiled=True)
    every = every.reshape(planes, sites, 2, share, col).transpose(0, 3, 2, 1, 4)
    return every.reshape(own_tokens, width)


def solution(mesh):
    placed = (
        P("neuron", None),
        P(),
        P(),
        P("expert", "neuron"),
        P("expert", None, "neuron"),
        P("expert", None, "neuron"),
        P("expert", "neuron", None),
    )

    def body(*args):
        return per_device(mesh.shape["expert"], *args)

    return jax.shard_map(body, mesh=mesh, in_specs=placed, out_specs=P("neuron", None), check_vma=False)
```

profile of v0, /device:TPU:2, one launch (start us, length us, event | category | flops | bytes accessed | tf_op | source)
XLA Modules:
  0.0 157.3 jit_solution(4671234056735503123)
XLA Ops:
  0.1 1.7 %collective-permute-done.theirs = bf16[32,4096]{1,0:T(8,128)(2,1)S(1)} collective-permute-done((bf16[32,4096]{1,0:T(8,128)(2,1)}, bf16[32,4096]{1,0:T(8,128)(2,1)S(1)}, u32[]{:S(2)}, u32[]{:S(2)}) %collective-permute-start) | collective-permute-done | bytes 262176 | tf_op jit(solution)/shard_map/ppermute | solution.py:248
  4.9 2.8 %collective-permute-start.2 = (bf16[64,1024]{1,0:T(8,128)(2,1)S(1)}, bf16[64,1024]{1,0:T(8,128)(2,1)S(1)}, u32[]{:S(2)}, u32[]{:S(2)}) collective-permute-start(bf16[64,1024]{1,0:T(8,128)(2,1)S(1)} %get-tuple-element.48.refs_0_), channel_id=1, source_target_pairs={{4,0},{5,1},{6,2},{7,3},{0,4},{1,5},{2,6},{3,7},{12,8},{13,9},{14,... | collective-permute-start | bytes 393224 | tf_op jit(solution)/shard_map/ppermute | solution.py:40
  9.8 2.9 %collective-permute-start.5 = (bf16[64,1024]{1,0:T(8,128)(2,1)S(1)}, bf16[64,1024]{1,0:T(8,128)(2,1)S(1)}, u32[]{:S(2)}, u32[]{:S(2)}) collective-permute-start(bf16[64,1024]{1,0:T(8,128)(2,1)S(1)} %get-tuple-element.49.refs_4_), channel_id=1, source_target_pairs={{16,0},{17,1},{18,2},{19,3},{20,4},{21,5},{22,6},{23,7},{24,8},{25... | collective-permute-start | bytes 393224 | tf_op jit(solution)/shard_map/ppermute | solution.py:41
  14.0 1.7 %shard_map.75 = (s32[1,1024]{1,0:T(1,128)S(1)}, s32[1,1024]{1,0:T(1,128)S(1)}, f32[512,1]{1,0:T(8,128)S(1)}, bf16[1024,512]{1,0:T(8,128)(2,1)S(1)}) custom-call(s32[4]{0:T(128)S(1)} %pad_add_fusion.place, s32[2,1024]{1,0:T(2,128)S(1)} %bitcast.28, f32[2,1024]{1,0:T(2,128)S(1)} %bitcast.29), custom_call_target="tpu_custom_call" | custom-call | flops 1000000000 | bytes 4194304 | tf_op jit(solution)/shard_map/pallas_call | solution.py:72
  15.8 2.4 %collective-permute-done.5.refs_6_ = bf16[64,1024]{1,0:T(8,128)(2,1)S(1)} collective-permute-done((bf16[64,1024]{1,0:T(8,128)(2,1)S(1)}, bf16[64,1024]{1,0:T(8,128)(2,1)S(1)}, u32[]{:S(2)}, u32[]{:S(2)}) %collective-permute-start.5) | collective-permute-done | bytes 131104 | tf_op jit(solution)/shard_map/ppermute | solution.py:41
  20.0 2.9 %collective-permute-start.8 = (bf16[256,1024]{1,0:T(8,128)(2,1)S(1)}, bf16[256,1024]{1,0:T(8,128)(2,1)S(1)}, u32[]{:S(2)}, u32[]{:S(2)}) collective-permute-start(bf16[256,1024]{1,0:T(8,128)(2,1)S(1)} %get-tuple-element.61.refs_0_), channel_id=1, source_target_pairs={{16,0},{17,1},{18,2},{19,3},{20,4},{21,5},{22,6},{23,7},{24,8},{25... | collective-permute-start | bytes 1572872 | tf_op jit(solution)/shard_map/ppermute | solution.py:41
  24.2 9.4 %collective-permute-done.9.refs_3_ = bf16[256,1024]{1,0:T(8,128)(2,1)S(1)} collective-permute-done((bf16[256,1024]{1,0:T(8,128)(2,1)S(1)}, bf16[256,1024]{1,0:T(8,128)(2,1)S(1)}, u32[]{:S(2)}, u32[]{:S(2)}) %collective-permute-start.9) | collective-permute-done | bytes 524320 | tf_op jit(solution)/shard_map/ppermute | solution.py:41
  34.5 10.5 %collective-permute-done.8.refs_2_ = bf16[256,1024]{1,0:T(8,128)(2,1)S(1)} collective-permute-done((bf16[256,1024]{1,0:T(8,128)(2,1)S(1)}, bf16[256,1024]{1,0:T(8,128)(2,1)S(1)}, u32[]{:S(2)}, u32[]{:S(2)}) %collective-permute-start.8) | collective-permute-done | bytes 524320 | tf_op jit(solution)/shard_map/ppermute | solution.py:41
  46.4 10.7 %collective-permute-done.10.refs_5_ = bf16[256,1024]{1,0:T(8,128)(2,1)S(1)} collective-permute-done((bf16[256,1024]{1,0:T(8,128)(2,1)S(1)}, bf16[256,1024]{1,0:T(8,128)(2,1)S(1)}, u32[]{:S(2)}, u32[]{:S(2)}) %collective-permute-start.10) | collective-permute-done | bytes 524320 | tf_op jit(solution)/shard_map/ppermute | solution.py:40
  57.2 2.9 %shard_map.76.rows = bf16[512,2048]{1,0:T(8,128)(2,1)S(1)} custom-call(s32[4]{0:T(128)S(1)} %pad_add_fusion.place, s32[1,1024]{1,0:T(1,128)S(1)} %get-tuple-element.59.slots, s32[1,1024]{1,0:T(1,128)S(1)} %get-tuple-element.60.slots_t, bf16[256,1024]{1,0:T(8,128)(2,1)S(1)} %get-tuple-element.61.refs_0_, ...), custom_call_target="tpu_custom_call" | custom-call | flops 2147483648 | bytes 4194304 | tf_op jit(solution)/shard_map/pallas_call | solution.py:72
  60.2 4.1 %shard_map.77 = (f32[512,448]{1,0:T(8,128)S(1)}, f32[512,448]{1,0:T(8,128)S(1)}) custom-call(s32[4]{0:T(128)S(1)} %pad_add_fusion.place, bf16[512,2048]{1,0:T(8,128)(2,1)S(1)} %shard_map.76.rows, bf16[448,4096]{1,0:T(8,128)(2,1)S(1)} %bitcast.21, bf16[448,4096]{1,0:T(8,128)(2,1)S(1)} %bitcast.23), custom_call_target="tpu_custom_call" | custom-call | flops 1879048192 | bytes 4194304 | tf_op jit(solution)/shard_map/pallas_call | solution.py:72
  64.3 4.8 %shard_map.78.near = bf16[512,448]{1,0:T(8,128)(2,1)S(1)} custom-call(s32[4]{0:T(128)S(1)} %pad_add_fusion.place, bf16[512,2048]{1,0:T(8,128)(2,1)S(1)} %collective-permute-done.13.rows, bf16[448,4096]{1,0:T(8,128)(2,1)S(1)} %bitcast.22, bf16[448,4096]{1,0:T(8,128)(2,1)S(1)} %bitcast.24, f32[512,448]{1,0:T(8,128)S(1)} %get-tuple-element.63.gate_near, ...), custom_call_target="tpu_custom_call" | custom-call | flops 1879048192 | bytes 4194304 | tf_op jit(solution)/shard_map/pallas_call | solution.py:72
  71.2 3.2 %shard_map.79 = (bf16[256,512]{1,0:T(8,128)(2,1)S(1)}, bf16[256,512]{1,0:T(8,128)(2,1)S(1)}, bf16[256,512]{1,0:T(8,128)(2,1)S(1)}, bf16[256,512]{1,0:T(8,128)(2,...) custom-call(s32[4]{0:T(128)S(1)} %pad_add_fusion.place, ...), custom_call_target="tpu_custom_call" | custom-call | flops 1879048192 | bytes 4194304 | tf_op jit(solution)/shard_map/pallas_call | solution.py:72
  75.8 2.0 %collective-permute-start.17 = (bf16[256,512]{1,0:T(8,128)(2,1)S(1)}, bf16[256,512]{1,0:T(8,128)(2,1)S(1)}, u32[]{:S(2)}, u32[]{:S(2)}) collective-permute-start(bf16[256,512]{1,0:T(8,128)(2,1)S(1)} %get-tuple-element.69), channel_id=1, source_target_pairs={{0,4},{1,5},{2,6},{3,7},{4,0},{5,1},{6,2},{7,3},{8,12},{9,13},{10,... | collective-permute-start | bytes 786440 | tf_op jit(solution)/shard_map/ppermute | solution.py:40
  78.8 2.0 %collective-permute-start.20 = (bf16[256,512]{1,0:T(8,128)(2,1)S(1)}, bf16[256,512]{1,0:T(8,128)(2,1)S(1)}, u32[]{:S(2)}, u32[]{:S(2)}) collective-permute-start(bf16[256,512]{1,0:T(8,128)(2,1)S(1)} %get-tuple-element.73), channel_id=1, source_target_pairs={{0,16},{1,17},{2,18},{3,19},{4,20},{5,21},{6,22},{7,23},{8,24},{9,... | collective-permute-start | bytes 786440 | tf_op jit(solution)/shard_map/ppermute | solution.py:41
  80.8 2.9 %collective-permute-done.16.refs_1_ = bf16[256,512]{1,0:T(8,128)(2,1)S(1)} collective-permute-done((bf16[256,512]{1,0:T(8,128)(2,1)S(1)}, bf16[256,512]{1,0:T(8,128)(2,1)S(1)}, u32[]{:S(2)}, u32[]{:S(2)}) %collective-permute-start.16) | collective-permute-done | bytes 262176 | tf_op jit(solution)/shard_map/ppermute | solution.py:40
  86.6 4.7 %collective-permute-done.18.refs_3_ = bf16[256,512]{1,0:T(8,128)(2,1)S(1)} collective-permute-done((bf16[256,512]{1,0:T(8,128)(2,1)S(1)}, bf16[256,512]{1,0:T(8,128)(2,1)S(1)}, u32[]{:S(2)}, u32[]{:S(2)}) %collective-permute-start.18) | collective-permute-done | bytes 262176 | tf_op jit(solution)/shard_map/ppermute | solution.py:40
  91.3 2.1 %collective-permute-done.19.refs_5_ = bf16[256,512]{1,0:T(8,128)(2,1)S(1)} collective-permute-done((bf16[256,512]{1,0:T(8,128)(2,1)S(1)}, bf16[256,512]{1,0:T(8,128)(2,1)S(1)}, u32[]{:S(2)}, u32[]{:S(2)}) %collective-permute-start.19) | collective-permute-done | bytes 262176 | tf_op jit(solution)/shard_map/ppermute | solution.py:41
  95.6 3.9 %collective-permute-start.23 = (bf16[256,128]{1,0:T(8,128)(2,1)S(1)}, bf16[256,128]{1,0:T(8,128)(2,1)S(1)}, u32[]{:S(2)}, u32[]{:S(2)}) collective-permute-start(bf16[256,128]{1,0:T(8,128)(2,1)S(1)} %get-tuple-element.77), channel_id=1, source_target_pairs={{0,16},{1,17},{2,18},{3,19},{4,20},{5,21},{6,22},{7,23},{8,24},{9,... | collective-permute-start | bytes 196616 | tf_op jit(solution)/shard_map/ppermute | solution.py:41
  100.6 3.7 %collective-permute-start.26 = (bf16[256,128]{1,0:T(8,128)(2,1)S(1)}, bf16[256,128]{1,0:T(8,128)(2,1)S(1)}, u32[]{:S(2)}, u32[]{:S(2)}) collective-permute-start(bf16[256,128]{1,0:T(8,128)(2,1)S(1)} %get-tuple-element.81), channel_id=1, source_target_pairs={{0,4},{1,5},{2,6},{3,7},{4,0},{5,1},{6,2},{7,3},{8,12},{9,13},{10,... | collective-permute-start | bytes 196616 | tf_op jit(solution)/shard_map/ppermute | solution.py:40
  106.5 2.0 %collective-permute-done.27.refs_7_ = bf16[256,128]{1,0:T(8,128)(2,1)S(1)} collective-permute-done((bf16[256,128]{1,0:T(8,128)(2,1)S(1)}, bf16[256,128]{1,0:T(8,128)(2,1)S(1)}, u32[]{:S(2)}, u32[]{:S(2)}) %collective-permute-start.27) | collective-permute-done | bytes 65568 | tf_op jit(solution)/shard_map/ppermute | solution.py:40
  109.5 18.8 %all_to_all.15 = bf16[8,128,128]{2,1,0:T(8,128)(2,1)S(1)} all-to-all(bf16[8,128,128]{2,1,0:T(8,128)(2,1)S(1)} %bitcast.27), channel_id=1, replica_groups=mesh['expert'=8,'neuron'=32] {'expert'}, dimensions={0} | all-to-all | bytes 524288 | tf_op jit(solution)/shard_map/all_to_all | solution.py:308
  128.3 12.9 %all_to_all.16 = bf16[32,4,128]{2,1,0:T(4,128)(2,1)S(1)} all-to-all(bf16[32,4,128]{2,1,0:T(4,128)(2,1)S(1)} %bitcast.31), channel_id=1, replica_groups=mesh['expert'=8,'neuron'=32] {'neuron'}, dimensions={0} | all-to-all | bytes 65536 | tf_op jit(solution)/shard_map/all_to_all | solution.py:310
  141.3 14.8 %all_to_all.17 = bf16[8,128,128]{2,1,0:T(8,128)(2,1)S(1)} all-to-all(bf16[8,128,128]{2,1,0:T(8,128)(2,1)S(1)} %broadcast_in_dim.8), channel_id=1, replica_groups=mesh['expert'=8,'neuron'=32] {'expert'}, dimensions={0} | all-to-all | bytes 524288 | tf_op jit(solution)/shard_map/all_to_all | solution.py:312
  (64 shorter events, 27.3 us)
Async XLA Ops:
  3.4 9.3 %collective-permute-start.3 = (bf16[64,1024]{1,0:T(8,128)(2,1)S(1)}, bf16[64,1024]{1,0:T(8,128)(2,1)S(1)}, u32[]{:S(2)}, u32[]{:S(2)}) collective-permute-start(bf16[64,1024]{1,0:T(8,128)(2,1)S(1)} %get-tuple-element.48.refs_0_), channel_id=1, source_target_pairs={{6,0},{7,1},{0,2},{1,3},{2,4},{3,5},{4,6},{5,7},{14,8},{15,9},{8,1... | collective-permute-start | bytes 393224 | tf_op jit(solution)/shard_map/ppermute | solution.py:40
  4.9 10.8 %collective-permute-start.2 = (bf16[64,1024]{1,0:T(8,128)(2,1)S(1)}, bf16[64,1024]{1,0:T(8,128)(2,1)S(1)}, u32[]{:S(2)}, u32[]{:S(2)}) collective-permute-start(bf16[64,1024]{1,0:T(8,128)(2,1)S(1)} %get-tuple-element.48.refs_0_), channel_id=1, source_target_pairs={{4,0},{5,1},{6,2},{7,3},{0,4},{1,5},{2,6},{3,7},{12,8},{13,9},{14,... | collective-permute-start | bytes 393224 | tf_op jit(solution)/shard_map/ppermute | solution.py:40
  7.8 8.0 %collective-permute-start.1 = (bf16[64,1024]{1,0:T(8,128)(2,1)S(1)}, bf16[64,1024]{1,0:T(8,128)(2,1)S(1)}, u32[]{:S(2)}, u32[]{:S(2)}) collective-permute-start(bf16[64,1024]{1,0:T(8,128)(2,1)S(1)} %get-tuple-element.48.refs_0_), channel_id=1, source_target_pairs={{2,0},{3,1},{4,2},{5,3},{6,4},{7,5},{0,6},{1,7},{10,8},{11,9},{12,... | collective-permute-start | bytes 393224 | tf_op jit(solution)/shard_map/ppermute | solution.py:40
  8.2 7.5 %collective-permute-start.6 = (bf16[64,1024]{1,0:T(8,128)(2,1)S(1)}, bf16[64,1024]{1,0:T(8,128)(2,1)S(1)}, u32[]{:S(2)}, u32[]{:S(2)}) collective-permute-start(bf16[64,1024]{1,0:T(8,128)(2,1)S(1)} %get-tuple-element.49.refs_4_), channel_id=1, source_target_pairs={{24,0},{25,1},{26,2},{27,3},{28,4},{29,5},{30,6},{31,7},{0,8},{1,9... | collective-permute-start | bytes 393224 | tf_op jit(solution)/shard_map/ppermute | solution.py:41
  9.8 8.4 %collective-permute-start.5 = (bf16[64,1024]{1,0:T(8,128)(2,1)S(1)}, bf16[64,1024]{1,0:T(8,128)(2,1)S(1)}, u32[]{:S(2)}, u32[]{:S(2)}) collective-permute-start(bf16[64,1024]{1,0:T(8,128)(2,1)S(1)} %get-tuple-element.49.refs_4_), channel_id=1, source_target_pairs={{16,0},{17,1},{18,2},{19,3},{20,4},{21,5},{22,6},{23,7},{24,8},{25... | collective-permute-start | bytes 393224 | tf_op jit(solution)/shard_map/ppermute | solution.py:41
  12.7 5.5 %collective-permute-start.4 = (bf16[64,1024]{1,0:T(8,128)(2,1)S(1)}, bf16[64,1024]{1,0:T(8,128)(2,1)S(1)}, u32[]{:S(2)}, u32[]{:S(2)}) collective-permute-start(bf16[64,1024]{1,0:T(8,128)(2,1)S(1)} %get-tuple-element.49.refs_4_), channel_id=1, source_target_pairs={{8,0},{9,1},{10,2},{11,3},{12,4},{13,5},{14,6},{15,7},{16,8},{17,9... | collective-permute-start | bytes 393224 | tf_op jit(solution)/shard_map/ppermute | solution.py:41
  18.8 14.7 %collective-permute-start.9 = (bf16[256,1024]{1,0:T(8,128)(2,1)S(1)}, bf16[256,1024]{1,0:T(8,128)(2,1)S(1)}, u32[]{:S(2)}, u32[]{:S(2)}) collective-permute-start(bf16[256,1024]{1,0:T(8,128)(2,1)S(1)} %get-tuple-element.61.refs_0_), channel_id=1, source_target_pairs={{24,0},{25,1},{26,2},{27,3},{28,4},{29,5},{30,6},{31,7},{0,8},{1,9... | collective-permute-start | bytes 1572872 | tf_op jit(solution)/shard_map/ppermute | solution.py:41
  20.0 25.0 %collective-permute-start.8 = (bf16[256,1024]{1,0:T(8,128)(2,1)S(1)}, bf16[256,1024]{1,0:T(8,128)(2,1)S(1)}, u32[]{:S(2)}, u32[]{:S(2)}) collective-permute-start(bf16[256,1024]{1,0:T(8,128)(2,1)S(1)} %get-tuple-element.61.refs_0_), channel_id=1, source_target_pairs={{16,0},{17,1},{18,2},{19,3},{20,4},{21,5},{22,6},{23,7},{24,8},{25... | collective-permute-start | bytes 1572872 | tf_op jit(solution)/shard_map/ppermute | solution.py:41
  22.9 48.3 %collective-permute-start.15 = (bf16[448,4096]{1,0:T(8,128)(2,1)S(1)}, bf16[448,4096]{1,0:T(8,128)(2,1)S(1)}, u32[]{:S(2)}, u32[]{:S(2)}) collective-permute-start(bf16[448,4096]{1,0:T(8,128)(2,1)S(1)} %bitcast.25), channel_id=1, source_target_pairs={{0,1},{1,0},{2,3},{3,2},{4,5},{5,4},{6,7},{7,6},{8,9},{9,8},{10,11... | collective-permute-start | bytes 11010056 | tf_op jit(solution)/shard_map/ppermute | solution.py:255
  22.9 23.5 %collective-permute-start.7 = (bf16[256,1024]{1,0:T(8,128)(2,1)S(1)}, bf16[256,1024]{1,0:T(8,128)(2,1)S(1)}, u32[]{:S(2)}, u32[]{:S(2)}) collective-permute-start(bf16[256,1024]{1,0:T(8,128)(2,1)S(1)} %get-tuple-element.61.refs_0_), channel_id=1, source_target_pairs={{8,0},{9,1},{10,2},{11,3},{12,4},{13,5},{14,6},{15,7},{16,8},{17,9... | collective-permute-start | bytes 1572872 | tf_op jit(solution)/shard_map/ppermute | solution.py:41
  24.2 22.3 %collective-permute-start.12 = (bf16[256,1024]{1,0:T(8,128)(2,1)S(1)}, bf16[256,1024]{1,0:T(8,128)(2,1)S(1)}, u32[]{:S(2)}, u32[]{:S(2)}) collective-permute-start(bf16[256,1024]{1,0:T(8,128)(2,1)S(1)} %get-tuple-element.62.refs_4_), channel_id=1, source_target_pairs={{6,0},{7,1},{0,2},{1,3},{2,4},{3,5},{4,6},{5,7},{14,8},{15,9},{8,1... | collective-permute-start | bytes 1572872 | tf_op jit(solution)/shard_map/ppermute | solution.py:40
  33.5 12.9 %collective-permute-start.11 = (bf16[256,1024]{1,0:T(8,128)(2,1)S(1)}, bf16[256,1024]{1,0:T(8,128)(2,1)S(1)}, u32[]{:S(2)}, u32[]{:S(2)}) collective-permute-start(bf16[256,1024]{1,0:T(8,128)(2,1)S(1)} %get-tuple-element.62.refs_4_), channel_id=1, source_target_pairs={{4,0},{5,1},{6,2},{7,3},{0,4},{1,5},{2,6},{3,7},{12,8},{13,9},{14,... | collective-permute-start | bytes 1572872 | tf_op jit(solution)/shard_map/ppermute | solution.py:40
  45.0 12.2 %collective-permute-start.10 = (bf16[256,1024]{1,0:T(8,128)(2,1)S(1)}, bf16[256,1024]{1,0:T(8,128)(2,1)S(1)}, u32[]{:S(2)}, u32[]{:S(2)}) collective-permute-start(bf16[256,1024]{1,0:T(8,128)(2,1)S(1)} %get-tuple-element.62.refs_4_), channel_id=1, source_target_pairs={{2,0},{3,1},{4,2},{5,3},{6,4},{7,5},{0,6},{1,7},{10,8},{11,9},{12,... | collective-permute-start | bytes 1572872 | tf_op jit(solution)/shard_map/ppermute | solution.py:40
  74.4 9.3 %collective-permute-start.16 = (bf16[256,512]{1,0:T(8,128)(2,1)S(1)}, bf16[256,512]{1,0:T(8,128)(2,1)S(1)}, u32[]{:S(2)}, u32[]{:S(2)}) collective-permute-start(bf16[256,512]{1,0:T(8,128)(2,1)S(1)} %get-tuple-element.68), channel_id=1, source_target_pairs={{0,2},{1,3},{2,4},{3,5},{4,6},{5,7},{6,0},{7,1},{8,10},{9,11},{10,... | collective-permute-start | bytes 786440 | tf_op jit(solution)/shard_map/ppermute | solution.py:40
  75.8 10.7 %collective-permute-start.17 = (bf16[256,512]{1,0:T(8,128)(2,1)S(1)}, bf16[256,512]{1,0:T(8,128)(2,1)S(1)}, u32[]{:S(2)}, u32[]{:S(2)}) collective-permute-start(bf16[256,512]{1,0:T(8,128)(2,1)S(1)} %get-tuple-element.69), channel_id=1, source_target_pairs={{0,4},{1,5},{2,6},{3,7},{4,0},{5,1},{6,2},{7,3},{8,12},{9,13},{10,... | collective-permute-start | bytes 786440 | tf_op jit(solution)/shard_map/ppermute | solution.py:40
  77.9 13.4 %collective-permute-start.18 = (bf16[256,512]{1,0:T(8,128)(2,1)S(1)}, bf16[256,512]{1,0:T(8,128)(2,1)S(1)}, u32[]{:S(2)}, u32[]{:S(2)}) collective-permute-start(bf16[256,512]{1,0:T(8,128)(2,1)S(1)} %get-tuple-element.70), channel_id=1, source_target_pairs={{0,6},{1,7},{2,0},{3,1},{4,2},{5,3},{6,4},{7,5},{8,14},{9,15},{10,... | collective-permute-start | bytes 786440 | tf_op jit(solution)/shard_map/ppermute | solution.py:40
  78.8 14.6 %collective-permute-start.19 = (bf16[256,512]{1,0:T(8,128)(2,1)S(1)}, bf16[256,512]{1,0:T(8,128)(2,1)S(1)}, u32[]{:S(2)}, u32[]{:S(2)}) collective-permute-start(bf16[256,512]{1,0:T(8,128)(2,1)S(1)} %get-tuple-element.72), channel_id=1, source_target_pairs={{0,8},{1,9},{2,10},{3,11},{4,12},{5,13},{6,14},{7,15},{8,16},{9,17... | collective-permute-start | bytes 786440 | tf_op jit(solution)/shard_map/ppermute | solution.py:41
  78.8 14.6 %collective-permute-start.20 = (bf16[256,512]{1,0:T(8,128)(2,1)S(1)}, bf16[256,512]{1,0:T(8,128)(2,1)S(1)}, u32[]{:S(2)}, u32[]{:S(2)}) collective-permute-start(bf16[256,512]{1,0:T(8,128)(2,1)S(1)} %get-tuple-element.73), channel_id=1, source_target_pairs={{0,16},{1,17},{2,18},{3,19},{4,20},{5,21},{6,22},{7,23},{8,24},{9,... | collective-permute-start | bytes 786440 | tf_op jit(solution)/shard_map/ppermute | solution.py:41
  83.7 10.2 %collective-permute-start.21 = (bf16[256,512]{1,0:T(8,128)(2,1)S(1)}, bf16[256,512]{1,0:T(8,128)(2,1)S(1)}, u32[]{:S(2)}, u32[]{:S(2)}) collective-permute-start(bf16[256,512]{1,0:T(8,128)(2,1)S(1)} %get-tuple-element.74), channel_id=1, source_target_pairs={{0,24},{1,25},{2,26},{3,27},{4,28},{5,29},{6,30},{7,31},{8,0},{9,1... | collective-permute-start | bytes 786440 | tf_op jit(solution)/shard_map/ppermute | solution.py:41
  95.0 9.3 %collective-permute-start.22 = (bf16[256,128]{1,0:T(8,128)(2,1)S(1)}, bf16[256,128]{1,0:T(8,128)(2,1)S(1)}, u32[]{:S(2)}, u32[]{:S(2)}) collective-permute-start(bf16[256,128]{1,0:T(8,128)(2,1)S(1)} %get-tuple-element.76), channel_id=1, source_target_pairs={{0,8},{1,9},{2,10},{3,11},{4,12},{5,13},{6,14},{7,15},{8,16},{9,17... | collective-permute-start | bytes 196616 | tf_op jit(solution)/shard_map/ppermute | solution.py:41
  95.6 9.6 %collective-permute-start.23 = (bf16[256,128]{1,0:T(8,128)(2,1)S(1)}, bf16[256,128]{1,0:T(8,128)(2,1)S(1)}, u32[]{:S(2)}, u32[]{:S(2)}) collective-permute-start(bf16[256,128]{1,0:T(8,128)(2,1)S(1)} %get-tuple-element.77), channel_id=1, source_target_pairs={{0,16},{1,17},{2,18},{3,19},{4,20},{5,21},{6,22},{7,23},{8,24},{9,... | collective-permute-start | bytes 196616 | tf_op jit(solution)/shard_map/ppermute | solution.py:41
  99.4 5.7 %collective-permute-start.24 = (bf16[256,128]{1,0:T(8,128)(2,1)S(1)}, bf16[256,128]{1,0:T(8,128)(2,1)S(1)}, u32[]{:S(2)}, u32[]{:S(2)}) collective-permute-start(bf16[256,128]{1,0:T(8,128)(2,1)S(1)} %get-tuple-element.78), channel_id=1, source_target_pairs={{0,24},{1,25},{2,26},{3,27},{4,28},{5,29},{6,30},{7,31},{8,0},{9,1... | collective-permute-start | bytes 196616 | tf_op jit(solution)/shard_map/ppermute | solution.py:41
  99.4 5.7 %collective-permute-start.25 = (bf16[256,128]{1,0:T(8,128)(2,1)S(1)}, bf16[256,128]{1,0:T(8,128)(2,1)S(1)}, u32[]{:S(2)}, u32[]{:S(2)}) collective-permute-start(bf16[256,128]{1,0:T(8,128)(2,1)S(1)} %get-tuple-element.80), channel_id=1, source_target_pairs={{0,2},{1,3},{2,4},{3,5},{4,6},{5,7},{6,0},{7,1},{8,10},{9,11},{10,... | collective-permute-start | bytes 196616 | tf_op jit(solution)/shard_map/ppermute | solution.py:40
  100.6 5.9 %collective-permute-start.26 = (bf16[256,128]{1,0:T(8,128)(2,1)S(1)}, bf16[256,128]{1,0:T(8,128)(2,1)S(1)}, u32[]{:S(2)}, u32[]{:S(2)}) collective-permute-start(bf16[256,128]{1,0:T(8,128)(2,1)S(1)} %get-tuple-element.81), channel_id=1, source_target_pairs={{0,4},{1,5},{2,6},{3,7},{4,0},{5,1},{6,2},{7,3},{8,12},{9,13},{10,... | collective-permute-start | bytes 196616 | tf_op jit(solution)/shard_map/ppermute | solution.py:40
  (11 other events, 128.9 us)
where the time goes:
time: 159 us; the launch traced here: 157 us
  waiting for transfers between devices  51.3 us (32%)
  blocking collectives  46.5 us (29%)
  starting transfers between devices  37.1 us (23%)
  Pallas kernels  19.9 us (13%)
  local copies, waits for them, and re-layouts  2.18 us (1%)
    ppermute x12, waiting for transfers between devices, ring_steps(): got_y[d] = lax.ppermute(by_y[d], 'neuron', perm_y(d))  24.9 us
    ppermute x12, waiting for transfers between devices, ring_steps(): got_x[d] = lax.ppermute(by_x[d], 'neuron', perm_x(d))  23.1 us
    pallas_call x9, Pallas kernels, call(): pl.pallas_call(body, grid_spec=pltpu.PrefetchScalarGridSpec(num_scalar_pr...  19.9 us
    ppermute x12, starting transfers between devices, ring_steps(): got_y[d] = lax.ppermute(by_y[d], 'neuron', perm_y(d))  19.2 us
    all_to_all x1, blocking collectives, per_device(): lax.all_to_all(placed.reshape(planes, members * share, col), 'expert', 0,...  18.8 us
    ppermute x12, starting transfers between devices, ring_steps(): got_x[d] = lax.ppermute(by_x[d], 'neuron', perm_x(d))  17.2 us
    all_to_all x1, blocking collectives, per_device(): every = lax.all_to_all(copies, 'expert', 0, 0, tiled=True)  14.8 us
    all_to_all x1, blocking collectives, per_device(): lax.all_to_all(mixed.reshape(members, share, col), 'neuron', 0, 0, tiled=...  12.9 us
  transfers between devices with their start and end apart: 28, of which 13 were waited for; matrix products, arithmetic and copies ran while one was open for 0% of the time, Pallas kernels for 9%

commit v1 on v0

v1 whole, which is shorter than its diff:
```python
import jax
import jax.numpy as jnp
from jax import lax
from jax.experimental import pallas as pl
from jax.experimental.pallas import tpu as pltpu
from jax.sharding import PartitionSpec as P


BLK = 64
RING = 4


def device(y, x, c):
    return ((y % RING) * RING + x % RING) * 2 + c


PLACES = [(y, x, c) for y in range(RING) for x in range(RING) for c in range(2)]
PARTNER = [(device(y, x, c), device(y, x, 1 - c)) for y, x, c in PLACES]


def turn(d, leg):
    pairs = []
    for y, x, c in PLACES:
        on = device(y, x + d, c) if c == leg else device(y + d, x, c)
        pairs.append((device(y, x, c), on))
    return pairs


def ring(leg, blocks, back):
    got = {0: blocks[0]}
    for d in STEPS:
        pairs = turn(d, leg)
        got[d] = lax.ppermute(blocks[d], "neuron", [(t, s) for s, t in pairs] if back else pairs)
    return [got[k] for k in range(RING)]


def relay(leg, left, right):
    on = turn(1, leg)
    back = [(t, s) for s, t in on]

    def send(value, pairs):
        return lax.ppermute(value, "neuron", pairs)

    left_before, right_after = send(left, on), send(right, back)
    right_before, left_after = send(right, on), send(left, back)
    left_far, right_far = send(left_before, on), send(right_after, back)
    return [left, left_after, left_far, left_before, right, right_after, right_far, right_before]


STEPS = (2, 1, 3)


def mm(a, b):
    return jnp.dot(a, b, preferred_element_type=jnp.float32)


LIMIT = pltpu.CompilerParams(vmem_limit_bytes=20 * 2**20)


def whole(*arrays):
    return [pl.BlockSpec(a.shape, lambda i, s, n=len(a.shape): (0,) * n) for a in arrays]


def call(body, place, ins, specs, outs, scratch=(), flops=10**9, steps=1):
    return pl.pallas_call(
        body,
        grid_spec=pltpu.PrefetchScalarGridSpec(
            num_scalar_prefetch=1, grid=(steps,), in_specs=specs, out_specs=whole(*outs), scratch_shapes=list(scratch)
        ),
        out_shape=outs,
        compiler_params=LIMIT,
        cost_estimate=pl.CostEstimate(flops=flops, bytes_accessed=4 * 2**20, transcendentals=0),
    )(place, *ins)


def rows_kernel(place, mine, theirs, out):
    rows = mine.shape[0]
    for source, core in ((mine, place[0]), (theirs, 1 - place[0])):
        out[pl.ds(pl.multiple_of(core * rows, rows), rows), :] = source[...]


def lines_kernel(place, *refs):
    rows, span = refs[0].shape[0], refs[-1].shape[1]
    for k in range(RING):
        at = pl.ds(pl.multiple_of((place[2] + k) % RING * rows, rows), rows)
        refs[-2][at, :] = refs[k][:, :span]
        refs[-1][at, :] = refs[k][:, span:]


def routing_kernel(place, ids, logits, slots, weight, spread):
    total_tokens, capacity = spread.shape
    lanes = 128
    first, second = (jnp.where(ids[k : k + 1, :] == place[1], 1.0, 0.0) for k in range(2))
    lead = 1.0 / (1.0 + jnp.exp(logits[1:2, :] - logits[0:1, :]))
    share = first * lead + second * (1.0 - lead)
    chosen = first + second
    chunks = [chosen[:, k : k + lanes] for k in range(0, total_tokens, lanes)]
    grid = jnp.concatenate(chunks, axis=0)
    earlier = lax.broadcasted_iota(jnp.int32, (lanes, lanes), 0) < lax.broadcasted_iota(jnp.int32, (lanes, lanes), 1)
    before = mm(grid.astype(jnp.bfloat16), jnp.where(earlier, 1.0, 0.0).astype(jnp.bfloat16))
    offset = jnp.zeros((1, 1), jnp.float32)
    out = []
    for k, chunk in enumerate(chunks):
        out.append(jnp.where(chunk > 0.0, before[k : k + 1, :] + offset, float(capacity)))
        offset = offset + jnp.sum(chunk, axis=1, keepdims=True)
    slot = jnp.concatenate(out, axis=1).astype(jnp.int32)
    per_chip = total_tokens // RING // RING
    across = jnp.concatenate(
        [slot[:, (y * RING + x) * per_chip : (y * RING + x + 1) * per_chip] for x in range(RING) for y in range(RING)], axis=1
    )
    slots[...] = jnp.where(place[0] == 0, slot, across)
    hit = slot == lax.broadcasted_iota(jnp.int32, (capacity, total_tokens), 0)
    weight[...] = jnp.sum(jnp.where(hit, share, 0.0), axis=1, keepdims=True)
    planes, own = place_counts(total_tokens)
    each, part = own // planes, total_tokens // planes
    step = 256
    for top in range(0, total_tokens, step):
        row = lax.broadcasted_iota(jnp.int32, (step, total_tokens), 0) + top
        token = row % part // each * own + row // part * each + row % each
        column = lax.broadcasted_iota(jnp.int32, (step, total_tokens), 1)
        mine = jnp.sum(jnp.where(token == column, slot.astype(jnp.float32), 0.0), axis=1, keepdims=True)
        index = lax.broadcasted_iota(jnp.int32, (step, capacity), 1)
        spread[top : top + step, :] = jnp.where(mine.astype(jnp.int32) == index, 1.0, 0.0).astype(jnp.bfloat16)


def place_counts(total_tokens):
    return 8, total_tokens // len(PLACES)


def dispatch_kernel(place, slots, *refs):
    blocks, out = refs[:-1], refs[-1]
    rows, span = blocks[0].shape
    capacity = out.shape[0]
    index = lax.broadcasted_iota(jnp.int32, (capacity, rows), 0)
    hot = []
    for k in range(RING):
        line = slots[:, pl.ds(pl.multiple_of((place[3] + k) % RING * rows, rows), rows)]
        hot.append(jnp.where(line == index, 1.0, 0.0).astype(jnp.bfloat16))
    for side in range(2):
        for n in range(0, span, 256):
            acc = mm(hot[0], blocks[side * RING][:, n : n + 256])
            for k in range(1, RING):
                acc = acc + mm(hot[k], blocks[side * RING + k][:, n : n + 256])
            out[:, side * span + n : side * span + n + 256] = acc.astype(jnp.bfloat16)


def turn_kernel(place, gate, up, out):
    units = gate.shape[0]
    out[:, :units] = gate[...].T
    out[:, units:] = up[...].T


def near_kernel(place, rows, both, out):
    out[...] = mm(rows[...], both[...])


def far_kernel(place, rows, both, near, live, keep, give, hidden):
    half_rows, units = keep.shape
    block = lax.broadcasted_iota(jnp.int32, (1, units), 1) // BLK
    kept = jnp.zeros((1, units), jnp.float32)
    for k in range(units // BLK):
        kept = jnp.where(block == k, live[0, k].astype(jnp.float32), kept)
    value = near[...] + mm(rows[...], both[...])
    gate_val, up_val = value[:, :units], value[:, units:]
    hidden[...] = (gate_val / (1.0 + jnp.exp(-gate_val)) * up_val * kept).astype(jnp.bfloat16)
    for out, core in ((keep, place[0]), (give, 1 - place[0])):
        out[...] = hidden[pl.ds(pl.multiple_of(core * half_rows, half_rows), half_rows), :]


def down_kernel(place, near, far, w_near, w_far, weight, *outs):
    rows, span = outs[0].shape
    col = span // RING
    scale = weight[pl.ds(pl.multiple_of(place[0] * rows, rows), rows), :]
    for d in range(RING):
        for j in range(RING):
            site = (place[2] + d) % RING * place[4] + j * place[5]
            cols = pl.ds(pl.multiple_of(site * col, col), col)
            value = mm(near[...], w_near[:, cols]) + mm(far[...], w_far[:, cols])
            outs[d][:, j * col : (j + 1) * col] = (value * scale).astype(jnp.bfloat16)


def total(refs):
    value = refs[0][...].astype(jnp.float32)
    for r in refs[1:]:
        value = value + r[...].astype(jnp.float32)
    return value


def middle_kernel(place, *refs):
    got, outs, part = refs[:RING], refs[RING : 2 * RING], refs[-1]
    col = outs[0].shape[1]
    part[...] = total(got).astype(jnp.bfloat16)
    for k in range(RING):
        outs[k][...] = part[:, pl.ds(pl.multiple_of((place[3] + k) % RING * col, col), col)]


def pair_kernel(place, *refs):
    got, outs, part = refs[:RING], refs[RING : RING + 2], refs[-1]
    col = outs[0].shape[1]
    part[...] = total(got).astype(jnp.bfloat16)
    for out, core in zip(outs, (place[0], 1 - place[0])):
        out[...] = part[:, pl.ds(pl.multiple_of(core * col, col), col)]


def last_kernel(place, spread, near, far, out):
    rows = near.shape[0]
    value = jnp.zeros(out.shape, jnp.float32)
    for part, core in ((near, place[0]), (far, 1 - place[0])):
        value = value + mm(spread[:, pl.ds(pl.multiple_of(core * rows, rows), rows)], part[...])
    out[...] = value.astype(jnp.bfloat16)


def per_device(planes, tokens, route_logits, expert_ids, block_live, w_gate, w_up, w_down):
    total_tokens = expert_ids.shape[0]
    own_tokens, width = tokens.shape
    capacity = total_tokens // 2
    sites = RING * RING
    members = 2 * sites
    share = own_tokens // planes
    half = width // 2
    col = half // sites
    place = lax.axis_index("neuron")
    core, x, y = place % 2, place // 2 % RING, place // (2 * RING)
    along_x = core == 0
    one, two = jnp.where(along_x, x, y), jnp.where(along_x, y, x)
    where = jnp.stack(
        [core, lax.axis_index("expert"), one, two, jnp.where(along_x, 1, RING), jnp.where(along_x, RING, 1)]
    ).astype(jnp.int32)
    where, tokens = lax.optimization_barrier((where, tokens))
    shape = jax.ShapeDtypeStruct
    units = w_gate.shape[2]
    bf16 = jnp.bfloat16

    theirs = lax.ppermute(tokens, "neuron", PARTNER)
    own_half = pl.BlockSpec((own_tokens, half), lambda i, s: (0, s[0]))
    chip_rows = call(rows_kernel, where, (tokens, theirs), [own_half, own_half], [shape((2 * own_tokens, half), bf16)])[0]
    chip_rows, w_down, expert_ids, route_logits = lax.optimization_barrier((chip_rows, w_down, expert_ids, route_logits))
    ins = ring(0, [chip_rows] * RING, True)
    down_far = lax.ppermute(w_down[0], "neuron", PARTNER)
    names = (expert_ids.T, route_logits.T)
    routed = call(
        routing_kernel, where, names, whole(*names),
        [shape((1, total_tokens), jnp.int32), shape((capacity, 1), jnp.float32), shape((total_tokens, capacity), bf16)],
    )
    line = call(lines_kernel, where, ins, whole(*ins), [shape((2 * RING * own_tokens, half // 2), bf16)] * 2)
    left, right, slots, slot_weight, spread = lax.optimization_barrier((*line, *routed))
    ins = (slots, *relay(1, left, right))
    cut = 512
    turned = pl.pallas_call(
        turn_kernel,
        grid_spec=pltpu.PrefetchScalarGridSpec(
            num_scalar_prefetch=1, grid=(width // cut,),
            in_specs=[pl.BlockSpec((units, cut), lambda i, s: (0, i))] * 2,
            out_specs=pl.BlockSpec((cut, 2 * units), lambda i, s: (i, 0)),
        ),
        out_shape=shape((width, 2 * units), bf16),
        compiler_params=LIMIT,
        cost_estimate=pl.CostEstimate(flops=10**9, bytes_accessed=4 * 2**20, transcendentals=0),
    )(where, w_gate[0].T, w_up[0].T)
    slots, turned = lax.optimization_barrier((ins[0], turned))
    ins = (slots, *ins[1:])
    near_in = call(
        dispatch_kernel, where, ins, whole(*ins), [shape((capacity, half), bf16)], flops=2 * capacity * total_tokens * half
    )[0]
    far_in = lax.ppermute(near_in, "neuron", PARTNER)
    near_half = pl.BlockSpec((half, 2 * units), lambda i, s: (s[0], 0))
    far_half = pl.BlockSpec((half, 2 * units), lambda i, s: (1 - s[0], 0))
    sums = call(
        near_kernel, where, (near_in, turned), [*whole(near_in), near_half],
        [shape((capacity, 2 * units), jnp.float32)], flops=4 * capacity * half * units,
    )
    rows = capacity // 2
    hidden, given = call(
        far_kernel, where, (far_in, turned, *sums, block_live),
        [*whole(far_in), far_half, *whole(*sums), pl.BlockSpec(memory_space=pltpu.SMEM)],
        [shape((rows, units), bf16)] * 2, [pltpu.VMEM((capacity, units), bf16)], flops=4 * capacity * half * units,
    )
    hidden_far = lax.ppermute(given, "neuron", PARTNER)
    ins = (hidden, hidden_far, w_down[0], down_far, slot_weight)
    pieces = call(
        down_kernel, where, ins, whole(*ins), [shape((rows, width // RING), bf16)] * RING, flops=4 * capacity * half * units
    )
    ins = ring(0, pieces, False)
    pieces = call(
        middle_kernel, where, ins, whole(*ins), [shape((rows, 2 * col), bf16)] * RING,
        [pltpu.VMEM((rows, width // RING), bf16)],
    )
    ins = ring(1, pieces, False)
    mine, given = call(
        pair_kernel, where, ins, whole(*ins), [shape((rows, col), bf16)] * 2, [pltpu.VMEM((rows, 2 * col), bf16)]
    )
    ins = (spread, mine, lax.ppermute(given, "neuron", PARTNER))
    placed = call(last_kernel, where, ins, whole(*ins), [shape((total_tokens, col), bf16)])[0]
    over = lax.all_to_all(placed.reshape(planes, members * share, col), "expert", 0, 0, tiled=True)
    mixed = jnp.sum(over.astype(jnp.float32), axis=0).astype(jnp.bfloat16)
    owned = lax.all_to_all(mixed.reshape(members, share, col), "neuron", 0, 0, tiled=True)
    copies = jnp.broadcast_to(owned.reshape(1, members * share, col), (planes, members * share, col))
    every = lax.all_to_all(copies, "expert", 0, 0, tiled=True)
    every = every.reshape(planes, members, share, col).transpose(0, 2, 1, 3)
    return every.reshape(own_tokens, width)


def solution(mesh):
    placed = (
        P("neuron", None),
        P(),
        P(),
        P("expert", "neuron"),
        P("expert", None, "neuron"),
        P("expert", None, "neuron"),
        P("expert", "neuron", None),
    )

    def body(*args):
        return per_device(mesh.shape["expert"], *args)

    return jax.shard_map(body, mesh=mesh, in_specs=placed, out_specs=P("neuron", None), check_vma=False)
```

time: 159 us -> 137 us (0.86)
  waiting for transfers between devices: 51.3 us -> 35.4 us
  starting transfers between devices: 37.1 us -> 24.5 us
  Pallas kernels: 19.9 us -> 23.3 us
  blocking collectives: 46.5 us -> 49 us
    ppermute x25 -> x17, waiting for transfers between devices: 49.5 us -> 32.4 us  [the longest x9 21.5 us: ring(): lax.ppermute(blocks[d], 'neuron', [(t, s) for s, t in pairs] if back else...]
    ppermute x25 -> x17, starting transfers between devices: 37 us -> 24.2 us  [the longest x9 15.3 us: ring(): lax.ppermute(blocks[d], 'neuron', [(t, s) for s, t in pairs] if back else...]
    pallas_call x0 -> x1, Pallas kernels: none -> 5.19 us  [per_device(): pl.pallas_call(turn_kernel, grid_spec=pltpu.PrefetchScalarGridSpec(num_sc...]
    pallas_call x9 -> x10, Pallas kernels: 19.9 us -> 18.1 us  [call(): pl.pallas_call(body, grid_spec=pltpu.PrefetchScalarGridSpec(num_scalar_pr...]
    all_to_all x1, blocking collectives: 18.8 us -> 20.5 us  [per_device(): lax.all_to_all(placed.reshape(planes, members * share, col), 'expert', 0,...]
  transfers between devices with their start and end apart: 28 -> 20, of which waited for: 13 -> 15; matrix products, arithmetic and copies ran while one was open for 0% -> 0% of each run, Pallas kernels for 9% -> 12%
where the time goes in v1:
time: 137 us; the launch traced here: 135 us
  blocking collectives  49 us (36%)
  waiting for transfers between devices  35.4 us (26%)
  starting transfers between devices  24.5 us (18%)
  Pallas kernels  23.3 us (17%)
  local copies, waits for them, and re-layouts  2.18 us (2%)
    ppermute x9, waiting for transfers between devices, ring(): lax.ppermute(blocks[d], 'neuron', [(t, s) for s, t in pairs] if back else...  21.5 us
    all_to_all x1, blocking collectives, per_device(): lax.all_to_all(placed.reshape(planes, members * share, col), 'expert', 0,...  20.5 us
    pallas_call x10, Pallas kernels, call(): pl.pallas_call(body, grid_spec=pltpu.PrefetchScalarGridSpec(num_scalar_pr...  18.1 us
    ppermute x9, starting transfers between devices, ring(): lax.ppermute(blocks[d], 'neuron', [(t, s) for s, t in pairs] if back else...  15.3 us
    all_to_all x1, blocking collectives, per_device(): every = lax.all_to_all(copies, 'expert', 0, 0, tiled=True)  14.8 us
    all_to_all x1, blocking collectives, per_device(): lax.all_to_all(mixed.reshape(members, share, col), 'neuron', 0, 0, tiled=...  13.7 us
    ppermute x6, starting transfers between devices, send(): return lax.ppermute(value, 'neuron', pairs)  8.58 us
    ppermute x6, waiting for transfers between devices, send(): return lax.ppermute(value, 'neuron', pairs)  8.26 us
  transfers between devices with their start and end apart: 20, of which 15 were waited for; matrix products, arithmetic and copies ran while one was open for 0% of the time, Pallas kernels for 12%

profile of v1, /device:TPU:2, one launch (start us, length us, event | category | flops | bytes accessed | tf_op | source)
XLA Modules:
  0.0 134.6 jit_solution(8287964713042861684)
XLA Ops:
  0.1 1.7 %collective-permute-done.theirs = bf16[32,4096]{1,0:T(8,128)(2,1)S(1)} collective-permute-done((bf16[32,4096]{1,0:T(8,128)(2,1)}, bf16[32,4096]{1,0:T(8,128)(2,1)S(1)}, u32[]{:S(2)}, u32[]{:S(2)}) %collective-permute-start) | collective-permute-done | bytes 262176 | tf_op jit(solution)/shard_map/ppermute | solution.py:234
  3.4 2.3 %collective-permute-start.1 = (bf16[64,2048]{1,0:T(8,128)(2,1)S(1)}, bf16[64,2048]{1,0:T(8,128)(2,1)S(1)}, u32[]{:S(2)}, u32[]{:S(2)}) collective-permute-start(bf16[64,2048]{1,0:T(8,128)(2,1)S(1)} %shard_map.73.refs_0_), channel_id=1, source_target_pairs={{2,0},{9,1},{4,2},{11,3},{6,4},{13,5},{0,6},{15,7},{10,8},{17,9},{... | collective-permute-start | bytes 786440 | tf_op jit(solution)/shard_map/ppermute | solution.py:33
  6.4 1.8 %collective-permute-start.3 = (bf16[64,2048]{1,0:T(8,128)(2,1)S(1)}, bf16[64,2048]{1,0:T(8,128)(2,1)S(1)}, u32[]{:S(2)}, u32[]{:S(2)}) collective-permute-start(bf16[64,2048]{1,0:T(8,128)(2,1)S(1)} %shard_map.73.refs_0_), channel_id=1, source_target_pairs={{6,0},{25,1},{0,2},{27,3},{2,4},{29,5},{4,6},{31,7},{14,8},{1,9},{... | collective-permute-start | bytes 786440 | tf_op jit(solution)/shard_map/ppermute | solution.py:33
  8.2 1.7 %shard_map.75 = (s32[1,1024]{1,0:T(1,128)S(1)}, f32[512,1]{1,0:T(8,128)S(1)}, bf16[1024,512]{1,0:T(8,128)(2,1)S(1)}) custom-call(s32[6]{0:T(128)S(1)} %stack.27.place, s32[2,1024]{1,0:T(2,128)S(1)} %bitcast.31, f32[2,1024]{1,0:T(2,128)S(1)} %bitcast.32), custom_call_target="tpu_custom_call" | custom-call | flops 1000000000 | bytes 4194304 | tf_op jit(solution)/shard_map/pallas_call | solution.py:65
  9.9 3.6 %collective-permute-done.2.refs_2_ = bf16[64,2048]{1,0:T(8,128)(2,1)S(1)} collective-permute-done((bf16[64,2048]{1,0:T(8,128)(2,1)S(1)}, bf16[64,2048]{1,0:T(8,128)(2,1)S(1)}, u32[]{:S(2)}, u32[]{:S(2)}) %collective-permute-start.2) | collective-permute-done | bytes 262176 | tf_op jit(solution)/shard_map/ppermute | solution.py:33
  17.0 1.7 %collective-permute-start.7 = (bf16[256,1024]{1,0:T(8,128)(2,1)S(1)}, bf16[256,1024]{1,0:T(8,128)(2,1)S(1)}, u32[]{:S(2)}, u32[]{:S(2)}) collective-permute-start(bf16[256,1024]{1,0:T(8,128)(2,1)S(1)} %get-tuple-element.49.refs_4_), channel_id=1, source_target_pairs={{8,0},{3,1},{10,2},{5,3},{12,4},{7,5},{14,6},{1,7},{16,8},{11,9},{... | collective-permute-start | bytes 1572872 | tf_op jit(solution)/shard_map/ppermute | solution.py:42
  18.7 1.8 %collective-permute-start.4 = (bf16[256,1024]{1,0:T(8,128)(2,1)S(1)}, bf16[256,1024]{1,0:T(8,128)(2,1)S(1)}, u32[]{:S(2)}, u32[]{:S(2)}) collective-permute-start(bf16[256,1024]{1,0:T(8,128)(2,1)S(1)} %get-tuple-element.48.refs_0_), channel_id=1, source_target_pairs={{8,0},{3,1},{10,2},{5,3},{12,4},{7,5},{14,6},{1,7},{16,8},{11,9},{... | collective-permute-start | bytes 1572872 | tf_op jit(solution)/shard_map/ppermute | solution.py:42
  20.7 5.1 %collective-permute-done.5.refs_3_ = bf16[256,1024]{1,0:T(8,128)(2,1)S(1)} collective-permute-done((bf16[256,1024]{1,0:T(8,128)(2,1)S(1)}, bf16[256,1024]{1,0:T(8,128)(2,1)S(1)}, u32[]{:S(2)}, u32[]{:S(2)}) %collective-permute-start.5) | collective-permute-done | bytes 524320 | tf_op jit(solution)/shard_map/ppermute | solution.py:42
  26.2 2.9 %collective-permute-start.8 = (bf16[256,1024]{1,0:T(8,128)(2,1)S(1)}, bf16[256,1024]{1,0:T(8,128)(2,1)S(1)}, u32[]{:S(2)}, u32[]{:S(2)}) collective-permute-start(bf16[256,1024]{1,0:T(8,128)(2,1)S(1)} %collective-permute-done.7.refs_5_), channel_id=1, source_target_pairs={{8,0},{3,1},{10,2},{5,3},{12,4},{7,5},{14,6},{1,7},{16,8},{11,9},{... | collective-permute-start | bytes 1572872 | tf_op jit(solution)/shard_map/ppermute | solution.py:42
  29.1 5.2 %shard_map.76.both = bf16[4096,896]{1,0:T(8,128)(2,1)S(1)} custom-call(s32[6]{0:T(128)S(1)} %stack.27.place, bf16[448,4096]{1,0:T(8,128)(2,1)S(1)} %bitcast.26, bf16[448,4096]{1,0:T(8,128)(2,1)S(1)} %bitcast.27), custom_call_target="tpu_custom_call" | custom-call | flops 1000000000 | bytes 4194304 | tf_op jit(solution)/shard_map/pallas_call | solution.py:249
  34.3 2.8 %collective-permute-done.6.refs_2_ = bf16[256,1024]{1,0:T(8,128)(2,1)S(1)} collective-permute-done((bf16[256,1024]{1,0:T(8,128)(2,1)S(1)}, bf16[256,1024]{1,0:T(8,128)(2,1)S(1)}, u32[]{:S(2)}, u32[]{:S(2)}) %collective-permute-start.6) | collective-permute-done | bytes 524320 | tf_op jit(solution)/shard_map/ppermute | solution.py:42
  37.4 2.9 %shard_map.77.rows = bf16[512,2048]{1,0:T(8,128)(2,1)S(1)} custom-call(s32[6]{0:T(128)S(1)} %stack.27.place, s32[1,1024]{1,0:T(1,128)S(1)} %get-tuple-element.47.slots, bf16[256,1024]{1,0:T(8,128)(2,1)S(1)} %get-tuple-element.48.refs_0_, bf16[256,1024]{1,0:T(8,128)(2,1)S(1)} %collective-permute-done.4.refs_1_, ...), custom_call_target="tpu_custom_call" | custom-call | flops 2147483648 | bytes 4194304 | tf_op jit(solution)/shard_map/pallas_call | solution.py:65
  40.6 2.9 %shard_map.78.near = f32[512,896]{1,0:T(8,128)S(1)} custom-call(s32[6]{0:T(128)S(1)} %stack.27.place, bf16[512,2048]{1,0:T(8,128)(2,1)S(1)} %shard_map.77.rows, bf16[4096,896]{1,0:T(8,128)(2,1)S(1)} %shard_map.76.both), custom_call_target="tpu_custom_call" | custom-call | flops 1879048192 | bytes 4194304 | tf_op jit(solution)/shard_map/pallas_call | solution.py:65
  44.7 3.8 %shard_map.79 = (bf16[256,448]{1,0:T(8,128)(2,1)S(1)}, bf16[256,448]{1,0:T(8,128)(2,1)S(1)}) custom-call(s32[6]{0:T(128)S(1)} %stack.27.place, bf16[512,2048]{1,0:T(8,128)(2,1)S(1)} %collective-permute-done.10.rows, bf16[4096,896]{1,0:T(8,128)(2,1)S(1)} %shard_map.76.both, f32[512,896]{1,0:T(8,128)S(1)} %shard_map.78.near, s32[1,7]{1,0:T(1,128)S(1)} %copy-done.3), custom_call_target="tpu_custom_call" | custom-call | flops 1879048192 | bytes 4194304 | tf_op jit(solution)/shard_map/pallas_call | solution.py:65
  50.2 3.0 %shard_map.80 = (bf16[256,1024]{1,0:T(8,128)(2,1)S(1)}, bf16[256,1024]{1,0:T(8,128)(2,1)S(1)}, bf16[256,1024]{1,0:T(8,128)(2,1)S(1)}, bf16[256,1024]{1,0:T(8,128)(2,1)S(1)}) custom-call(s32[6]{0:T(128)S(1)} %stack.27.place, bf16[256,448]{1,0:T(8,128)(2,1)S(1)} %get-tuple-element.51.near, bf16[256,448]{1,0:T(8,128)(2,1)S(1)} %collective-permute-done.11.far, ...), custom_call_target="tpu_custom_call" | custom-call | flops 1879048192 | bytes 4194304 | tf_op jit(solution)/shard_map/pallas_call | solution.py:65
  54.7 3.3 %collective-permute-start.14 = (bf16[256,1024]{1,0:T(8,128)(2,1)S(1)}, bf16[256,1024]{1,0:T(8,128)(2,1)S(1)}, u32[]{:S(2)}, u32[]{:S(2)}) collective-permute-start(bf16[256,1024]{1,0:T(8,128)(2,1)S(1)} %get-tuple-element.57), channel_id=1, source_target_pairs={{0,4},{1,17},{2,6},{3,19},{4,0},{5,21},{6,2},{7,23},{8,12},{9,25},... | collective-permute-start | bytes 1572872 | tf_op jit(solution)/shard_map/ppermute | solution.py:33
  58.0 5.1 %collective-permute-done.13.refs_1_ = bf16[256,1024]{1,0:T(8,128)(2,1)S(1)} collective-permute-done((bf16[256,1024]{1,0:T(8,128)(2,1)S(1)}, bf16[256,1024]{1,0:T(8,128)(2,1)S(1)}, u32[]{:S(2)}, u32[]{:S(2)}) %collective-permute-start.13) | collective-permute-done | bytes 524320 | tf_op jit(solution)/shard_map/ppermute | solution.py:33
  63.1 2.4 %collective-permute-done.14.refs_2_ = bf16[256,1024]{1,0:T(8,128)(2,1)S(1)} collective-permute-done((bf16[256,1024]{1,0:T(8,128)(2,1)S(1)}, bf16[256,1024]{1,0:T(8,128)(2,1)S(1)}, u32[]{:S(2)}, u32[]{:S(2)}) %collective-permute-start.14) | collective-permute-done | bytes 524320 | tf_op jit(solution)/shard_map/ppermute | solution.py:33
  65.5 5.5 %collective-permute-done.15.refs_3_ = bf16[256,1024]{1,0:T(8,128)(2,1)S(1)} collective-permute-done((bf16[256,1024]{1,0:T(8,128)(2,1)S(1)}, bf16[256,1024]{1,0:T(8,128)(2,1)S(1)}, u32[]{:S(2)}, u32[]{:S(2)}) %collective-permute-start.15) | collective-permute-done | bytes 524320 | tf_op jit(solution)/shard_map/ppermute | solution.py:33
  73.8 2.8 %collective-permute-start.17 = (bf16[256,256]{1,0:T(8,128)(2,1)S(1)}, bf16[256,256]{1,0:T(8,128)(2,1)S(1)}, u32[]{:S(2)}, u32[]{:S(2)}) collective-permute-start(bf16[256,256]{1,0:T(8,128)(2,1)S(1)} %get-tuple-element.61), channel_id=1, source_target_pairs={{0,16},{1,5},{2,18},{3,7},{4,20},{5,1},{6,22},{7,3},{8,24},{9,13},... | collective-permute-start | bytes 393224 | tf_op jit(solution)/shard_map/ppermute | solution.py:33
  78.4 2.5 %collective-permute-done.17.refs_2_ = bf16[256,256]{1,0:T(8,128)(2,1)S(1)} collective-permute-done((bf16[256,256]{1,0:T(8,128)(2,1)S(1)}, bf16[256,256]{1,0:T(8,128)(2,1)S(1)}, u32[]{:S(2)}, u32[]{:S(2)}) %collective-permute-start.17) | collective-permute-done | bytes 131104 | tf_op jit(solution)/shard_map/ppermute | solution.py:33
  84.4 20.5 %all_to_all.15 = bf16[8,128,128]{2,1,0:T(8,128)(2,1)S(1)} all-to-all(bf16[8,128,128]{2,1,0:T(8,128)(2,1)S(1)} %bitcast.30), channel_id=1, replica_groups=mesh['expert'=8,'neuron'=32] {'expert'}, dimensions={0} | all-to-all | bytes 524288 | tf_op jit(solution)/shard_map/all_to_all | solution.py:294
  105.0 13.7 %all_to_all.16 = bf16[32,4,128]{2,1,0:T(4,128)(2,1)S(1)} all-to-all(bf16[32,4,128]{2,1,0:T(4,128)(2,1)S(1)} %bitcast.35), channel_id=1, replica_groups=mesh['expert'=8,'neuron'=32] {'neuron'}, dimensions={0} | all-to-all | bytes 65536 | tf_op jit(solution)/shard_map/all_to_all | solution.py:296
  118.7 14.8 %all_to_all.17 = bf16[8,128,128]{2,1,0:T(8,128)(2,1)S(1)} all-to-all(bf16[8,128,128]{2,1,0:T(8,128)(2,1)S(1)} %broadcast_in_dim.8), channel_id=1, replica_groups=mesh['expert'=8,'neuron'=32] {'expert'}, dimensions={0} | all-to-all | bytes 524288 | tf_op jit(solution)/shard_map/all_to_all | solution.py:298
  (50 shorter events, 20.8 us)
Async XLA Ops:
  0.0 8.2 %copy-start.5 = (s32[1024,2]{0,1:T(2,128)S(1)}, s32[1024,2]{0,1:T(2,128)}, u32[]{:S(2)}) copy-start(s32[1024,2]{0,1:T(2,128)} %param.9) | copy-start | bytes 24580
  0.1 1.8 %collective-permute-start = (bf16[32,4096]{1,0:T(8,128)(2,1)}, bf16[32,4096]{1,0:T(8,128)(2,1)S(1)}, u32[]{:S(2)}, u32[]{:S(2)}) collective-permute-start(bf16[32,4096]{1,0:T(8,128)(2,1)} %mine), channel_id=1, source_target_pairs={{0,1},{1,0},{2,3},{3,2},{4,5},{5,4},{6,7},{7,6},{8,9},{9,8},{10,11... | collective-permute-start | bytes 786440 | tf_op jit(solution)/shard_map/ppermute | solution.py:234
  2.8 15.8 %copy-start.2 = (bf16[1,448,4096]{2,1,0:T(8,128)(2,1)S(1)}, bf16[1,448,4096]{2,1,0:T(8,128)(2,1)}, u32[]{:S(2)}) copy-start(bf16[1,448,4096]{2,1,0:T(8,128)(2,1)} %param.13) | copy-start | bytes 11010052
  3.4 6.5 %collective-permute-start.1 = (bf16[64,2048]{1,0:T(8,128)(2,1)S(1)}, bf16[64,2048]{1,0:T(8,128)(2,1)S(1)}, u32[]{:S(2)}, u32[]{:S(2)}) collective-permute-start(bf16[64,2048]{1,0:T(8,128)(2,1)S(1)} %shard_map.73.refs_0_), channel_id=1, source_target_pairs={{2,0},{9,1},{4,2},{11,3},{6,4},{13,5},{0,6},{15,7},{10,8},{17,9},{... | collective-permute-start | bytes 786440 | tf_op jit(solution)/shard_map/ppermute | solution.py:33
  5.7 7.9 %collective-permute-start.2 = (bf16[64,2048]{1,0:T(8,128)(2,1)S(1)}, bf16[64,2048]{1,0:T(8,128)(2,1)S(1)}, u32[]{:S(2)}, u32[]{:S(2)}) collective-permute-start(bf16[64,2048]{1,0:T(8,128)(2,1)S(1)} %shard_map.73.refs_0_), channel_id=1, source_target_pairs={{4,0},{17,1},{6,2},{19,3},{0,4},{21,5},{2,6},{23,7},{12,8},{25,9},... | collective-permute-start | bytes 786440 | tf_op jit(solution)/shard_map/ppermute | solution.py:33
  6.4 8.3 %collective-permute-start.3 = (bf16[64,2048]{1,0:T(8,128)(2,1)S(1)}, bf16[64,2048]{1,0:T(8,128)(2,1)S(1)}, u32[]{:S(2)}, u32[]{:S(2)}) collective-permute-start(bf16[64,2048]{1,0:T(8,128)(2,1)S(1)} %shard_map.73.refs_0_), channel_id=1, source_target_pairs={{6,0},{25,1},{0,2},{27,3},{2,4},{29,5},{4,6},{31,7},{14,8},{1,9},{... | collective-permute-start | bytes 786440 | tf_op jit(solution)/shard_map/ppermute | solution.py:33
  8.2 20.8 %copy-start = (bf16[1,4096,448]{1,2,0:T(8,128)(2,1)S(1)}, bf16[1,4096,448]{1,2,0:T(8,128)(2,1)}, u32[]{:S(2)}) copy-start(bf16[1,4096,448]{1,2,0:T(8,128)(2,1)} %param.11) | copy-start | bytes 11010052
  8.2 20.8 %copy-start.1 = (bf16[1,4096,448]{1,2,0:T(8,128)(2,1)S(1)}, bf16[1,4096,448]{1,2,0:T(8,128)(2,1)}, u32[]{:S(2)}) copy-start(bf16[1,4096,448]{1,2,0:T(8,128)(2,1)} %param.12) | copy-start | bytes 11010052
  15.3 10.5 %collective-permute-start.5 = (bf16[256,1024]{1,0:T(8,128)(2,1)S(1)}, bf16[256,1024]{1,0:T(8,128)(2,1)S(1)}, u32[]{:S(2)}, u32[]{:S(2)}) collective-permute-start(bf16[256,1024]{1,0:T(8,128)(2,1)S(1)} %get-tuple-element.48.refs_0_), channel_id=1, source_target_pairs={{0,8},{1,3},{2,10},{3,5},{4,12},{5,7},{6,14},{7,1},{8,16},{9,11},{... | collective-permute-start | bytes 1572872 | tf_op jit(solution)/shard_map/ppermute | solution.py:42
  17.0 9.2 %collective-permute-start.7 = (bf16[256,1024]{1,0:T(8,128)(2,1)S(1)}, bf16[256,1024]{1,0:T(8,128)(2,1)S(1)}, u32[]{:S(2)}, u32[]{:S(2)}) collective-permute-start(bf16[256,1024]{1,0:T(8,128)(2,1)S(1)} %get-tuple-element.49.refs_4_), channel_id=1, source_target_pairs={{8,0},{3,1},{10,2},{5,3},{12,4},{7,5},{14,6},{1,7},{16,8},{11,9},{... | collective-permute-start | bytes 1572872 | tf_op jit(solution)/shard_map/ppermute | solution.py:42
  18.7 31.5 %collective-permute-start.12 = (bf16[448,4096]{1,0:T(8,128)(2,1)S(1)}, bf16[448,4096]{1,0:T(8,128)(2,1)S(1)}, u32[]{:S(2)}, u32[]{:S(2)}) collective-permute-start(bf16[448,4096]{1,0:T(8,128)(2,1)S(1)} %bitcast.28), channel_id=1, source_target_pairs={{0,1},{1,0},{2,3},{3,2},{4,5},{5,4},{6,7},{7,6},{8,9},{9,8},{10,11... | collective-permute-start | bytes 11010056 | tf_op jit(solution)/shard_map/ppermute | solution.py:239
  18.7 15.6 %collective-permute-start.4 = (bf16[256,1024]{1,0:T(8,128)(2,1)S(1)}, bf16[256,1024]{1,0:T(8,128)(2,1)S(1)}, u32[]{:S(2)}, u32[]{:S(2)}) collective-permute-start(bf16[256,1024]{1,0:T(8,128)(2,1)S(1)} %get-tuple-element.48.refs_0_), channel_id=1, source_target_pairs={{8,0},{3,1},{10,2},{5,3},{12,4},{7,5},{14,6},{1,7},{16,8},{11,9},{... | collective-permute-start | bytes 1572872 | tf_op jit(solution)/shard_map/ppermute | solution.py:42
  20.5 13.8 %collective-permute-start.9 = (bf16[256,1024]{1,0:T(8,128)(2,1)S(1)}, bf16[256,1024]{1,0:T(8,128)(2,1)S(1)}, u32[]{:S(2)}, u32[]{:S(2)}) collective-permute-start(bf16[256,1024]{1,0:T(8,128)(2,1)S(1)} %get-tuple-element.49.refs_4_), channel_id=1, source_target_pairs={{0,8},{1,3},{2,10},{3,5},{4,12},{5,7},{6,14},{7,1},{8,16},{9,11},{... | collective-permute-start | bytes 1572872 | tf_op jit(solution)/shard_map/ppermute | solution.py:42
  25.8 11.2 %collective-permute-start.6 = (bf16[256,1024]{1,0:T(8,128)(2,1)S(1)}, bf16[256,1024]{1,0:T(8,128)(2,1)S(1)}, u32[]{:S(2)}, u32[]{:S(2)}) collective-permute-start(bf16[256,1024]{1,0:T(8,128)(2,1)S(1)} %collective-permute-done.5.refs_3_), channel_id=1, source_target_pairs={{0,8},{1,3},{2,10},{3,5},{4,12},{5,7},{6,14},{7,1},{8,16},{9,11},{... | collective-permute-start | bytes 1572872 | tf_op jit(solution)/shard_map/ppermute | solution.py:42
  26.2 11.2 %collective-permute-start.8 = (bf16[256,1024]{1,0:T(8,128)(2,1)S(1)}, bf16[256,1024]{1,0:T(8,128)(2,1)S(1)}, u32[]{:S(2)}, u32[]{:S(2)}) collective-permute-start(bf16[256,1024]{1,0:T(8,128)(2,1)S(1)} %collective-permute-done.7.refs_5_), channel_id=1, source_target_pairs={{8,0},{3,1},{10,2},{5,3},{12,4},{7,5},{14,6},{1,7},{16,8},{11,9},{... | collective-permute-start | bytes 1572872 | tf_op jit(solution)/shard_map/ppermute | solution.py:42
  40.3 4.4 %collective-permute-start.10 = (bf16[512,2048]{1,0:T(8,128)(2,1)S(1)}, bf16[512,2048]{1,0:T(8,128)(2,1)S(1)}, u32[]{:S(2)}, u32[]{:S(2)}) collective-permute-start(bf16[512,2048]{1,0:T(8,128)(2,1)S(1)} %shard_map.77.rows), channel_id=1, source_target_pairs={{0,1},{1,0},{2,3},{3,2},{4,5},{5,4},{6,7},{7,6},{8,9},{9,8},{10,11... | collective-permute-start | bytes 6291464 | tf_op jit(solution)/shard_map/ppermute | solution.py:265
  48.6 1.6 %collective-permute-start.11 = (bf16[256,448]{1,0:T(8,128)(2,1)S(1)}, bf16[256,448]{1,0:T(8,128)(2,1)S(1)}, u32[]{:S(2)}, u32[]{:S(2)}) collective-permute-start(bf16[256,448]{1,0:T(8,128)(2,1)S(1)} %get-tuple-element.52), channel_id=1, source_target_pairs={{0,1},{1,0},{2,3},{3,2},{4,5},{5,4},{6,7},{7,6},{8,9},{9,8},{10,11... | collective-permute-start | bytes 688136 | tf_op jit(solution)/shard_map/ppermute | solution.py:278
  53.1 10.0 %collective-permute-start.13 = (bf16[256,1024]{1,0:T(8,128)(2,1)S(1)}, bf16[256,1024]{1,0:T(8,128)(2,1)S(1)}, u32[]{:S(2)}, u32[]{:S(2)}) collective-permute-start(bf16[256,1024]{1,0:T(8,128)(2,1)S(1)} %get-tuple-element.56), channel_id=1, source_target_pairs={{0,2},{1,9},{2,4},{3,11},{4,6},{5,13},{6,0},{7,15},{8,10},{9,17},{... | collective-permute-start | bytes 1572872 | tf_op jit(solution)/shard_map/ppermute | solution.py:33
  54.7 10.8 %collective-permute-start.14 = (bf16[256,1024]{1,0:T(8,128)(2,1)S(1)}, bf16[256,1024]{1,0:T(8,128)(2,1)S(1)}, u32[]{:S(2)}, u32[]{:S(2)}) collective-permute-start(bf16[256,1024]{1,0:T(8,128)(2,1)S(1)} %get-tuple-element.57), channel_id=1, source_target_pairs={{0,4},{1,17},{2,6},{3,19},{4,0},{5,21},{6,2},{7,23},{8,12},{9,25},... | collective-permute-start | bytes 1572872 | tf_op jit(solution)/shard_map/ppermute | solution.py:33
  58.0 13.0 %collective-permute-start.15 = (bf16[256,1024]{1,0:T(8,128)(2,1)S(1)}, bf16[256,1024]{1,0:T(8,128)(2,1)S(1)}, u32[]{:S(2)}, u32[]{:S(2)}) collective-permute-start(bf16[256,1024]{1,0:T(8,128)(2,1)S(1)} %get-tuple-element.58), channel_id=1, source_target_pairs={{0,6},{1,25},{2,0},{3,27},{4,2},{5,29},{6,4},{7,31},{8,14},{9,1},{... | collective-permute-start | bytes 1572872 | tf_op jit(solution)/shard_map/ppermute | solution.py:33
  72.1 6.3 %collective-permute-start.16 = (bf16[256,256]{1,0:T(8,128)(2,1)S(1)}, bf16[256,256]{1,0:T(8,128)(2,1)S(1)}, u32[]{:S(2)}, u32[]{:S(2)}) collective-permute-start(bf16[256,256]{1,0:T(8,128)(2,1)S(1)} %get-tuple-element.60), channel_id=1, source_target_pairs={{0,8},{1,3},{2,10},{3,5},{4,12},{5,7},{6,14},{7,1},{8,16},{9,11},{... | collective-permute-start | bytes 393224 | tf_op jit(solution)/shard_map/ppermute | solution.py:33
  73.8 7.1 %collective-permute-start.17 = (bf16[256,256]{1,0:T(8,128)(2,1)S(1)}, bf16[256,256]{1,0:T(8,128)(2,1)S(1)}, u32[]{:S(2)}, u32[]{:S(2)}) collective-permute-start(bf16[256,256]{1,0:T(8,128)(2,1)S(1)} %get-tuple-element.61), channel_id=1, source_target_pairs={{0,16},{1,5},{2,18},{3,7},{4,20},{5,1},{6,22},{7,3},{8,24},{9,13},... | collective-permute-start | bytes 393224 | tf_op jit(solution)/shard_map/ppermute | solution.py:33
  76.5 5.0 %collective-permute-start.18 = (bf16[256,256]{1,0:T(8,128)(2,1)S(1)}, bf16[256,256]{1,0:T(8,128)(2,1)S(1)}, u32[]{:S(2)}, u32[]{:S(2)}) collective-permute-start(bf16[256,256]{1,0:T(8,128)(2,1)S(1)} %get-tuple-element.62), channel_id=1, source_target_pairs={{0,24},{1,7},{2,26},{3,1},{4,28},{5,3},{6,30},{7,5},{8,0},{9,15},{... | collective-permute-start | bytes 393224 | tf_op jit(solution)/shard_map/ppermute | solution.py:33
  82.1 1.3 collective-permute-start.19
  (3 other events, 13.6 us)

commit v2 on v1

--- a/solution.py
+++ b/solution.py
@@ -1,3 +1,5 @@
+import functools
+
 import jax
 import jax.numpy as jnp
 from jax import lax
@@ -44,10 +46,11 @@
     left_before, right_after = send(left, on), send(right, back)
     right_before, left_after = send(right, on), send(left, back)
     left_far, right_far = send(left_before, on), send(right_after, back)
-    return [left, left_after, left_far, left_before, right, right_after, right_far, right_before]
+    return [left, left_after, left_before, right, right_after, right_before], left_far, right_far
 
 
 STEPS = (2, 1, 3)
+DOWN_STEPS = ((2,), (1, 3), (0,))
 
 
 def mm(a, b):
@@ -127,21 +130,30 @@
     return 8, total_tokens // len(PLACES)
 
 
+def hot_rows(place, slots, k, capacity, rows):
+    line = slots[:, pl.ds(pl.multiple_of((place[3] + k) % RING * rows, rows), rows)]
+    index = lax.broadcasted_iota(jnp.int32, (capacity, rows), 0)
+    return jnp.where(line == index, 1.0, 0.0).astype(jnp.bfloat16)
+
+
 def dispatch_kernel(place, slots, *refs):
-    blocks, out = refs[:-1], refs[-1]
-    rows, span = blocks[0].shape
-    capacity = out.shape[0]
-    index = lax.broadcasted_iota(jnp.int32, (capacity, rows), 0)
-    hot = []
-    for k in range(RING):
-        line = slots[:, pl.ds(pl.multiple_of((place[3] + k) % RING * rows, rows), rows)]
-        hot.append(jnp.where(line == index, 1.0, 0.0).astype(jnp.bfloat16))
-    for side in range(2):
+    outs = refs[-2:]
+    rows, span = refs[0].shape
+    hot = [hot_rows(place, slots, k, outs[0].shape[0], rows) for k in (0, 1, 3)]
+    for side, out in enumerate(outs):
+        blocks = refs[3 * side : 3 * side + 3]
         for n in range(0, span, 256):
-            acc = mm(hot[0], blocks[side * RING][:, n : n + 256])
-            for k in range(1, RING):
-                acc = acc + mm(hot[k], blocks[side * RING + k][:, n : n + 256])
-            out[:, side * span + n : side * span + n + 256] = acc.astype(jnp.bfloat16)
+            acc = mm(hot[0], blocks[0][:, n : n + 256])
+            acc = acc + mm(hot[1], blocks[1][:, n : n + 256]) + mm(hot[2], blocks[2][:, n : n + 256])
+            out[:, n : n + 256] = acc.astype(jnp.bfloat16)
+
+
+def finish_kernel(place, slots, part, block, out):
+    rows, span = block.shape
+    hot = hot_rows(place, slots, 2, out.shape[0], rows)
+    for n in range(0, span, 256):
+        acc = part[:, n : n + 256].astype(jnp.float32) + mm(hot, block[:, n : n + 256])
+        out[:, n : n + 256] = acc.astype(jnp.bfloat16)
 
 
 def turn_kernel(place, gate, up, out):
@@ -150,33 +162,32 @@
     out[:, units:] = up[...].T
 
 
-def near_kernel(place, rows, both, out):
-    out[...] = mm(rows[...], both[...])
-
-
-def far_kernel(place, rows, both, near, live, keep, give, hidden):
-    half_rows, units = keep.shape
+def near_kernel(place, left, right, both, out):
+    cut = left.shape[1]
+    out[...] = mm(left[...], both[:cut, :]) + mm(right[...], both[cut:, :])
+
+
+def far_kernel(place, left, right, both, near, live, out):
+    cut, units = left.shape[1], out.shape[1]
     block = lax.broadcasted_iota(jnp.int32, (1, units), 1) // BLK
     kept = jnp.zeros((1, units), jnp.float32)
     for k in range(units // BLK):
         kept = jnp.where(block == k, live[0, k].astype(jnp.float32), kept)
-    value = near[...] + mm(rows[...], both[...])
+    value = near[...] + (mm(left[...], both[:cut, :]) + mm(right[...], both[cut:, :]))
     gate_val, up_val = value[:, :units], value[:, units:]
-    hidden[...] = (gate_val / (1.0 + jnp.exp(-gate_val)) * up_val * kept).astype(jnp.bfloat16)
-    for out, core in ((keep, place[0]), (give, 1 - place[0])):
-        out[...] = hidden[pl.ds(pl.multiple_of(core * half_rows, half_rows), half_rows), :]
-
-
-def down_kernel(place, near, far, w_near, w_far, weight, *outs):
+    out[...] = (gate_val / (1.0 + jnp.exp(-gate_val)) * up_val * kept).astype(jnp.bfloat16)
+
+
+def down_kernel(steps, place, near, far, w_near, w_far, weight, *outs):
     rows, span = outs[0].shape
     col = span // RING
     scale = weight[pl.ds(pl.multiple_of(place[0] * rows, rows), rows), :]
-    for d in range(RING):
+    for d, out in zip(steps, outs):
         for j in range(RING):
             site = (place[2] + d) % RING * place[4] + j * place[5]
             cols = pl.ds(pl.multiple_of(site * col, col), col)
             value = mm(near[...], w_near[:, cols]) + mm(far[...], w_far[:, cols])
-            outs[d][:, j * col : (j + 1) * col] = (value * scale).astype(jnp.bfloat16)
+            out[:, j * col : (j + 1) * col] = (value * scale).astype(jnp.bfloat16)
 
 
 def total(refs):
@@ -244,7 +255,6 @@
     )
     line = call(lines_kernel, where, ins, whole(*ins), [shape((2 * RING * own_tokens, half // 2), bf16)] * 2)
     left, right, slots, slot_weight, spread = lax.optimization_barrier((*line, *routed))
-    ins = (slots, *relay(1, left, right))
     cut = 512
     turned = pl.pallas_call(
         turn_kernel,
@@ -257,29 +267,46 @@
         compiler_params=LIMIT,
         cost_estimate=pl.CostEstimate(flops=10**9, bytes_accessed=4 * 2**20, transcendentals=0),
     )(where, w_gate[0].T, w_up[0].T)
-    slots, turned = lax.optimization_barrier((ins[0], turned))
-    ins = (slots, *ins[1:])
-    near_in = call(
-        dispatch_kernel, where, ins, whole(*ins), [shape((capacity, half), bf16)], flops=2 * capacity * total_tokens * half
-    )[0]
-    far_in = lax.ppermute(near_in, "neuron", PARTNER)
+    blocks, left_far, right_far = relay(1, left, right)
+    slots, turned = lax.optimization_barrier((slots, turned))
+    ins = (slots, *blocks)
+    parts = call(
+        dispatch_kernel, where, ins, whole(*ins), [shape((capacity, half // 2), bf16)] * 2, flops=capacity * total_tokens * half
+    )
+    near_in, far_in = [], []
+    for part, block in ((parts[0], left_far), (parts[1], right_far)):
+        ins = (slots, part, block)
+        near_in += call(finish_kernel, where, ins, whole(*ins), [shape((capacity, half // 2), bf16)], flops=capacity**2 * half)
+        far_in.append(lax.ppermute(near_in[-1], "neuron", PARTNER))
     near_half = pl.BlockSpec((half, 2 * units), lambda i, s: (s[0], 0))
     far_half = pl.BlockSpec((half, 2 * units), lambda i, s: (1 - s[0], 0))
     sums = call(
-        near_kernel, where, (near_in, turned), [*whole(near_in), near_half],
+        near_kernel, where, (*near_in, turned), [*whole(*near_in), near_half],
         [shape((capacity, 2 * units), jnp.float32)], flops=4 * capacity * half * units,
-    )
+    )[0]
     rows = capacity // 2
-    hidden, given = call(
-        far_kernel, where, (far_in, turned, *sums, block_live),
-        [*whole(far_in), far_half, *whole(*sums), pl.BlockSpec(memory_space=pltpu.SMEM)],
-        [shape((rows, units), bf16)] * 2, [pltpu.VMEM((capacity, units), bf16)], flops=4 * capacity * half * units,
-    )
+
+    def far_rows(which):
+        def half_of(span):
+            return pl.BlockSpec((rows, span), lambda i, s: (which(s[0]), 0))
+
+        return call(
+            far_kernel, where, (*far_in, turned, sums, block_live),
+            [half_of(half // 2), half_of(half // 2), far_half, half_of(2 * units), pl.BlockSpec(memory_space=pltpu.SMEM)],
+            [shape((rows, units), bf16)], flops=2 * capacity * half * units,
+        )[0]
+
+    given = far_rows(lambda c: 1 - c)
     hidden_far = lax.ppermute(given, "neuron", PARTNER)
+    hidden = far_rows(lambda c: c)
     ins = (hidden, hidden_far, w_down[0], down_far, slot_weight)
-    pieces = call(
-        down_kernel, where, ins, whole(*ins), [shape((rows, width // RING), bf16)] * RING, flops=4 * capacity * half * units
-    )
+    pieces = {}
+    for steps in DOWN_STEPS:
+        outs = call(
+            functools.partial(down_kernel, steps), where, ins, whole(*ins),
+            [shape((rows, width // RING), bf16)] * len(steps), flops=len(steps) * capacity * half * units,
+        )
+        pieces.update(zip(steps, outs))
     ins = ring(0, pieces, False)
     pieces = call(
         middle_kernel, where, ins, whole(*ins), [shape((rows, 2 * col), bf16)] * RING,

time: 137 us -> 132 us (0.964)
  waiting for transfers between devices: 35.4 us -> 28 us
  Pallas kernels: 23.3 us -> 27.4 us
    pallas_call x10 -> x15, Pallas kernels: 18.1 us -> 22.2 us  [call(): pl.pallas_call(body, grid_spec=pltpu.PrefetchScalarGridSpec(num_scalar_pr...]
    ppermute x9, starting transfers between devices: 15.3 us -> 12.4 us  [ring(): lax.ppermute(blocks[d], 'neuron', [(t, s) for s, t in pairs] if back else...]
    ppermute x9, waiting for transfers between devices: 21.5 us -> 19 us  [ring(): lax.ppermute(blocks[d], 'neuron', [(t, s) for s, t in pairs] if back else...]
    ppermute x6, waiting for transfers between devices: 8.26 us -> 6.03 us  [send(): return lax.ppermute(value, 'neuron', pairs)]
    ppermute x6, starting transfers between devices: 8.58 us -> 10 us  [send(): return lax.ppermute(value, 'neuron', pairs)]
    ppermute x1, waiting for transfers between devices: 1.4 us -> 0.01 us  [per_device(): hidden_far = lax.ppermute(given, 'neuron', PARTNER)]
  transfers between devices with their start and end apart: 20 -> 21, of which waited for: 15 -> 11; matrix products, arithmetic and copies ran while one was open for 0% -> 0% of each run, Pallas kernels for 12% -> 18%
where the time goes in v2:
time: 132 us; the launch traced here: 130 us
  blocking collectives  48 us (36%)
  waiting for transfers between devices  28 us (21%)
  Pallas kernels  27.4 us (21%)
  starting transfers between devices  23.7 us (18%)
  local copies, waits for them, and re-layouts  2.18 us (2%)
    pallas_call x15, Pallas kernels, call(): pl.pallas_call(body, grid_spec=pltpu.PrefetchScalarGridSpec(num_scalar_pr...  22.2 us
    all_to_all x1, blocking collectives, per_device(): lax.all_to_all(placed.reshape(planes, members * share, col), 'expert', 0,...  20.4 us
    ppermute x9, waiting for transfers between devices, ring(): lax.ppermute(blocks[d], 'neuron', [(t, s) for s, t in pairs] if back else...  19 us
    all_to_all x1, blocking collectives, per_device(): every = lax.all_to_all(copies, 'expert', 0, 0, tiled=True)  14.8 us
    all_to_all x1, blocking collectives, per_device(): lax.all_to_all(mixed.reshape(members, share, col), 'neuron', 0, 0, tiled=...  12.7 us
    ppermute x9, starting transfers between devices, ring(): lax.ppermute(blocks[d], 'neuron', [(t, s) for s, t in pairs] if back else...  12.4 us
    ppermute x6, starting transfers between devices, send(): return lax.ppermute(value, 'neuron', pairs)  10 us
    ppermute x6, waiting for transfers between devices, send(): return lax.ppermute(value, 'neuron', pairs)  6.03 us
  transfers between devices with their start and end apart: 21, of which 11 were waited for; matrix products, arithmetic and copies ran while one was open for 0% of the time, Pallas kernels for 18%

profile of v2, /device:TPU:2, one launch (start us, length us, event | category | flops | bytes accessed | tf_op | source)
XLA Modules:
  0.0 129.6 jit_solution(9820106168249328296)
XLA Ops:
  0.1 1.7 %collective-permute-done.theirs = bf16[32,4096]{1,0:T(8,128)(2,1)S(1)} collective-permute-done((bf16[32,4096]{1,0:T(8,128)(2,1)}, bf16[32,4096]{1,0:T(8,128)(2,1)S(1)}, u32[]{:S(2)}, u32[]{:S(2)}) %collective-permute-start) | collective-permute-done | bytes 262176 | tf_op jit(solution)/shard_map/ppermute | solution.py:245
  3.6 2.2 %collective-permute-start.1 = (bf16[64,2048]{1,0:T(8,128)(2,1)S(1)}, bf16[64,2048]{1,0:T(8,128)(2,1)S(1)}, u32[]{:S(2)}, u32[]{:S(2)}) collective-permute-start(bf16[64,2048]{1,0:T(8,128)(2,1)S(1)} %shard_map.73.refs_0_), channel_id=1, source_target_pairs={{2,0},{9,1},{4,2},{11,3},{6,4},{13,5},{0,6},{15,7},{10,8},{17,9},{... | collective-permute-start | bytes 786440 | tf_op jit(solution)/shard_map/ppermute | solution.py:35
  6.6 1.8 %collective-permute-start.3 = (bf16[64,2048]{1,0:T(8,128)(2,1)S(1)}, bf16[64,2048]{1,0:T(8,128)(2,1)S(1)}, u32[]{:S(2)}, u32[]{:S(2)}) collective-permute-start(bf16[64,2048]{1,0:T(8,128)(2,1)S(1)} %shard_map.73.refs_0_), channel_id=1, source_target_pairs={{6,0},{25,1},{0,2},{27,3},{2,4},{29,5},{4,6},{31,7},{14,8},{1,9},{... | collective-permute-start | bytes 786440 | tf_op jit(solution)/shard_map/ppermute | solution.py:35
  10.1 3.6 %collective-permute-done.2.refs_2_ = bf16[64,2048]{1,0:T(8,128)(2,1)S(1)} collective-permute-done((bf16[64,2048]{1,0:T(8,128)(2,1)S(1)}, bf16[64,2048]{1,0:T(8,128)(2,1)S(1)}, u32[]{:S(2)}, u32[]{:S(2)}) %collective-permute-start.2) | collective-permute-done | bytes 262176 | tf_op jit(solution)/shard_map/ppermute | solution.py:35
  15.5 3.1 %collective-permute-start.6 = (bf16[256,1024]{1,0:T(8,128)(2,1)S(1)}, bf16[256,1024]{1,0:T(8,128)(2,1)S(1)}, u32[]{:S(2)}, u32[]{:S(2)}) collective-permute-start(bf16[256,1024]{1,0:T(8,128)(2,1)S(1)} %get-tuple-element.47.refs_3_), channel_id=1, source_target_pairs={{8,0},{3,1},{10,2},{5,3},{12,4},{7,5},{14,6},{1,7},{16,8},{11,9},{... | collective-permute-start | bytes 1572872 | tf_op jit(solution)/shard_map/ppermute | solution.py:44
  18.6 3.2 %collective-permute-start.4 = (bf16[256,1024]{1,0:T(8,128)(2,1)S(1)}, bf16[256,1024]{1,0:T(8,128)(2,1)S(1)}, u32[]{:S(2)}, u32[]{:S(2)}) collective-permute-start(bf16[256,1024]{1,0:T(8,128)(2,1)S(1)} %get-tuple-element.46.refs_0_), channel_id=1, source_target_pairs={{8,0},{3,1},{10,2},{5,3},{12,4},{7,5},{14,6},{1,7},{16,8},{11,9},{... | collective-permute-start | bytes 1572872 | tf_op jit(solution)/shard_map/ppermute | solution.py:44
  21.8 3.5 %collective-permute-done.6.refs_4_ = bf16[256,1024]{1,0:T(8,128)(2,1)S(1)} collective-permute-done((bf16[256,1024]{1,0:T(8,128)(2,1)S(1)}, bf16[256,1024]{1,0:T(8,128)(2,1)S(1)}, u32[]{:S(2)}, u32[]{:S(2)}) %collective-permute-start.6) | collective-permute-done | bytes 524320 | tf_op jit(solution)/shard_map/ppermute | solution.py:44
  25.3 3.7 %collective-permute-start.10 = (bf16[256,1024]{1,0:T(8,128)(2,1)S(1)}, bf16[256,1024]{1,0:T(8,128)(2,1)S(1)}, u32[]{:S(2)}, u32[]{:S(2)}) collective-permute-start(bf16[256,1024]{1,0:T(8,128)(2,1)S(1)} %collective-permute-done.6.refs_4_), channel_id=1, source_target_pairs={{8,0},{3,1},{10,2},{5,3},{12,4},{7,5},{14,6},{1,7},{16,8},{11,9},{... | collective-permute-start | bytes 1572872 | tf_op jit(solution)/shard_map/ppermute | solution.py:44
  29.0 5.2 %shard_map.76.both = bf16[4096,896]{1,0:T(8,128)(2,1)S(1)} custom-call(s32[6]{0:T(128)S(1)} %stack.27.place, bf16[448,4096]{1,0:T(8,128)(2,1)S(1)} %bitcast.30, bf16[448,4096]{1,0:T(8,128)(2,1)S(1)} %bitcast.31), custom_call_target="tpu_custom_call" | custom-call | flops 1000000000 | bytes 4194304 | tf_op jit(solution)/shard_map/pallas_call | solution.py:259
  34.6 2.3 %shard_map.77 = (bf16[512,1024]{1,0:T(8,128)(2,1)S(1)}, bf16[512,1024]{1,0:T(8,128)(2,1)S(1)}) custom-call(s32[6]{0:T(128)S(1)} %stack.27.place, s32[1,1024]{1,0:T(1,128)S(1)} %get-tuple-element.45.slots, bf16[256,1024]{1,0:T(8,128)(2,1)S(1)} %get-tuple-element.46.refs_0_, bf16[256,1024]{1,0:T(8,128)(2,1)S(1)} %collective-permute-done.4.refs_1_, ...), custom_call_target="tpu_custom_call" | custom-call | flops 1073741824 | bytes 4194304 | tf_op jit(solution)/shard_map/pallas_call | solution.py:68
  38.0 2.2 %collective-permute-done.8.block = bf16[256,1024]{1,0:T(8,128)(2,1)S(1)} collective-permute-done((bf16[256,1024]{1,0:T(8,128)(2,1)S(1)}, bf16[256,1024]{1,0:T(8,128)(2,1)S(1)}, u32[]{:S(2)}, u32[]{:S(2)}) %collective-permute-start.8) | collective-permute-done | bytes 524320 | tf_op jit(solution)/shard_map/ppermute | solution.py:44
  41.5 2.9 %shard_map.80.near = f32[512,896]{1,0:T(8,128)S(1)} custom-call(s32[6]{0:T(128)S(1)} %stack.27.place, bf16[512,1024]{1,0:T(8,128)(2,1)S(1)} %shard_map.78.left, bf16[512,1024]{1,0:T(8,128)(2,1)S(1)} %shard_map.79.right, bf16[4096,896]{1,0:T(8,128)(2,1)S(1)} %shard_map.76.both), custom_call_target="tpu_custom_call" | custom-call | flops 1879048192 | bytes 4194304 | tf_op jit(solution)/shard_map/pallas_call | solution.py:68
  44.4 2.5 %shard_map.82 = bf16[256,448]{1,0:T(8,128)(2,1)S(1)} custom-call(s32[6]{0:T(128)S(1)} %stack.27.place, bf16[512,1024]{1,0:T(8,128)(2,1)S(1)} %collective-permute-done.9.left, bf16[512,1024]{1,0:T(8,128)(2,1)S(1)} %collective-permute-done.11.right, bf16[4096,896]{1,0:T(8,128)(2,1)S(1)} %shard_map.76.both, f32[512,896]{1,0:T(8,128)S(1)} %shard_map.80.near, ...), custom_call_target="tpu_custom_call" | custom-call | flops 939524096 | bytes 4194304 | tf_op jit(solution)/shard_map/pallas_call | solution.py:68
  47.5 2.5 %shard_map.81.near = bf16[256,448]{1,0:T(8,128)(2,1)S(1)} custom-call(s32[6]{0:T(128)S(1)} %stack.27.place, bf16[512,1024]{1,0:T(8,128)(2,1)S(1)} %collective-permute-done.9.left, bf16[512,1024]{1,0:T(8,128)(2,1)S(1)} %collective-permute-done.11.right, bf16[4096,896]{1,0:T(8,128)(2,1)S(1)} %shard_map.76.both, f32[512,896]{1,0:T(8,128)S(1)} %shard_map.80.near, ...), custom_call_target="tpu_custom_call" | custom-call | flops 939524096 | bytes 4194304 | tf_op jit(solution)/shard_map/pallas_call | solution.py:68
  51.4 2.3 %collective-permute-start.15 = (bf16[256,1024]{1,0:T(8,128)(2,1)S(1)}, bf16[256,1024]{1,0:T(8,128)(2,1)S(1)}, u32[]{:S(2)}, u32[]{:S(2)}) collective-permute-start(bf16[256,1024]{1,0:T(8,128)(2,1)S(1)} %shard_map.85), channel_id=1, source_target_pairs={{0,4},{1,17},{2,6},{3,19},{4,0},{5,21},{6,2},{7,23},{8,12},{9,25},... | collective-permute-start | bytes 1572872 | tf_op jit(solution)/shard_map/ppermute | solution.py:35
  53.6 1.8 %shard_map.84 = (bf16[256,1024]{1,0:T(8,128)(2,1)S(1)}, bf16[256,1024]{1,0:T(8,128)(2,1)S(1)}) custom-call(s32[6]{0:T(128)S(1)} %stack.27.place, bf16[256,448]{1,0:T(8,128)(2,1)S(1)} %shard_map.81.near, bf16[256,448]{1,0:T(8,128)(2,1)S(1)} %collective-permute-done.12.far, bf16[448,4096]{1,0:T(8,128)(2,1)S(1)} %bitcast.28, ...), custom_call_target="tpu_custom_call" | custom-call | flops 939524096 | bytes 4194304 | tf_op jit(solution)/shard_map/pallas_call | solution.py:68
  55.5 2.1 %collective-permute-start.14 = (bf16[256,1024]{1,0:T(8,128)(2,1)S(1)}, bf16[256,1024]{1,0:T(8,128)(2,1)S(1)}, u32[]{:S(2)}, u32[]{:S(2)}) collective-permute-start(bf16[256,1024]{1,0:T(8,128)(2,1)S(1)} %get-tuple-element.53), channel_id=1, source_target_pairs={{0,2},{1,9},{2,4},{3,11},{4,6},{5,13},{6,0},{7,15},{8,10},{9,17},{... | collective-permute-start | bytes 1572872 | tf_op jit(solution)/shard_map/ppermute | solution.py:35
  58.9 3.4 %collective-permute-done.15.refs_2_ = bf16[256,1024]{1,0:T(8,128)(2,1)S(1)} collective-permute-done((bf16[256,1024]{1,0:T(8,128)(2,1)S(1)}, bf16[256,1024]{1,0:T(8,128)(2,1)S(1)}, u32[]{:S(2)}, u32[]{:S(2)}) %collective-permute-start.15) | collective-permute-done | bytes 524320 | tf_op jit(solution)/shard_map/ppermute | solution.py:35
  62.2 5.6 %collective-permute-done.14.refs_1_ = bf16[256,1024]{1,0:T(8,128)(2,1)S(1)} collective-permute-done((bf16[256,1024]{1,0:T(8,128)(2,1)S(1)}, bf16[256,1024]{1,0:T(8,128)(2,1)S(1)}, u32[]{:S(2)}, u32[]{:S(2)}) %collective-permute-start.14) | collective-permute-done | bytes 524320 | tf_op jit(solution)/shard_map/ppermute | solution.py:35
  69.0 2.5 %collective-permute-start.18 = (bf16[256,256]{1,0:T(8,128)(2,1)S(1)}, bf16[256,256]{1,0:T(8,128)(2,1)S(1)}, u32[]{:S(2)}, u32[]{:S(2)}) collective-permute-start(bf16[256,256]{1,0:T(8,128)(2,1)S(1)} %get-tuple-element.57), channel_id=1, source_target_pairs={{0,16},{1,5},{2,18},{3,7},{4,20},{5,1},{6,22},{7,3},{8,24},{9,13},... | collective-permute-start | bytes 393224 | tf_op jit(solution)/shard_map/ppermute | solution.py:35
  72.2 4.3 %collective-permute-done.17.refs_1_ = bf16[256,256]{1,0:T(8,128)(2,1)S(1)} collective-permute-done((bf16[256,256]{1,0:T(8,128)(2,1)S(1)}, bf16[256,256]{1,0:T(8,128)(2,1)S(1)}, u32[]{:S(2)}, u32[]{:S(2)}) %collective-permute-start.17) | collective-permute-done | bytes 131104 | tf_op jit(solution)/shard_map/ppermute | solution.py:35
  80.5 20.4 %all_to_all.15 = bf16[8,128,128]{2,1,0:T(8,128)(2,1)S(1)} all-to-all(bf16[8,128,128]{2,1,0:T(8,128)(2,1)S(1)} %bitcast.32), channel_id=1, replica_groups=mesh['expert'=8,'neuron'=32] {'expert'}, dimensions={0} | all-to-all | bytes 524288 | tf_op jit(solution)/shard_map/all_to_all | solution.py:321
  101.0 12.7 %all_to_all.16 = bf16[32,4,128]{2,1,0:T(4,128)(2,1)S(1)} all-to-all(bf16[32,4,128]{2,1,0:T(4,128)(2,1)S(1)} %bitcast.37), channel_id=1, replica_groups=mesh['expert'=8,'neuron'=32] {'neuron'}, dimensions={0} | all-to-all | bytes 65536 | tf_op jit(solution)/shard_map/all_to_all | solution.py:323
  113.7 14.8 %all_to_all.17 = bf16[8,128,128]{2,1,0:T(8,128)(2,1)S(1)} all-to-all(bf16[8,128,128]{2,1,0:T(8,128)(2,1)S(1)} %broadcast_in_dim.8), channel_id=1, replica_groups=mesh['expert'=8,'neuron'=32] {'expert'}, dimensions={0} | all-to-all | bytes 524288 | tf_op jit(solution)/shard_map/all_to_all | solution.py:325
  (57 shorter events, 18.8 us)
Async XLA Ops:
  0.0 8.4 %copy-start.5 = (s32[1024,2]{0,1:T(2,128)S(1)}, s32[1024,2]{0,1:T(2,128)}, u32[]{:S(2)}) copy-start(s32[1024,2]{0,1:T(2,128)} %param.9) | copy-start | bytes 24580
  0.1 1.8 %collective-permute-start = (bf16[32,4096]{1,0:T(8,128)(2,1)}, bf16[32,4096]{1,0:T(8,128)(2,1)S(1)}, u32[]{:S(2)}, u32[]{:S(2)}) collective-permute-start(bf16[32,4096]{1,0:T(8,128)(2,1)} %mine), channel_id=1, source_target_pairs={{0,1},{1,0},{2,3},{3,2},{4,5},{5,4},{6,7},{7,6},{8,9},{9,8},{10,11... | collective-permute-start | bytes 786440 | tf_op jit(solution)/shard_map/ppermute | solution.py:245
  3.4 46.7 %collective-permute-start.13 = (bf16[448,4096]{1,0:T(8,128)(2,1)S(1)}, bf16[448,4096]{1,0:T(8,128)(2,1)S(1)}, u32[]{:S(2)}, u32[]{:S(2)}) collective-permute-start(bf16[448,4096]{1,0:T(8,128)(2,1)S(1)} %bitcast.26), channel_id=1, source_target_pairs={{0,1},{1,0},{2,3},{3,2},{4,5},{5,4},{6,7},{7,6},{8,9},{9,8},{10,11... | collective-permute-start | bytes 11010056 | tf_op jit(solution)/shard_map/ppermute | solution.py:250
  3.6 6.5 %collective-permute-start.1 = (bf16[64,2048]{1,0:T(8,128)(2,1)S(1)}, bf16[64,2048]{1,0:T(8,128)(2,1)S(1)}, u32[]{:S(2)}, u32[]{:S(2)}) collective-permute-start(bf16[64,2048]{1,0:T(8,128)(2,1)S(1)} %shard_map.73.refs_0_), channel_id=1, source_target_pairs={{2,0},{9,1},{4,2},{11,3},{6,4},{13,5},{0,6},{15,7},{10,8},{17,9},{... | collective-permute-start | bytes 786440 | tf_op jit(solution)/shard_map/ppermute | solution.py:35
  5.9 7.9 %collective-permute-start.2 = (bf16[64,2048]{1,0:T(8,128)(2,1)S(1)}, bf16[64,2048]{1,0:T(8,128)(2,1)S(1)}, u32[]{:S(2)}, u32[]{:S(2)}) collective-permute-start(bf16[64,2048]{1,0:T(8,128)(2,1)S(1)} %shard_map.73.refs_0_), channel_id=1, source_target_pairs={{4,0},{17,1},{6,2},{19,3},{0,4},{21,5},{2,6},{23,7},{12,8},{25,9},... | collective-permute-start | bytes 786440 | tf_op jit(solution)/shard_map/ppermute | solution.py:35
  6.6 8.3 %collective-permute-start.3 = (bf16[64,2048]{1,0:T(8,128)(2,1)S(1)}, bf16[64,2048]{1,0:T(8,128)(2,1)S(1)}, u32[]{:S(2)}, u32[]{:S(2)}) collective-permute-start(bf16[64,2048]{1,0:T(8,128)(2,1)S(1)} %shard_map.73.refs_0_), channel_id=1, source_target_pairs={{6,0},{25,1},{0,2},{27,3},{2,4},{29,5},{4,6},{31,7},{14,8},{1,9},{... | collective-permute-start | bytes 786440 | tf_op jit(solution)/shard_map/ppermute | solution.py:35
  8.4 20.6 %copy-start.1 = (bf16[1,4096,448]{1,2,0:T(8,128)(2,1)S(1)}, bf16[1,4096,448]{1,2,0:T(8,128)(2,1)}, u32[]{:S(2)}) copy-start(bf16[1,4096,448]{1,2,0:T(8,128)(2,1)} %param.11) | copy-start | bytes 11010052
  8.4 20.6 %copy-start.2 = (bf16[1,4096,448]{1,2,0:T(8,128)(2,1)S(1)}, bf16[1,4096,448]{1,2,0:T(8,128)(2,1)}, u32[]{:S(2)}) copy-start(bf16[1,4096,448]{1,2,0:T(8,128)(2,1)} %param.12) | copy-start | bytes 11010052
  15.5 9.8 %collective-permute-start.6 = (bf16[256,1024]{1,0:T(8,128)(2,1)S(1)}, bf16[256,1024]{1,0:T(8,128)(2,1)S(1)}, u32[]{:S(2)}, u32[]{:S(2)}) collective-permute-start(bf16[256,1024]{1,0:T(8,128)(2,1)S(1)} %get-tuple-element.47.refs_3_), channel_id=1, source_target_pairs={{8,0},{3,1},{10,2},{5,3},{12,4},{7,5},{14,6},{1,7},{16,8},{11,9},{... | collective-permute-start | bytes 1572872 | tf_op jit(solution)/shard_map/ppermute | solution.py:44
  18.6 10.4 %collective-permute-start.5 = (bf16[256,1024]{1,0:T(8,128)(2,1)S(1)}, bf16[256,1024]{1,0:T(8,128)(2,1)S(1)}, u32[]{:S(2)}, u32[]{:S(2)}) collective-permute-start(bf16[256,1024]{1,0:T(8,128)(2,1)S(1)} %get-tuple-element.46.refs_0_), channel_id=1, source_target_pairs={{0,8},{1,3},{2,10},{3,5},{4,12},{5,7},{6,14},{7,1},{8,16},{9,11},{... | collective-permute-start | bytes 1572872 | tf_op jit(solution)/shard_map/ppermute | solution.py:44
  18.6 15.6 %collective-permute-start.4 = (bf16[256,1024]{1,0:T(8,128)(2,1)S(1)}, bf16[256,1024]{1,0:T(8,128)(2,1)S(1)}, u32[]{:S(2)}, u32[]{:S(2)}) collective-permute-start(bf16[256,1024]{1,0:T(8,128)(2,1)S(1)} %get-tuple-element.46.refs_0_), channel_id=1, source_target_pairs={{8,0},{3,1},{10,2},{5,3},{12,4},{7,5},{14,6},{1,7},{16,8},{11,9},{... | collective-permute-start | bytes 1572872 | tf_op jit(solution)/shard_map/ppermute | solution.py:44
  21.8 12.8 %collective-permute-start.7 = (bf16[256,1024]{1,0:T(8,128)(2,1)S(1)}, bf16[256,1024]{1,0:T(8,128)(2,1)S(1)}, u32[]{:S(2)}, u32[]{:S(2)}) collective-permute-start(bf16[256,1024]{1,0:T(8,128)(2,1)S(1)} %get-tuple-element.47.refs_3_), channel_id=1, source_target_pairs={{0,8},{1,3},{2,10},{3,5},{4,12},{5,7},{6,14},{7,1},{8,16},{9,11},{... | collective-permute-start | bytes 1572872 | tf_op jit(solution)/shard_map/ppermute | solution.py:44
  25.3 11.7 %collective-permute-start.10 = (bf16[256,1024]{1,0:T(8,128)(2,1)S(1)}, bf16[256,1024]{1,0:T(8,128)(2,1)S(1)}, u32[]{:S(2)}, u32[]{:S(2)}) collective-permute-start(bf16[256,1024]{1,0:T(8,128)(2,1)S(1)} %collective-permute-done.6.refs_4_), channel_id=1, source_target_pairs={{8,0},{3,1},{10,2},{5,3},{12,4},{7,5},{14,6},{1,7},{16,8},{11,9},{... | collective-permute-start | bytes 1572872 | tf_op jit(solution)/shard_map/ppermute | solution.py:44
  29.0 11.2 %collective-permute-start.8 = (bf16[256,1024]{1,0:T(8,128)(2,1)S(1)}, bf16[256,1024]{1,0:T(8,128)(2,1)S(1)}, u32[]{:S(2)}, u32[]{:S(2)}) collective-permute-start(bf16[256,1024]{1,0:T(8,128)(2,1)S(1)} %collective-permute-done.5.refs_2_), channel_id=1, source_target_pairs={{0,8},{1,3},{2,10},{3,5},{4,12},{5,7},{6,14},{7,1},{8,16},{9,11},{... | collective-permute-start | bytes 1572872 | tf_op jit(solution)/shard_map/ppermute | solution.py:44
  37.9 6.4 %collective-permute-start.11 = (bf16[512,1024]{1,0:T(8,128)(2,1)S(1)}, bf16[512,1024]{1,0:T(8,128)(2,1)S(1)}, u32[]{:S(2)}, u32[]{:S(2)}) collective-permute-start(bf16[512,1024]{1,0:T(8,128)(2,1)S(1)} %shard_map.79.right), channel_id=1, source_target_pairs={{0,1},{1,0},{2,3},{3,2},{4,5},{5,4},{6,7},{7,6},{8,9},{9,8},{10,11... | collective-permute-start | bytes 3145736 | tf_op jit(solution)/shard_map/ppermute | solution.py:280
  41.2 3.2 %collective-permute-start.9 = (bf16[512,1024]{1,0:T(8,128)(2,1)S(1)}, bf16[512,1024]{1,0:T(8,128)(2,1)S(1)}, u32[]{:S(2)}, u32[]{:S(2)}) collective-permute-start(bf16[512,1024]{1,0:T(8,128)(2,1)S(1)} %shard_map.78.left), channel_id=1, source_target_pairs={{0,1},{1,0},{2,3},{3,2},{4,5},{5,4},{6,7},{7,6},{8,9},{9,8},{10,11... | collective-permute-start | bytes 3145736 | tf_op jit(solution)/shard_map/ppermute | solution.py:280
  46.9 3.1 %collective-permute-start.12 = (bf16[256,448]{1,0:T(8,128)(2,1)S(1)}, bf16[256,448]{1,0:T(8,128)(2,1)S(1)}, u32[]{:S(2)}, u32[]{:S(2)}) collective-permute-start(bf16[256,448]{1,0:T(8,128)(2,1)S(1)} %shard_map.82), channel_id=1, source_target_pairs={{0,1},{1,0},{2,3},{3,2},{4,5},{5,4},{6,7},{7,6},{8,9},{9,8},{10,11... | collective-permute-start | bytes 688136 | tf_op jit(solution)/shard_map/ppermute | solution.py:300
  51.4 10.9 %collective-permute-start.15 = (bf16[256,1024]{1,0:T(8,128)(2,1)S(1)}, bf16[256,1024]{1,0:T(8,128)(2,1)S(1)}, u32[]{:S(2)}, u32[]{:S(2)}) collective-permute-start(bf16[256,1024]{1,0:T(8,128)(2,1)S(1)} %shard_map.85), channel_id=1, source_target_pairs={{0,4},{1,17},{2,6},{3,19},{4,0},{5,21},{6,2},{7,23},{8,12},{9,25},... | collective-permute-start | bytes 1572872 | tf_op jit(solution)/shard_map/ppermute | solution.py:35
  55.5 12.3 %collective-permute-start.14 = (bf16[256,1024]{1,0:T(8,128)(2,1)S(1)}, bf16[256,1024]{1,0:T(8,128)(2,1)S(1)}, u32[]{:S(2)}, u32[]{:S(2)}) collective-permute-start(bf16[256,1024]{1,0:T(8,128)(2,1)S(1)} %get-tuple-element.53), channel_id=1, source_target_pairs={{0,2},{1,9},{2,4},{3,11},{4,6},{5,13},{6,0},{7,15},{8,10},{9,17},{... | collective-permute-start | bytes 1572872 | tf_op jit(solution)/shard_map/ppermute | solution.py:35
  57.6 10.2 %collective-permute-start.16 = (bf16[256,1024]{1,0:T(8,128)(2,1)S(1)}, bf16[256,1024]{1,0:T(8,128)(2,1)S(1)}, u32[]{:S(2)}, u32[]{:S(2)}) collective-permute-start(bf16[256,1024]{1,0:T(8,128)(2,1)S(1)} %get-tuple-element.54), channel_id=1, source_target_pairs={{0,6},{1,25},{2,0},{3,27},{4,2},{5,29},{6,4},{7,31},{8,14},{9,1},{... | collective-permute-start | bytes 1572872 | tf_op jit(solution)/shard_map/ppermute | solution.py:35
  68.9 7.7 %collective-permute-start.17 = (bf16[256,256]{1,0:T(8,128)(2,1)S(1)}, bf16[256,256]{1,0:T(8,128)(2,1)S(1)}, u32[]{:S(2)}, u32[]{:S(2)}) collective-permute-start(bf16[256,256]{1,0:T(8,128)(2,1)S(1)} %get-tuple-element.56), channel_id=1, source_target_pairs={{0,8},{1,3},{2,10},{3,5},{4,12},{5,7},{6,14},{7,1},{8,16},{9,11},{... | collective-permute-start | bytes 393224 | tf_op jit(solution)/shard_map/ppermute | solution.py:35
  69.0 7.6 %collective-permute-start.18 = (bf16[256,256]{1,0:T(8,128)(2,1)S(1)}, bf16[256,256]{1,0:T(8,128)(2,1)S(1)}, u32[]{:S(2)}, u32[]{:S(2)}) collective-permute-start(bf16[256,256]{1,0:T(8,128)(2,1)S(1)} %get-tuple-element.57), channel_id=1, source_target_pairs={{0,16},{1,5},{2,18},{3,7},{4,20},{5,1},{6,22},{7,3},{8,24},{9,13},... | collective-permute-start | bytes 393224 | tf_op jit(solution)/shard_map/ppermute | solution.py:35
  71.6 5.9 %collective-permute-start.19 = (bf16[256,256]{1,0:T(8,128)(2,1)S(1)}, bf16[256,256]{1,0:T(8,128)(2,1)S(1)}, u32[]{:S(2)}, u32[]{:S(2)}) collective-permute-start(bf16[256,256]{1,0:T(8,128)(2,1)S(1)} %get-tuple-element.58), channel_id=1, source_target_pairs={{0,24},{1,7},{2,26},{3,1},{4,28},{5,3},{6,30},{7,5},{8,0},{9,15},{... | collective-permute-start | bytes 393224 | tf_op jit(solution)/shard_map/ppermute | solution.py:35
  78.2 1.3 %collective-permute-start.20 = (bf16[256,128]{1,0:T(8,128)(2,1)S(1)}, bf16[256,128]{1,0:T(8,128)(2,1)S(1)}, u32[]{:S(2)}, u32[]{:S(2)}) collective-permute-start(bf16[256,128]{1,0:T(8,128)(2,1)S(1)} %get-tuple-element.60), channel_id=1, source_target_pairs={{0,1},{1,0},{2,3},{3,2},{4,5},{5,4},{6,7},{7,6},{8,9},{9,8},{10,11... | collective-permute-start | bytes 196616 | tf_op jit(solution)/shard_map/ppermute | solution.py:319
  (4 other events, 15.8 us)

commit v3 on v2

--- a/solution.py
+++ b/solution.py
@@ -80,6 +80,10 @@
     rows = mine.shape[0]
     for source, core in ((mine, place[0]), (theirs, 1 - place[0])):
         out[pl.ds(pl.multiple_of(core * rows, rows), rows), :] = source[...]
+
+
+def copy_kernel(place, source, out):
+    out[...] = source[...]
 
 
 def lines_kernel(place, *refs):
@@ -190,35 +194,35 @@
             out[:, j * col : (j + 1) * col] = (value * scale).astype(jnp.bfloat16)
 
 
-def total(refs):
-    value = refs[0][...].astype(jnp.float32)
+def total_of(refs, block, col):
+    cols = pl.ds(pl.multiple_of(block * col, col), col)
+    value = refs[0][:, cols].astype(jnp.float32)
     for r in refs[1:]:
-        value = value + r[...].astype(jnp.float32)
-    return value
-
-
-def middle_kernel(place, *refs):
-    got, outs, part = refs[:RING], refs[RING : 2 * RING], refs[-1]
-    col = outs[0].shape[1]
-    part[...] = total(got).astype(jnp.bfloat16)
-    for k in range(RING):
-        outs[k][...] = part[:, pl.ds(pl.multiple_of((place[3] + k) % RING * col, col), col)]
-
-
-def pair_kernel(place, *refs):
-    got, outs, part = refs[:RING], refs[RING : RING + 2], refs[-1]
-    col = outs[0].shape[1]
-    part[...] = total(got).astype(jnp.bfloat16)
-    for out, core in zip(outs, (place[0], 1 - place[0])):
-        out[...] = part[:, pl.ds(pl.multiple_of(core * col, col), col)]
+        value = value + r[:, cols].astype(jnp.float32)
+    return value.astype(jnp.bfloat16)
+
+
+def middle_kernel(steps, place, *refs):
+    got, outs = refs[:RING], refs[RING:]
+    for k, out in zip(steps, outs):
+        out[...] = total_of(got, (place[3] + k) % RING, out.shape[1])
+
+
+def given_kernel(place, *refs):
+    refs[-1][...] = total_of(refs[:-1], 1 - place[0], refs[-1].shape[1])
+
+
+def placed_kernel(place, spread, *refs):
+    got, out = refs[:-1], refs[-1]
+    rows = got[0].shape[0]
+    at = pl.ds(pl.multiple_of(place[0] * rows, rows), rows)
+    out[...] = mm(spread[:, at], total_of(got, place[0], out.shape[1]))
 
 
 def last_kernel(place, spread, near, far, out):
-    rows = near.shape[0]
-    value = jnp.zeros(out.shape, jnp.float32)
-    for part, core in ((near, place[0]), (far, 1 - place[0])):
-        value = value + mm(spread[:, pl.ds(pl.multiple_of(core * rows, rows), rows)], part[...])
-    out[...] = value.astype(jnp.bfloat16)
+    rows = far.shape[0]
+    at = pl.ds(pl.multiple_of((1 - place[0]) * rows, rows), rows)
+    out[...] = (near[...] + mm(spread[:, at], far[...])).astype(jnp.bfloat16)
 
 
 def per_device(planes, tokens, route_logits, expert_ids, block_live, w_gate, w_up, w_down):
@@ -244,7 +248,10 @@
 
     theirs = lax.ppermute(tokens, "neuron", PARTNER)
     own_half = pl.BlockSpec((own_tokens, half), lambda i, s: (0, s[0]))
-    chip_rows = call(rows_kernel, where, (tokens, theirs), [own_half, own_half], [shape((2 * own_tokens, half), bf16)])[0]
+    mine = call(copy_kernel, where, (tokens,), [own_half], [shape((own_tokens, half), bf16)])[0]
+    chip_rows = call(
+        rows_kernel, where, (mine, theirs), [*whole(mine), own_half], [shape((2 * own_tokens, half), bf16)]
+    )[0]
     chip_rows, w_down, expert_ids, route_logits = lax.optimization_barrier((chip_rows, w_down, expert_ids, route_logits))
     ins = ring(0, [chip_rows] * RING, True)
     down_far = lax.ppermute(w_down[0], "neuron", PARTNER)
@@ -308,20 +315,22 @@
         )
         pieces.update(zip(steps, outs))
     ins = ring(0, pieces, False)
-    pieces = call(
-        middle_kernel, where, ins, whole(*ins), [shape((rows, 2 * col), bf16)] * RING,
-        [pltpu.VMEM((rows, width // RING), bf16)],
-    )
+    pieces = {}
+    for steps in DOWN_STEPS:
+        outs = call(
+            functools.partial(middle_kernel, steps), where, ins, whole(*ins), [shape((rows, 2 * col), bf16)] * len(steps)
+        )
+        pieces.update(zip(steps, outs))
     ins = ring(1, pieces, False)
-    mine, given = call(
-        pair_kernel, where, ins, whole(*ins), [shape((rows, col), bf16)] * 2, [pltpu.VMEM((rows, 2 * col), bf16)]
-    )
-    ins = (spread, mine, lax.ppermute(given, "neuron", PARTNER))
+    given = call(given_kernel, where, ins, whole(*ins), [shape((rows, col), bf16)])[0]
+    other = lax.ppermute(given, "neuron", PARTNER)
+    ins = (spread, *ins)
+    near_placed = call(placed_kernel, where, ins, whole(*ins), [shape((total_tokens, col), jnp.float32)])[0]
+    ins = (spread, near_placed, other)
     placed = call(last_kernel, where, ins, whole(*ins), [shape((total_tokens, col), bf16)])[0]
-    over = lax.all_to_all(placed.reshape(planes, members * share, col), "expert", 0, 0, tiled=True)
-    mixed = jnp.sum(over.astype(jnp.float32), axis=0).astype(jnp.bfloat16)
-    owned = lax.all_to_all(mixed.reshape(members, share, col), "neuron", 0, 0, tiled=True)
-    copies = jnp.broadcast_to(owned.reshape(1, members * share, col), (planes, members * share, col))
+    over = lax.all_to_all(placed, ("expert", "neuron"), 0, 0, tiled=True)
+    owned = jnp.sum(over.reshape(planes, members * share, col).astype(jnp.float32), axis=0).astype(bf16)
+    copies = jnp.broadcast_to(owned[None], (planes, members * share, col))
     every = lax.all_to_all(copies, "expert", 0, 0, tiled=True)
     every = every.reshape(planes, members, share, col).transpose(0, 2, 1, 3)
     return every.reshape(own_tokens, width)

time: 132 us -> 123 us (0.932); the launches traced: 130 us -> 123 us
  blocking collectives: 48 us -> 42.7 us
  waiting for transfers between devices: 28 us -> 23.4 us
  Pallas kernels: 27.4 us -> 29.4 us
    all_to_all x2 -> x1, blocking collectives: 33.2 us -> 28.2 us  [per_device(): over = lax.all_to_all(placed, ('expert', 'neuron'), 0, 0, tiled=True)]
    ppermute x9, waiting for transfers between devices: 19 us -> 16.9 us  [ring(): lax.ppermute(blocks[d], 'neuron', [(t, s) for s, t in pairs] if back else...]
    pallas_call x15 -> x19, Pallas kernels: 22.2 us -> 24.2 us  [call(): pl.pallas_call(body, grid_spec=pltpu.PrefetchScalarGridSpec(num_scalar_pr...]
    ppermute x1, waiting for transfers between devices: 1.73 us -> 0.07 us  [per_device(): theirs = lax.ppermute(tokens, 'neuron', PARTNER)]
  transfers between devices with their start and end apart: 21 -> 21, of which waited for: 11 -> 11; matrix products, arithmetic and copies ran while one was open for 0% -> 0% of each run, Pallas kernels for 18% -> 21%
where the time goes in v3:
time: 123 us
  blocking collectives  42.7 us (35%)
  Pallas kernels  29.4 us (24%)
  starting transfers between devices  24.4 us (20%)
  waiting for transfers between devices  23.4 us (19%)
  local copies, waits for them, and re-layouts  2.32 us (2%)
    all_to_all x1, blocking collectives, per_device(): over = lax.all_to_all(placed, ('expert', 'neuron'), 0, 0, tiled=True)  28.2 us
    pallas_call x19, Pallas kernels, call(): pl.pallas_call(body, grid_spec=pltpu.PrefetchScalarGridSpec(num_scalar_pr...  24.2 us
    ppermute x9, waiting for transfers between devices, ring(): lax.ppermute(blocks[d], 'neuron', [(t, s) for s, t in pairs] if back else...  16.9 us
    all_to_all x1, blocking collectives, per_device(): every = lax.all_to_all(copies, 'expert', 0, 0, tiled=True)  14.5 us
    ppermute x9, starting transfers between devices, ring(): lax.ppermute(blocks[d], 'neuron', [(t, s) for s, t in pairs] if back else...  12.6 us
    ppermute x6, starting transfers between devices, send(): return lax.ppermute(value, 'neuron', pairs)  10 us
    ppermute x6, waiting for transfers between devices, send(): return lax.ppermute(value, 'neuron', pairs)  6.03 us
    pallas_call x1, Pallas kernels, per_device(): pl.pallas_call(turn_kernel, grid_spec=pltpu.PrefetchScalarGridSpec(num_sc...  5.19 us
  transfers between devices with their start and end apart: 21, of which 11 were waited for; matrix products, arithmetic and copies ran while one was open for 0% of the time, Pallas kernels for 21%

profile of v3, /device:TPU:2, one launch (start us, length us, event | category | flops | bytes accessed | tf_op | source)
XLA Modules:
  0.0 122.6 jit_solution(4304637560771213052)
XLA Ops:
  3.2 1.9 %collective-permute-start.1 = (bf16[64,2048]{1,0:T(8,128)(2,1)S(1)}, bf16[64,2048]{1,0:T(8,128)(2,1)S(1)}, u32[]{:S(2)}, u32[]{:S(2)}) collective-permute-start(bf16[64,2048]{1,0:T(8,128)(2,1)S(1)} %shard_map.74.refs_0_), channel_id=1, source_target_pairs={{2,0},{9,1},{4,2},{11,3},{6,4},{13,5},{0,6},{15,7},{10,8},{17,9},{... | collective-permute-start | bytes 786440 | tf_op jit(solution)/shard_map/ppermute | solution.py:35
  6.1 1.8 %collective-permute-start.3 = (bf16[64,2048]{1,0:T(8,128)(2,1)S(1)}, bf16[64,2048]{1,0:T(8,128)(2,1)S(1)}, u32[]{:S(2)}, u32[]{:S(2)}) collective-permute-start(bf16[64,2048]{1,0:T(8,128)(2,1)S(1)} %shard_map.74.refs_0_), channel_id=1, source_target_pairs={{6,0},{25,1},{0,2},{27,3},{2,4},{29,5},{4,6},{31,7},{14,8},{1,9},{... | collective-permute-start | bytes 786440 | tf_op jit(solution)/shard_map/ppermute | solution.py:35
  7.9 1.7 %shard_map.76 = (s32[1,1024]{1,0:T(1,128)S(1)}, f32[512,1]{1,0:T(8,128)S(1)}, bf16[1024,512]{1,0:T(8,128)(2,1)S(1)}) custom-call(s32[6]{0:T(128)S(1)} %stack.27.place, s32[2,1024]{1,0:T(2,128)S(1)} %bitcast.34, f32[2,1024]{1,0:T(2,128)S(1)} %bitcast.35), custom_call_target="tpu_custom_call" | custom-call | flops 1000000000 | bytes 4194304 | tf_op jit(solution)/shard_map/pallas_call | solution.py:68
  9.6 3.6 %collective-permute-done.2.refs_2_ = bf16[64,2048]{1,0:T(8,128)(2,1)S(1)} collective-permute-done((bf16[64,2048]{1,0:T(8,128)(2,1)S(1)}, bf16[64,2048]{1,0:T(8,128)(2,1)S(1)}, u32[]{:S(2)}, u32[]{:S(2)}) %collective-permute-start.2) | collective-permute-done | bytes 262176 | tf_op jit(solution)/shard_map/ppermute | solution.py:35
  15.1 3.1 %collective-permute-start.6 = (bf16[256,1024]{1,0:T(8,128)(2,1)S(1)}, bf16[256,1024]{1,0:T(8,128)(2,1)S(1)}, u32[]{:S(2)}, u32[]{:S(2)}) collective-permute-start(bf16[256,1024]{1,0:T(8,128)(2,1)S(1)} %get-tuple-element.43.refs_3_), channel_id=1, source_target_pairs={{8,0},{3,1},{10,2},{5,3},{12,4},{7,5},{14,6},{1,7},{16,8},{11,9},{... | collective-permute-start | bytes 1572872 | tf_op jit(solution)/shard_map/ppermute | solution.py:44
  18.1 3.2 %collective-permute-start.4 = (bf16[256,1024]{1,0:T(8,128)(2,1)S(1)}, bf16[256,1024]{1,0:T(8,128)(2,1)S(1)}, u32[]{:S(2)}, u32[]{:S(2)}) collective-permute-start(bf16[256,1024]{1,0:T(8,128)(2,1)S(1)} %get-tuple-element.42.refs_0_), channel_id=1, source_target_pairs={{8,0},{3,1},{10,2},{5,3},{12,4},{7,5},{14,6},{1,7},{16,8},{11,9},{... | collective-permute-start | bytes 1572872 | tf_op jit(solution)/shard_map/ppermute | solution.py:44
  21.4 3.5 %collective-permute-done.6.refs_4_ = bf16[256,1024]{1,0:T(8,128)(2,1)S(1)} collective-permute-done((bf16[256,1024]{1,0:T(8,128)(2,1)S(1)}, bf16[256,1024]{1,0:T(8,128)(2,1)S(1)}, u32[]{:S(2)}, u32[]{:S(2)}) %collective-permute-start.6) | collective-permute-done | bytes 524320 | tf_op jit(solution)/shard_map/ppermute | solution.py:44
  24.8 3.7 %collective-permute-start.10 = (bf16[256,1024]{1,0:T(8,128)(2,1)S(1)}, bf16[256,1024]{1,0:T(8,128)(2,1)S(1)}, u32[]{:S(2)}, u32[]{:S(2)}) collective-permute-start(bf16[256,1024]{1,0:T(8,128)(2,1)S(1)} %collective-permute-done.6.refs_4_), channel_id=1, source_target_pairs={{8,0},{3,1},{10,2},{5,3},{12,4},{7,5},{14,6},{1,7},{16,8},{11,9},{... | collective-permute-start | bytes 1572872 | tf_op jit(solution)/shard_map/ppermute | solution.py:44
  28.6 5.2 %shard_map.77.both = bf16[4096,896]{1,0:T(8,128)(2,1)S(1)} custom-call(s32[6]{0:T(128)S(1)} %stack.27.place, bf16[448,4096]{1,0:T(8,128)(2,1)S(1)} %bitcast.31, bf16[448,4096]{1,0:T(8,128)(2,1)S(1)} %bitcast.32), custom_call_target="tpu_custom_call" | custom-call | flops 1000000000 | bytes 4194304 | tf_op jit(solution)/shard_map/pallas_call | solution.py:266
  34.2 2.3 %shard_map.78 = (bf16[512,1024]{1,0:T(8,128)(2,1)S(1)}, bf16[512,1024]{1,0:T(8,128)(2,1)S(1)}) custom-call(s32[6]{0:T(128)S(1)} %stack.27.place, s32[1,1024]{1,0:T(1,128)S(1)} %get-tuple-element.41.slots, bf16[256,1024]{1,0:T(8,128)(2,1)S(1)} %get-tuple-element.42.refs_0_, bf16[256,1024]{1,0:T(8,128)(2,1)S(1)} %collective-permute-done.4.refs_1_, ...), custom_call_target="tpu_custom_call" | custom-call | flops 1073741824 | bytes 4194304 | tf_op jit(solution)/shard_map/pallas_call | solution.py:68
  37.6 2.2 %collective-permute-done.8.block = bf16[256,1024]{1,0:T(8,128)(2,1)S(1)} collective-permute-done((bf16[256,1024]{1,0:T(8,128)(2,1)S(1)}, bf16[256,1024]{1,0:T(8,128)(2,1)S(1)}, u32[]{:S(2)}, u32[]{:S(2)}) %collective-permute-start.8) | collective-permute-done | bytes 524320 | tf_op jit(solution)/shard_map/ppermute | solution.py:44
  41.0 2.9 %shard_map.81.near = f32[512,896]{1,0:T(8,128)S(1)} custom-call(s32[6]{0:T(128)S(1)} %stack.27.place, bf16[512,1024]{1,0:T(8,128)(2,1)S(1)} %shard_map.79.left, bf16[512,1024]{1,0:T(8,128)(2,1)S(1)} %shard_map.80.right, bf16[4096,896]{1,0:T(8,128)(2,1)S(1)} %shard_map.77.both), custom_call_target="tpu_custom_call" | custom-call | flops 1879048192 | bytes 4194304 | tf_op jit(solution)/shard_map/pallas_call | solution.py:68
  44.0 2.5 %shard_map.83 = bf16[256,448]{1,0:T(8,128)(2,1)S(1)} custom-call(s32[6]{0:T(128)S(1)} %stack.27.place, bf16[512,1024]{1,0:T(8,128)(2,1)S(1)} %collective-permute-done.9.left, bf16[512,1024]{1,0:T(8,128)(2,1)S(1)} %collective-permute-done.11.right, bf16[4096,896]{1,0:T(8,128)(2,1)S(1)} %shard_map.77.both, f32[512,896]{1,0:T(8,128)S(1)} %shard_map.81.near, ...), custom_call_target="tpu_custom_call" | custom-call | flops 939524096 | bytes 4194304 | tf_op jit(solution)/shard_map/pallas_call | solution.py:68
  47.1 2.5 %shard_map.82.near = bf16[256,448]{1,0:T(8,128)(2,1)S(1)} custom-call(s32[6]{0:T(128)S(1)} %stack.27.place, bf16[512,1024]{1,0:T(8,128)(2,1)S(1)} %collective-permute-done.9.left, bf16[512,1024]{1,0:T(8,128)(2,1)S(1)} %collective-permute-done.11.right, bf16[4096,896]{1,0:T(8,128)(2,1)S(1)} %shard_map.77.both, f32[512,896]{1,0:T(8,128)S(1)} %shard_map.81.near, ...), custom_call_target="tpu_custom_call" | custom-call | flops 939524096 | bytes 4194304 | tf_op jit(solution)/shard_map/pallas_call | solution.py:68
  50.9 2.3 %collective-permute-start.15 = (bf16[256,1024]{1,0:T(8,128)(2,1)S(1)}, bf16[256,1024]{1,0:T(8,128)(2,1)S(1)}, u32[]{:S(2)}, u32[]{:S(2)}) collective-permute-start(bf16[256,1024]{1,0:T(8,128)(2,1)S(1)} %shard_map.86), channel_id=1, source_target_pairs={{0,4},{1,17},{2,6},{3,19},{4,0},{5,21},{6,2},{7,23},{8,12},{9,25},... | collective-permute-start | bytes 1572872 | tf_op jit(solution)/shard_map/ppermute | solution.py:35
  53.2 1.8 %shard_map.85 = (bf16[256,1024]{1,0:T(8,128)(2,1)S(1)}, bf16[256,1024]{1,0:T(8,128)(2,1)S(1)}) custom-call(s32[6]{0:T(128)S(1)} %stack.27.place, bf16[256,448]{1,0:T(8,128)(2,1)S(1)} %shard_map.82.near, bf16[256,448]{1,0:T(8,128)(2,1)S(1)} %collective-permute-done.12.far, bf16[448,4096]{1,0:T(8,128)(2,1)S(1)} %bitcast.29, ...), custom_call_target="tpu_custom_call" | custom-call | flops 939524096 | bytes 4194304 | tf_op jit(solution)/shard_map/pallas_call | solution.py:68
  55.1 2.0 %collective-permute-start.14 = (bf16[256,1024]{1,0:T(8,128)(2,1)S(1)}, bf16[256,1024]{1,0:T(8,128)(2,1)S(1)}, u32[]{:S(2)}, u32[]{:S(2)}) collective-permute-start(bf16[256,1024]{1,0:T(8,128)(2,1)S(1)} %get-tuple-element.49), channel_id=1, source_target_pairs={{0,2},{1,9},{2,4},{3,11},{4,6},{5,13},{6,0},{7,15},{8,10},{9,17},{... | collective-permute-start | bytes 1572872 | tf_op jit(solution)/shard_map/ppermute | solution.py:35
  58.5 3.3 %collective-permute-done.15.refs_2_ = bf16[256,1024]{1,0:T(8,128)(2,1)S(1)} collective-permute-done((bf16[256,1024]{1,0:T(8,128)(2,1)S(1)}, bf16[256,1024]{1,0:T(8,128)(2,1)S(1)}, u32[]{:S(2)}, u32[]{:S(2)}) %collective-permute-start.15) | collective-permute-done | bytes 524320 | tf_op jit(solution)/shard_map/ppermute | solution.py:35
  61.8 5.6 %collective-permute-done.14.refs_1_ = bf16[256,1024]{1,0:T(8,128)(2,1)S(1)} collective-permute-done((bf16[256,1024]{1,0:T(8,128)(2,1)S(1)}, bf16[256,1024]{1,0:T(8,128)(2,1)S(1)}, u32[]{:S(2)}, u32[]{:S(2)}) %collective-permute-start.14) | collective-permute-done | bytes 524320 | tf_op jit(solution)/shard_map/ppermute | solution.py:35
  68.8 2.0 %collective-permute-start.17 = (bf16[256,256]{1,0:T(8,128)(2,1)S(1)}, bf16[256,256]{1,0:T(8,128)(2,1)S(1)}, u32[]{:S(2)}, u32[]{:S(2)}) collective-permute-start(bf16[256,256]{1,0:T(8,128)(2,1)S(1)} %get-tuple-element.51), channel_id=1, source_target_pairs={{0,8},{1,3},{2,10},{3,5},{4,12},{5,7},{6,14},{7,1},{8,16},{9,11},{... | collective-permute-start | bytes 393224 | tf_op jit(solution)/shard_map/ppermute | solution.py:35
  70.8 1.3 %collective-permute-start.19 = (bf16[256,256]{1,0:T(8,128)(2,1)S(1)}, bf16[256,256]{1,0:T(8,128)(2,1)S(1)}, u32[]{:S(2)}, u32[]{:S(2)}) collective-permute-start(bf16[256,256]{1,0:T(8,128)(2,1)S(1)} %get-tuple-element.52), channel_id=1, source_target_pairs={{0,24},{1,7},{2,26},{3,1},{4,28},{5,3},{6,30},{7,5},{8,0},{9,15},{... | collective-permute-start | bytes 393224 | tf_op jit(solution)/shard_map/ppermute | solution.py:35
  72.8 1.9 %collective-permute-done.18.refs_2_ = bf16[256,256]{1,0:T(8,128)(2,1)S(1)} collective-permute-done((bf16[256,256]{1,0:T(8,128)(2,1)S(1)}, bf16[256,256]{1,0:T(8,128)(2,1)S(1)}, u32[]{:S(2)}, u32[]{:S(2)}) %collective-permute-start.18) | collective-permute-done | bytes 131104 | tf_op jit(solution)/shard_map/ppermute | solution.py:35
  78.7 28.2 %all_to_all.14 = bf16[256,4,128]{2,1,0:T(4,128)(2,1)S(1)} all-to-all(bf16[256,4,128]{2,1,0:T(4,128)(2,1)S(1)} %bitcast.33), channel_id=1, replica_groups=mesh['expert'=8,'neuron'=32] {'expert','neuron'}, dimensions={0} | all-to-all | bytes 524288 | tf_op jit(solution)/shard_map/all_to_all | solution.py:331
  107.0 14.5 %all_to_all.15 = bf16[8,128,128]{2,1,0:T(8,128)(2,1)S(1)} all-to-all(bf16[8,128,128]{2,1,0:T(8,128)(2,1)S(1)} %broadcast_in_dim.2), channel_id=1, replica_groups=mesh['expert'=8,'neuron'=32] {'expert'}, dimensions={0} | all-to-all | bytes 524288 | tf_op jit(solution)/shard_map/all_to_all | solution.py:334
  (60 shorter events, 19.2 us)
Async XLA Ops:
  0.1 1.8 %collective-permute-start = (bf16[32,4096]{1,0:T(8,128)(2,1)}, bf16[32,4096]{1,0:T(8,128)(2,1)S(1)}, u32[]{:S(2)}, u32[]{:S(2)}) collective-permute-start(bf16[32,4096]{1,0:T(8,128)(2,1)} %source), channel_id=1, source_target_pairs={{0,1},{1,0},{2,3},{3,2},{4,5},{5,4},{6,7},{7,6},{8,9},{9,8},{10,11... | collective-permute-start | bytes 786440 | tf_op jit(solution)/shard_map/ppermute | solution.py:249
  1.2 6.7 %copy-start.6 = (f32[1024,2]{0,1:T(2,128)S(1)}, f32[1024,2]{0,1:T(2,128)}, u32[]{:S(2)}) copy-start(f32[1024,2]{0,1:T(2,128)} %param.8) | copy-start | bytes 24580
  2.4 47.2 %collective-permute-start.13 = (bf16[448,4096]{1,0:T(8,128)(2,1)S(1)}, bf16[448,4096]{1,0:T(8,128)(2,1)S(1)}, u32[]{:S(2)}, u32[]{:S(2)}) collective-permute-start(bf16[448,4096]{1,0:T(8,128)(2,1)S(1)} %bitcast.27), channel_id=1, source_target_pairs={{0,1},{1,0},{2,3},{3,2},{4,5},{5,4},{6,7},{7,6},{8,9},{9,8},{10,11... | collective-permute-start | bytes 11010056 | tf_op jit(solution)/shard_map/ppermute | solution.py:257
  3.2 6.5 %collective-permute-start.1 = (bf16[64,2048]{1,0:T(8,128)(2,1)S(1)}, bf16[64,2048]{1,0:T(8,128)(2,1)S(1)}, u32[]{:S(2)}, u32[]{:S(2)}) collective-permute-start(bf16[64,2048]{1,0:T(8,128)(2,1)S(1)} %shard_map.74.refs_0_), channel_id=1, source_target_pairs={{2,0},{9,1},{4,2},{11,3},{6,4},{13,5},{0,6},{15,7},{10,8},{17,9},{... | collective-permute-start | bytes 786440 | tf_op jit(solution)/shard_map/ppermute | solution.py:35
  5.1 8.2 %collective-permute-start.2 = (bf16[64,2048]{1,0:T(8,128)(2,1)S(1)}, bf16[64,2048]{1,0:T(8,128)(2,1)S(1)}, u32[]{:S(2)}, u32[]{:S(2)}) collective-permute-start(bf16[64,2048]{1,0:T(8,128)(2,1)S(1)} %shard_map.74.refs_0_), channel_id=1, source_target_pairs={{4,0},{17,1},{6,2},{19,3},{0,4},{21,5},{2,6},{23,7},{12,8},{25,9},... | collective-permute-start | bytes 786440 | tf_op jit(solution)/shard_map/ppermute | solution.py:35
  6.1 8.3 %collective-permute-start.3 = (bf16[64,2048]{1,0:T(8,128)(2,1)S(1)}, bf16[64,2048]{1,0:T(8,128)(2,1)S(1)}, u32[]{:S(2)}, u32[]{:S(2)}) collective-permute-start(bf16[64,2048]{1,0:T(8,128)(2,1)S(1)} %shard_map.74.refs_0_), channel_id=1, source_target_pairs={{6,0},{25,1},{0,2},{27,3},{2,4},{29,5},{4,6},{31,7},{14,8},{1,9},{... | collective-permute-start | bytes 786440 | tf_op jit(solution)/shard_map/ppermute | solution.py:35
  7.9 20.6 %copy-start.1 = (bf16[1,4096,448]{1,2,0:T(8,128)(2,1)S(1)}, bf16[1,4096,448]{1,2,0:T(8,128)(2,1)}, u32[]{:S(2)}) copy-start(bf16[1,4096,448]{1,2,0:T(8,128)(2,1)} %param.11) | copy-start | bytes 11010052
  7.9 20.6 %copy-start.2 = (bf16[1,4096,448]{1,2,0:T(8,128)(2,1)S(1)}, bf16[1,4096,448]{1,2,0:T(8,128)(2,1)}, u32[]{:S(2)}) copy-start(bf16[1,4096,448]{1,2,0:T(8,128)(2,1)} %param.12) | copy-start | bytes 11010052
  15.1 9.8 %collective-permute-start.6 = (bf16[256,1024]{1,0:T(8,128)(2,1)S(1)}, bf16[256,1024]{1,0:T(8,128)(2,1)S(1)}, u32[]{:S(2)}, u32[]{:S(2)}) collective-permute-start(bf16[256,1024]{1,0:T(8,128)(2,1)S(1)} %get-tuple-element.43.refs_3_), channel_id=1, source_target_pairs={{8,0},{3,1},{10,2},{5,3},{12,4},{7,5},{14,6},{1,7},{16,8},{11,9},{... | collective-permute-start | bytes 1572872 | tf_op jit(solution)/shard_map/ppermute | solution.py:44
  18.1 10.4 %collective-permute-start.5 = (bf16[256,1024]{1,0:T(8,128)(2,1)S(1)}, bf16[256,1024]{1,0:T(8,128)(2,1)S(1)}, u32[]{:S(2)}, u32[]{:S(2)}) collective-permute-start(bf16[256,1024]{1,0:T(8,128)(2,1)S(1)} %get-tuple-element.42.refs_0_), channel_id=1, source_target_pairs={{0,8},{1,3},{2,10},{3,5},{4,12},{5,7},{6,14},{7,1},{8,16},{9,11},{... | collective-permute-start | bytes 1572872 | tf_op jit(solution)/shard_map/ppermute | solution.py:44
  18.1 15.6 %collective-permute-start.4 = (bf16[256,1024]{1,0:T(8,128)(2,1)S(1)}, bf16[256,1024]{1,0:T(8,128)(2,1)S(1)}, u32[]{:S(2)}, u32[]{:S(2)}) collective-permute-start(bf16[256,1024]{1,0:T(8,128)(2,1)S(1)} %get-tuple-element.42.refs_0_), channel_id=1, source_target_pairs={{8,0},{3,1},{10,2},{5,3},{12,4},{7,5},{14,6},{1,7},{16,8},{11,9},{... | collective-permute-start | bytes 1572872 | tf_op jit(solution)/shard_map/ppermute | solution.py:44
  21.4 12.8 %collective-permute-start.7 = (bf16[256,1024]{1,0:T(8,128)(2,1)S(1)}, bf16[256,1024]{1,0:T(8,128)(2,1)S(1)}, u32[]{:S(2)}, u32[]{:S(2)}) collective-permute-start(bf16[256,1024]{1,0:T(8,128)(2,1)S(1)} %get-tuple-element.43.refs_3_), channel_id=1, source_target_pairs={{0,8},{1,3},{2,10},{3,5},{4,12},{5,7},{6,14},{7,1},{8,16},{9,11},{... | collective-permute-start | bytes 1572872 | tf_op jit(solution)/shard_map/ppermute | solution.py:44
  24.8 11.7 %collective-permute-start.10 = (bf16[256,1024]{1,0:T(8,128)(2,1)S(1)}, bf16[256,1024]{1,0:T(8,128)(2,1)S(1)}, u32[]{:S(2)}, u32[]{:S(2)}) collective-permute-start(bf16[256,1024]{1,0:T(8,128)(2,1)S(1)} %collective-permute-done.6.refs_4_), channel_id=1, source_target_pairs={{8,0},{3,1},{10,2},{5,3},{12,4},{7,5},{14,6},{1,7},{16,8},{11,9},{... | collective-permute-start | bytes 1572872 | tf_op jit(solution)/shard_map/ppermute | solution.py:44
  28.5 11.2 %collective-permute-start.8 = (bf16[256,1024]{1,0:T(8,128)(2,1)S(1)}, bf16[256,1024]{1,0:T(8,128)(2,1)S(1)}, u32[]{:S(2)}, u32[]{:S(2)}) collective-permute-start(bf16[256,1024]{1,0:T(8,128)(2,1)S(1)} %collective-permute-done.5.refs_2_), channel_id=1, source_target_pairs={{0,8},{1,3},{2,10},{3,5},{4,12},{5,7},{6,14},{7,1},{8,16},{9,11},{... | collective-permute-start | bytes 1572872 | tf_op jit(solution)/shard_map/ppermute | solution.py:44
  37.5 6.4 %collective-permute-start.11 = (bf16[512,1024]{1,0:T(8,128)(2,1)S(1)}, bf16[512,1024]{1,0:T(8,128)(2,1)S(1)}, u32[]{:S(2)}, u32[]{:S(2)}) collective-permute-start(bf16[512,1024]{1,0:T(8,128)(2,1)S(1)} %shard_map.80.right), channel_id=1, source_target_pairs={{0,1},{1,0},{2,3},{3,2},{4,5},{5,4},{6,7},{7,6},{8,9},{9,8},{10,11... | collective-permute-start | bytes 3145736 | tf_op jit(solution)/shard_map/ppermute | solution.py:287
  40.8 3.2 %collective-permute-start.9 = (bf16[512,1024]{1,0:T(8,128)(2,1)S(1)}, bf16[512,1024]{1,0:T(8,128)(2,1)S(1)}, u32[]{:S(2)}, u32[]{:S(2)}) collective-permute-start(bf16[512,1024]{1,0:T(8,128)(2,1)S(1)} %shard_map.79.left), channel_id=1, source_target_pairs={{0,1},{1,0},{2,3},{3,2},{4,5},{5,4},{6,7},{7,6},{8,9},{9,8},{10,11... | collective-permute-start | bytes 3145736 | tf_op jit(solution)/shard_map/ppermute | solution.py:287
  46.5 3.1 %collective-permute-start.12 = (bf16[256,448]{1,0:T(8,128)(2,1)S(1)}, bf16[256,448]{1,0:T(8,128)(2,1)S(1)}, u32[]{:S(2)}, u32[]{:S(2)}) collective-permute-start(bf16[256,448]{1,0:T(8,128)(2,1)S(1)} %shard_map.83), channel_id=1, source_target_pairs={{0,1},{1,0},{2,3},{3,2},{4,5},{5,4},{6,7},{7,6},{8,9},{9,8},{10,11... | collective-permute-start | bytes 688136 | tf_op jit(solution)/shard_map/ppermute | solution.py:307
  50.9 10.9 %collective-permute-start.15 = (bf16[256,1024]{1,0:T(8,128)(2,1)S(1)}, bf16[256,1024]{1,0:T(8,128)(2,1)S(1)}, u32[]{:S(2)}, u32[]{:S(2)}) collective-permute-start(bf16[256,1024]{1,0:T(8,128)(2,1)S(1)} %shard_map.86), channel_id=1, source_target_pairs={{0,4},{1,17},{2,6},{3,19},{4,0},{5,21},{6,2},{7,23},{8,12},{9,25},... | collective-permute-start | bytes 1572872 | tf_op jit(solution)/shard_map/ppermute | solution.py:35
  55.1 12.3 %collective-permute-start.14 = (bf16[256,1024]{1,0:T(8,128)(2,1)S(1)}, bf16[256,1024]{1,0:T(8,128)(2,1)S(1)}, u32[]{:S(2)}, u32[]{:S(2)}) collective-permute-start(bf16[256,1024]{1,0:T(8,128)(2,1)S(1)} %get-tuple-element.49), channel_id=1, source_target_pairs={{0,2},{1,9},{2,4},{3,11},{4,6},{5,13},{6,0},{7,15},{8,10},{9,17},{... | collective-permute-start | bytes 1572872 | tf_op jit(solution)/shard_map/ppermute | solution.py:35
  57.1 10.2 %collective-permute-start.16 = (bf16[256,1024]{1,0:T(8,128)(2,1)S(1)}, bf16[256,1024]{1,0:T(8,128)(2,1)S(1)}, u32[]{:S(2)}, u32[]{:S(2)}) collective-permute-start(bf16[256,1024]{1,0:T(8,128)(2,1)S(1)} %get-tuple-element.50), channel_id=1, source_target_pairs={{0,6},{1,25},{2,0},{3,27},{4,2},{5,29},{6,4},{7,31},{8,14},{9,1},{... | collective-permute-start | bytes 1572872 | tf_op jit(solution)/shard_map/ppermute | solution.py:35
  68.0 6.7 %collective-permute-start.18 = (bf16[256,256]{1,0:T(8,128)(2,1)S(1)}, bf16[256,256]{1,0:T(8,128)(2,1)S(1)}, u32[]{:S(2)}, u32[]{:S(2)}) collective-permute-start(bf16[256,256]{1,0:T(8,128)(2,1)S(1)} %shard_map.89), channel_id=1, source_target_pairs={{0,16},{1,5},{2,18},{3,7},{4,20},{5,1},{6,22},{7,3},{8,24},{9,13},... | collective-permute-start | bytes 393224 | tf_op jit(solution)/shard_map/ppermute | solution.py:35
  68.8 7.1 %collective-permute-start.17 = (bf16[256,256]{1,0:T(8,128)(2,1)S(1)}, bf16[256,256]{1,0:T(8,128)(2,1)S(1)}, u32[]{:S(2)}, u32[]{:S(2)}) collective-permute-start(bf16[256,256]{1,0:T(8,128)(2,1)S(1)} %get-tuple-element.51), channel_id=1, source_target_pairs={{0,8},{1,3},{2,10},{3,5},{4,12},{5,7},{6,14},{7,1},{8,16},{9,11},{... | collective-permute-start | bytes 393224 | tf_op jit(solution)/shard_map/ppermute | solution.py:35
  70.8 5.2 %collective-permute-start.19 = (bf16[256,256]{1,0:T(8,128)(2,1)S(1)}, bf16[256,256]{1,0:T(8,128)(2,1)S(1)}, u32[]{:S(2)}, u32[]{:S(2)}) collective-permute-start(bf16[256,256]{1,0:T(8,128)(2,1)S(1)} %get-tuple-element.52), channel_id=1, source_target_pairs={{0,24},{1,7},{2,26},{3,1},{4,28},{5,3},{6,30},{7,5},{8,0},{9,15},{... | collective-permute-start | bytes 393224 | tf_op jit(solution)/shard_map/ppermute | solution.py:35
  76.5 1.3 %collective-permute-start.20 = (bf16[256,128]{1,0:T(8,128)(2,1)S(1)}, bf16[256,128]{1,0:T(8,128)(2,1)S(1)}, u32[]{:S(2)}, u32[]{:S(2)}) collective-permute-start(bf16[256,128]{1,0:T(8,128)(2,1)S(1)} %shard_map.91), channel_id=1, source_target_pairs={{0,1},{1,0},{2,3},{3,2},{4,5},{5,4},{6,7},{7,6},{8,9},{9,8},{10,11... | collective-permute-start | bytes 196616 | tf_op jit(solution)/shard_map/ppermute | solution.py:326
  (4 other events, 13.3 us)

commit v4 on v3

--- a/solution.py
+++ b/solution.py
@@ -64,7 +64,25 @@
     return [pl.BlockSpec(a.shape, lambda i, s, n=len(a.shape): (0,) * n) for a in arrays]
 
 
+def place_of():
+    n = lax.axis_index("neuron")
+    core, x, y = n & 1, (n >> 1) & (RING - 1), n >> 3
+    along_x = core == 0
+    return [
+        core, lax.axis_index("expert"), jnp.where(along_x, x, y), jnp.where(along_x, y, x),
+        jnp.where(along_x, 1, RING), jnp.where(along_x, RING, 1),
+    ]
+
+
 def call(body, place, ins, specs, outs, scratch=(), flops=10**9, steps=1):
+    cost = pl.CostEstimate(flops=flops, bytes_accessed=4 * 2**20, transcendentals=0)
+    if specs is None:
+        def inner(*refs):
+            body(place_of(), *refs)
+
+        return pl.pallas_call(
+            inner, out_shape=outs, scratch_shapes=list(scratch), compiler_params=LIMIT, cost_estimate=cost
+        )(*ins)
     return pl.pallas_call(
         body,
         grid_spec=pltpu.PrefetchScalarGridSpec(
@@ -72,7 +90,7 @@
         ),
         out_shape=outs,
         compiler_params=LIMIT,
-        cost_estimate=pl.CostEstimate(flops=flops, bytes_accessed=4 * 2**20, transcendentals=0),
+        cost_estimate=cost,
     )(place, *ins)
 
 
@@ -95,7 +113,7 @@
 
 
 def routing_kernel(place, ids, logits, slots, weight, spread):
-    total_tokens, capacity = spread.shape
+    total_tokens, capacity = ids.shape[1], spread.shape[1]
     lanes = 128
     first, second = (jnp.where(ids[k : k + 1, :] == place[1], 1.0, 0.0) for k in range(2))
     lead = 1.0 / (1.0 + jnp.exp(logits[1:2, :] - logits[0:1, :]))
@@ -119,11 +137,12 @@
     hit = slot == lax.broadcasted_iota(jnp.int32, (capacity, total_tokens), 0)
     weight[...] = jnp.sum(jnp.where(hit, share, 0.0), axis=1, keepdims=True)
     planes, own = place_counts(total_tokens)
-    each, part = own // planes, total_tokens // planes
+    rows = spread.shape[0]
+    each, part = own // planes, rows // planes
     step = 256
-    for top in range(0, total_tokens, step):
+    for top in range(0, rows, step):
         row = lax.broadcasted_iota(jnp.int32, (step, total_tokens), 0) + top
-        token = row % part // each * own + row // part * each + row % each
+        token = (row % part // each * 2 + place[0]) * own + row // part * each + row % each
         column = lax.broadcasted_iota(jnp.int32, (step, total_tokens), 1)
         mine = jnp.sum(jnp.where(token == column, slot.astype(jnp.float32), 0.0), axis=1, keepdims=True)
         index = lax.broadcasted_iota(jnp.int32, (step, capacity), 1)
@@ -156,8 +175,7 @@
     rows, span = block.shape
     hot = hot_rows(place, slots, 2, out.shape[0], rows)
     for n in range(0, span, 256):
-        acc = part[:, n : n + 256].astype(jnp.float32) + mm(hot, block[:, n : n + 256])
-        out[:, n : n + 256] = acc.astype(jnp.bfloat16)
+        out[:, n : n + 256] = part[:, n : n + 256] + mm(hot, block[:, n : n + 256]).astype(jnp.bfloat16)
 
 
 def turn_kernel(place, gate, up, out):
@@ -167,8 +185,10 @@
 
 
 def near_kernel(place, left, right, both, out):
-    cut = left.shape[1]
-    out[...] = mm(left[...], both[:cut, :]) + mm(right[...], both[cut:, :])
+    cut, units = left.shape[1], out.shape[1]
+    for n in range(0, units, 256):
+        to = min(n + 256, units)
+        out[:, n:to] = mm(left[...], both[:cut, n:to]) + mm(right[...], both[cut:, n:to])
 
 
 def far_kernel(place, left, right, both, near, live, out):
@@ -208,15 +228,17 @@
         out[...] = total_of(got, (place[3] + k) % RING, out.shape[1])
 
 
-def given_kernel(place, *refs):
-    refs[-1][...] = total_of(refs[:-1], 1 - place[0], refs[-1].shape[1])
-
-
-def placed_kernel(place, spread, *refs):
-    got, out = refs[:-1], refs[-1]
-    rows = got[0].shape[0]
+def mine_kernel(place, *refs):
+    value = refs[0][...].astype(jnp.float32)
+    for r in refs[1:-1]:
+        value = value + r[...].astype(jnp.float32)
+    refs[-1][...] = value.astype(jnp.bfloat16)
+
+
+def placed_kernel(place, spread, mine, out):
+    rows = mine.shape[0]
     at = pl.ds(pl.multiple_of(place[0] * rows, rows), rows)
-    out[...] = mm(spread[:, at], total_of(got, place[0], out.shape[1]))
+    out[...] = mm(spread[:, at], mine[...])
 
 
 def last_kernel(place, spread, near, far, out):
@@ -257,10 +279,10 @@
     down_far = lax.ppermute(w_down[0], "neuron", PARTNER)
     names = (expert_ids.T, route_logits.T)
     routed = call(
-        routing_kernel, where, names, whole(*names),
-        [shape((1, total_tokens), jnp.int32), shape((capacity, 1), jnp.float32), shape((total_tokens, capacity), bf16)],
+        routing_kernel, where, names, None,
+        [shape((1, total_tokens), jnp.int32), shape((capacity, 1), jnp.float32), shape((total_tokens // 2, capacity), bf16)],
     )
-    line = call(lines_kernel, where, ins, whole(*ins), [shape((2 * RING * own_tokens, half // 2), bf16)] * 2)
+    line = call(lines_kernel, where, ins, None, [shape((2 * RING * own_tokens, half // 2), bf16)] * 2)
     left, right, slots, slot_weight, spread = lax.optimization_barrier((*line, *routed))
     cut = 512
     turned = pl.pallas_call(
@@ -278,12 +300,12 @@
     slots, turned = lax.optimization_barrier((slots, turned))
     ins = (slots, *blocks)
     parts = call(
-        dispatch_kernel, where, ins, whole(*ins), [shape((capacity, half // 2), bf16)] * 2, flops=capacity * total_tokens * half
+        dispatch_kernel, where, ins, None, [shape((capacity, half // 2), bf16)] * 2, flops=capacity * total_tokens * half
     )
     near_in, far_in = [], []
     for part, block in ((parts[0], left_far), (parts[1], right_far)):
         ins = (slots, part, block)
-        near_in += call(finish_kernel, where, ins, whole(*ins), [shape((capacity, half // 2), bf16)], flops=capacity**2 * half)
+        near_in += call(finish_kernel, where, ins, None, [shape((capacity, half // 2), bf16)], flops=capacity**2 * half)
         far_in.append(lax.ppermute(near_in[-1], "neuron", PARTNER))
     near_half = pl.BlockSpec((half, 2 * units), lambda i, s: (s[0], 0))
     far_half = pl.BlockSpec((half, 2 * units), lambda i, s: (1 - s[0], 0))
@@ -310,7 +332,7 @@
     pieces = {}
     for steps in DOWN_STEPS:
         outs = call(
-            functools.partial(down_kernel, steps), where, ins, whole(*ins),
+            functools.partial(down_kernel, steps), where, ins, None,
             [shape((rows, width // RING), bf16)] * len(steps), flops=len(steps) * capacity * half * units,
         )
         pieces.update(zip(steps, outs))
@@ -318,21 +340,22 @@
     pieces = {}
     for steps in DOWN_STEPS:
         outs = call(
-            functools.partial(middle_kernel, steps), where, ins, whole(*ins), [shape((rows, 2 * col), bf16)] * len(steps)
+            functools.partial(middle_kernel, steps), where, ins, None, [shape((rows, 2 * col), bf16)] * len(steps)
         )
         pieces.update(zip(steps, outs))
     ins = ring(1, pieces, False)
-    given = call(given_kernel, where, ins, whole(*ins), [shape((rows, col), bf16)])[0]
-    other = lax.ppermute(given, "neuron", PARTNER)
-    ins = (spread, *ins)
-    near_placed = call(placed_kernel, where, ins, whole(*ins), [shape((total_tokens, col), jnp.float32)])[0]
+    mine = call(mine_kernel, where, ins, None, [shape((rows, 2 * col), bf16)])[0]
+    other = lax.ppermute(mine, "neuron", PARTNER)
+    ins = (spread, mine)
+    near_placed = call(placed_kernel, where, ins, None, [shape((total_tokens // 2, 2 * col), jnp.float32)])[0]
     ins = (spread, near_placed, other)
-    placed = call(last_kernel, where, ins, whole(*ins), [shape((total_tokens, col), bf16)])[0]
-    over = lax.all_to_all(placed, ("expert", "neuron"), 0, 0, tiled=True)
-    owned = jnp.sum(over.reshape(planes, members * share, col).astype(jnp.float32), axis=0).astype(bf16)
-    copies = jnp.broadcast_to(owned[None], (planes, members * share, col))
+    placed = call(last_kernel, where, ins, None, [shape((total_tokens // 2, 2 * col), bf16)])[0]
+    same_core = [[z * members + 2 * s + c for z in range(planes) for s in range(sites)] for c in range(2)]
+    over = lax.all_to_all(placed, ("expert", "neuron"), 0, 0, axis_index_groups=same_core, tiled=True)
+    owned = jnp.sum(over.reshape(planes, sites * share, 2 * col).astype(jnp.float32), axis=0).astype(bf16)
+    copies = jnp.broadcast_to(owned[None], (planes, sites * share, 2 * col))
     every = lax.all_to_all(copies, "expert", 0, 0, tiled=True)
-    every = every.reshape(planes, members, share, col).transpose(0, 2, 1, 3)
+    every = every.reshape(planes, sites, share, 2 * col).transpose(0, 2, 1, 3)
     return every.reshape(own_tokens, width)
 
 

time: 123 us -> 119 us (0.967)
  Pallas kernels: 29.4 us -> 21.3 us
  waiting for transfers between devices: 23.4 us -> 28.3 us
    pallas_call x19 -> x5, Pallas kernels: 24.2 us -> 9.03 us  [call(): pl.pallas_call(body, grid_spec=pltpu.PrefetchScalarGridSpec(num_scalar_pr...]
    pallas_call x0 -> x14, Pallas kernels: none -> 7.12 us  [call(): pl.pallas_call(inner, out_shape=outs, scratch_shapes=list(scratch), compi...]
    ppermute x9, waiting for transfers between devices: 16.9 us -> 20 us  [ring(): lax.ppermute(blocks[d], 'neuron', [(t, s) for s, t in pairs] if back else...]
    all_to_all x1, blocking collectives: 14.5 us -> 12.9 us  [per_device(): every = lax.all_to_all(copies, 'expert', 0, 0, tiled=True)]
  transfers between devices with their start and end apart: 21 -> 21, of which waited for: 11 -> 13; matrix products, arithmetic and copies ran while one was open for 0% -> 0% of each run, Pallas kernels for 21% -> 17%
where the time goes in v4:
time: 119 us; the launch traced here: 118 us
  blocking collectives  41.6 us (35%)
  waiting for transfers between devices  28.3 us (24%)
  starting transfers between devices  24.4 us (21%)
  Pallas kernels  21.3 us (18%)
  local copies, waits for them, and re-layouts  2.44 us (2%)
    all_to_all x1, blocking collectives, per_device(): lax.all_to_all(placed, ('expert', 'neuron'), 0, 0, axis_index_groups=same...  28.7 us
    ppermute x9, waiting for transfers between devices, ring(): lax.ppermute(blocks[d], 'neuron', [(t, s) for s, t in pairs] if back else...  20 us
    all_to_all x1, blocking collectives, per_device(): every = lax.all_to_all(copies, 'expert', 0, 0, tiled=True)  12.9 us
    ppermute x9, starting transfers between devices, ring(): lax.ppermute(blocks[d], 'neuron', [(t, s) for s, t in pairs] if back else...  12.5 us
    ppermute x6, starting transfers between devices, send(): return lax.ppermute(value, 'neuron', pairs)  10 us
    pallas_call x5, Pallas kernels, call(): pl.pallas_call(body, grid_spec=pltpu.PrefetchScalarGridSpec(num_scalar_pr...  9.03 us
    ppermute x6, waiting for transfers between devices, send(): return lax.ppermute(value, 'neuron', pairs)  7.13 us
    pallas_call x14, Pallas kernels, call(): pl.pallas_call(inner, out_shape=outs, scratch_shapes=list(scratch), compi...  7.12 us
  transfers between devices with their start and end apart: 21, of which 13 were waited for; matrix products, arithmetic and copies ran while one was open for 0% of the time, Pallas kernels for 17%

profile of v4, /device:TPU:2, one launch (start us, length us, event | category | flops | bytes accessed | tf_op | source)
XLA Modules:
  0.0 118.4 jit_solution(16217915460557211932)
XLA Ops:
  3.2 1.9 %collective-permute-start.1 = (bf16[64,2048]{1,0:T(8,128)(2,1)S(1)}, bf16[64,2048]{1,0:T(8,128)(2,1)S(1)}, u32[]{:S(2)}, u32[]{:S(2)}) collective-permute-start(bf16[64,2048]{1,0:T(8,128)(2,1)S(1)} %shard_map.74.refs_0_), channel_id=1, source_target_pairs={{2,0},{9,1},{4,2},{11,3},{6,4},{13,5},{0,6},{15,7},{10,8},{17,9},{... | collective-permute-start | bytes 786440 | tf_op jit(solution)/shard_map/ppermute | solution.py:35
  6.1 1.8 %collective-permute-start.3 = (bf16[64,2048]{1,0:T(8,128)(2,1)S(1)}, bf16[64,2048]{1,0:T(8,128)(2,1)S(1)}, u32[]{:S(2)}, u32[]{:S(2)}) collective-permute-start(bf16[64,2048]{1,0:T(8,128)(2,1)S(1)} %shard_map.74.refs_0_), channel_id=1, source_target_pairs={{6,0},{25,1},{0,2},{27,3},{2,4},{29,5},{4,6},{31,7},{14,8},{1,9},{... | collective-permute-start | bytes 786440 | tf_op jit(solution)/shard_map/ppermute | solution.py:35
  9.5 3.7 %collective-permute-done.2.refs_2_ = bf16[64,2048]{1,0:T(8,128)(2,1)S(1)} collective-permute-done((bf16[64,2048]{1,0:T(8,128)(2,1)S(1)}, bf16[64,2048]{1,0:T(8,128)(2,1)S(1)}, u32[]{:S(2)}, u32[]{:S(2)}) %collective-permute-start.2) | collective-permute-done | bytes 262176 | tf_op jit(solution)/shard_map/ppermute | solution.py:35
  14.5 3.1 %collective-permute-start.6 = (bf16[256,1024]{1,0:T(8,128)(2,1)S(1)}, bf16[256,1024]{1,0:T(8,128)(2,1)S(1)}, u32[]{:S(2)}, u32[]{:S(2)}) collective-permute-start(bf16[256,1024]{1,0:T(8,128)(2,1)S(1)} %get-tuple-element.43.refs_4_), channel_id=1, source_target_pairs={{8,0},{3,1},{10,2},{5,3},{12,4},{7,5},{14,6},{1,7},{16,8},{11,9},{... | collective-permute-start | bytes 1572872 | tf_op jit(solution)/shard_map/ppermute | solution.py:44
  17.6 3.2 %collective-permute-start.4 = (bf16[256,1024]{1,0:T(8,128)(2,1)S(1)}, bf16[256,1024]{1,0:T(8,128)(2,1)S(1)}, u32[]{:S(2)}, u32[]{:S(2)}) collective-permute-start(bf16[256,1024]{1,0:T(8,128)(2,1)S(1)} %get-tuple-element.42.refs_1_), channel_id=1, source_target_pairs={{8,0},{3,1},{10,2},{5,3},{12,4},{7,5},{14,6},{1,7},{16,8},{11,9},{... | collective-permute-start | bytes 1572872 | tf_op jit(solution)/shard_map/ppermute | solution.py:44
  20.9 3.5 %collective-permute-done.6.refs_5_ = bf16[256,1024]{1,0:T(8,128)(2,1)S(1)} collective-permute-done((bf16[256,1024]{1,0:T(8,128)(2,1)S(1)}, bf16[256,1024]{1,0:T(8,128)(2,1)S(1)}, u32[]{:S(2)}, u32[]{:S(2)}) %collective-permute-start.6) | collective-permute-done | bytes 524320 | tf_op jit(solution)/shard_map/ppermute | solution.py:44
  24.3 3.7 %collective-permute-start.10 = (bf16[256,1024]{1,0:T(8,128)(2,1)S(1)}, bf16[256,1024]{1,0:T(8,128)(2,1)S(1)}, u32[]{:S(2)}, u32[]{:S(2)}) collective-permute-start(bf16[256,1024]{1,0:T(8,128)(2,1)S(1)} %collective-permute-done.6.refs_5_), channel_id=1, source_target_pairs={{8,0},{3,1},{10,2},{5,3},{12,4},{7,5},{14,6},{1,7},{16,8},{11,9},{... | collective-permute-start | bytes 1572872 | tf_op jit(solution)/shard_map/ppermute | solution.py:44
  28.0 5.2 %shard_map.77.both = bf16[4096,896]{1,0:T(8,128)(2,1)S(1)} custom-call(s32[6]{0:T(128)S(1)} %stack.27.place, bf16[448,4096]{1,0:T(8,128)(2,1)S(1)} %bitcast.25, bf16[448,4096]{1,0:T(8,128)(2,1)S(1)} %bitcast.26), custom_call_target="tpu_custom_call" | custom-call | flops 1000000000 | bytes 4194304 | tf_op jit(solution)/shard_map/pallas_call | solution.py:288
  33.6 1.8 %shard_map.78 = (bf16[512,1024]{1,0:T(8,128)(2,1)S(1)}, bf16[512,1024]{1,0:T(8,128)(2,1)S(1)}) custom-call(s32[1,1024]{1,0:T(1,128)S(1)} %get-tuple-element.41.refs_0_, bf16[256,1024]{1,0:T(8,128)(2,1)S(1)} %get-tuple-element.42.refs_1_, bf16[256,1024]{1,0:T(8,128)(2,1)S(1)} %collective-permute-done.4.refs_2_, ...), custom_call_target="tpu_custom_call" | custom-call | flops 1073741824 | bytes 4194304 | tf_op jit(solution)/shard_map/pallas_call | solution.py:83
  36.1 3.2 %collective-permute-done.8.refs_2_ = bf16[256,1024]{1,0:T(8,128)(2,1)S(1)} collective-permute-done((bf16[256,1024]{1,0:T(8,128)(2,1)S(1)}, bf16[256,1024]{1,0:T(8,128)(2,1)S(1)}, u32[]{:S(2)}, u32[]{:S(2)}) %collective-permute-start.8) | collective-permute-done | bytes 524320 | tf_op jit(solution)/shard_map/ppermute | solution.py:44
  40.0 2.9 %shard_map.81.near = f32[512,896]{1,0:T(8,128)S(1)} custom-call(s32[6]{0:T(128)S(1)} %stack.27.place, bf16[512,1024]{1,0:T(8,128)(2,1)S(1)} %shard_map.79.left, bf16[512,1024]{1,0:T(8,128)(2,1)S(1)} %shard_map.80.right, bf16[4096,896]{1,0:T(8,128)(2,1)S(1)} %shard_map.77.both), custom_call_target="tpu_custom_call" | custom-call | flops 1879048192 | bytes 4194304 | tf_op jit(solution)/shard_map/pallas_call | solution.py:86
  42.9 2.5 %shard_map.83 = bf16[256,448]{1,0:T(8,128)(2,1)S(1)} custom-call(s32[6]{0:T(128)S(1)} %stack.27.place, bf16[512,1024]{1,0:T(8,128)(2,1)S(1)} %collective-permute-done.9.left, bf16[512,1024]{1,0:T(8,128)(2,1)S(1)} %collective-permute-done.11.right, bf16[4096,896]{1,0:T(8,128)(2,1)S(1)} %shard_map.77.both, f32[512,896]{1,0:T(8,128)S(1)} %shard_map.81.near, ...), custom_call_target="tpu_custom_call" | custom-call | flops 939524096 | bytes 4194304 | tf_op jit(solution)/shard_map/pallas_call | solution.py:86
  46.0 2.5 %shard_map.82.refs_0_ = bf16[256,448]{1,0:T(8,128)(2,1)S(1)} custom-call(s32[6]{0:T(128)S(1)} %stack.27.place, bf16[512,1024]{1,0:T(8,128)(2,1)S(1)} %collective-permute-done.9.left, bf16[512,1024]{1,0:T(8,128)(2,1)S(1)} %collective-permute-done.11.right, bf16[4096,896]{1,0:T(8,128)(2,1)S(1)} %shard_map.77.both, f32[512,896]{1,0:T(8,128)S(1)} %shard_map.81.near, ...), custom_call_target="tpu_custom_call" | custom-call | flops 939524096 | bytes 4194304 | tf_op jit(solution)/shard_map/pallas_call | solution.py:86
  49.3 2.2 %collective-permute-start.15 = (bf16[256,1024]{1,0:T(8,128)(2,1)S(1)}, bf16[256,1024]{1,0:T(8,128)(2,1)S(1)}, u32[]{:S(2)}, u32[]{:S(2)}) collective-permute-start(bf16[256,1024]{1,0:T(8,128)(2,1)S(1)} %shard_map.86), channel_id=1, source_target_pairs={{0,4},{1,17},{2,6},{3,19},{4,0},{5,21},{6,2},{7,23},{8,12},{9,25},... | collective-permute-start | bytes 1572872 | tf_op jit(solution)/shard_map/ppermute | solution.py:35
  51.5 1.3 %shard_map.85 = (bf16[256,1024]{1,0:T(8,128)(2,1)S(1)}, bf16[256,1024]{1,0:T(8,128)(2,1)S(1)}) custom-call(bf16[256,448]{1,0:T(8,128)(2,1)S(1)} %shard_map.82.refs_0_, bf16[256,448]{1,0:T(8,128)(2,1)S(1)} %collective-permute-done.12.refs_1_, bf16[448,4096]{1,0:T(8,128)(2,1)S(1)} %bitcast.23, bf16[448,4096]{1,0:T(8,128)(2,1)S(1)} %collective-permute-done.13.refs_3_, ...), custom_call_target="tpu_custom_call" | custom-call | flops 939524096 | bytes 4194304 | tf_op jit(solution)/shard_map/pallas_call | solution.py:83
  52.9 2.1 %collective-permute-start.14 = (bf16[256,1024]{1,0:T(8,128)(2,1)S(1)}, bf16[256,1024]{1,0:T(8,128)(2,1)S(1)}, u32[]{:S(2)}, u32[]{:S(2)}) collective-permute-start(bf16[256,1024]{1,0:T(8,128)(2,1)S(1)} %get-tuple-element.49), channel_id=1, source_target_pairs={{0,2},{1,9},{2,4},{3,11},{4,6},{5,13},{6,0},{7,15},{8,10},{9,17},{... | collective-permute-start | bytes 1572872 | tf_op jit(solution)/shard_map/ppermute | solution.py:35
  55.7 4.5 %collective-permute-done.15.refs_2_ = bf16[256,1024]{1,0:T(8,128)(2,1)S(1)} collective-permute-done((bf16[256,1024]{1,0:T(8,128)(2,1)S(1)}, bf16[256,1024]{1,0:T(8,128)(2,1)S(1)}, u32[]{:S(2)}, u32[]{:S(2)}) %collective-permute-start.15) | collective-permute-done | bytes 524320 | tf_op jit(solution)/shard_map/ppermute | solution.py:35
  60.2 5.6 %collective-permute-done.14.refs_1_ = bf16[256,1024]{1,0:T(8,128)(2,1)S(1)} collective-permute-done((bf16[256,1024]{1,0:T(8,128)(2,1)S(1)}, bf16[256,1024]{1,0:T(8,128)(2,1)S(1)}, u32[]{:S(2)}, u32[]{:S(2)}) %collective-permute-start.14) | collective-permute-done | bytes 524320 | tf_op jit(solution)/shard_map/ppermute | solution.py:35
  66.1 1.6 %collective-permute-start.17 = (bf16[256,256]{1,0:T(8,128)(2,1)S(1)}, bf16[256,256]{1,0:T(8,128)(2,1)S(1)}, u32[]{:S(2)}, u32[]{:S(2)}) collective-permute-start(bf16[256,256]{1,0:T(8,128)(2,1)S(1)} %get-tuple-element.51), channel_id=1, source_target_pairs={{0,8},{1,3},{2,10},{3,5},{4,12},{5,7},{6,14},{7,1},{8,16},{9,11},{... | collective-permute-start | bytes 393224 | tf_op jit(solution)/shard_map/ppermute | solution.py:35
  67.7 1.7 %collective-permute-start.19 = (bf16[256,256]{1,0:T(8,128)(2,1)S(1)}, bf16[256,256]{1,0:T(8,128)(2,1)S(1)}, u32[]{:S(2)}, u32[]{:S(2)}) collective-permute-start(bf16[256,256]{1,0:T(8,128)(2,1)S(1)} %get-tuple-element.52), channel_id=1, source_target_pairs={{0,24},{1,7},{2,26},{3,1},{4,28},{5,3},{6,30},{7,5},{8,0},{9,15},{... | collective-permute-start | bytes 393224 | tf_op jit(solution)/shard_map/ppermute | solution.py:35
  69.5 3.0 %collective-permute-done.18.refs_2_ = bf16[256,256]{1,0:T(8,128)(2,1)S(1)} collective-permute-done((bf16[256,256]{1,0:T(8,128)(2,1)S(1)}, bf16[256,256]{1,0:T(8,128)(2,1)S(1)}, u32[]{:S(2)}, u32[]{:S(2)}) %collective-permute-start.18) | collective-permute-done | bytes 131104 | tf_op jit(solution)/shard_map/ppermute | solution.py:35
  72.5 1.3 %collective-permute-done.17.refs_1_ = bf16[256,256]{1,0:T(8,128)(2,1)S(1)} collective-permute-done((bf16[256,256]{1,0:T(8,128)(2,1)S(1)}, bf16[256,256]{1,0:T(8,128)(2,1)S(1)}, u32[]{:S(2)}, u32[]{:S(2)}) %collective-permute-start.17) | collective-permute-done | bytes 131104 | tf_op jit(solution)/shard_map/ppermute | solution.py:35
  75.6 28.7 %all_to_all.14 = bf16[128,4,256]{2,1,0:T(4,128)(2,1)S(1)} all-to-all(bf16[128,4,256]{2,1,0:T(4,128)(2,1)S(1)} %all_to_all.9), channel_id=1, replica_groups={{0,2,4,6,8,10,12,14,16,18,20,22,24,26,28,30,32,34,36,38,40,42,44,46,48,..., dimensions={0} | all-to-all | bytes 524288 | tf_op jit(solution)/shard_map/all_to_all | solution.py:354
  104.4 12.9 %all_to_all.15 = bf16[8,64,256]{2,1,0:T(8,128)(2,1)S(1)} all-to-all(bf16[8,64,256]{2,1,0:T(8,128)(2,1)S(1)} %broadcast_in_dim.2), channel_id=1, replica_groups=mesh['expert'=8,'neuron'=32] {'expert'}, dimensions={0} | all-to-all | bytes 524288 | tf_op jit(solution)/shard_map/all_to_all | solution.py:357
  (62 shorter events, 14.3 us)
Async XLA Ops:
  0.1 1.8 %collective-permute-start = (bf16[32,4096]{1,0:T(8,128)(2,1)}, bf16[32,4096]{1,0:T(8,128)(2,1)S(1)}, u32[]{:S(2)}, u32[]{:S(2)}) collective-permute-start(bf16[32,4096]{1,0:T(8,128)(2,1)} %source), channel_id=1, source_target_pairs={{0,1},{1,0},{2,3},{3,2},{4,5},{5,4},{6,7},{7,6},{8,9},{9,8},{10,11... | collective-permute-start | bytes 786440 | tf_op jit(solution)/shard_map/ppermute | solution.py:271
  1.2 6.7 %copy-start.6 = (f32[1024,2]{0,1:T(2,128)S(1)}, f32[1024,2]{0,1:T(2,128)}, u32[]{:S(2)}) copy-start(f32[1024,2]{0,1:T(2,128)} %param.8) | copy-start | bytes 24580
  2.4 46.1 %collective-permute-start.13 = (bf16[448,4096]{1,0:T(8,128)(2,1)S(1)}, bf16[448,4096]{1,0:T(8,128)(2,1)S(1)}, u32[]{:S(2)}, u32[]{:S(2)}) collective-permute-start(bf16[448,4096]{1,0:T(8,128)(2,1)S(1)} %bitcast.21), channel_id=1, source_target_pairs={{0,1},{1,0},{2,3},{3,2},{4,5},{5,4},{6,7},{7,6},{8,9},{9,8},{10,11... | collective-permute-start | bytes 11010056 | tf_op jit(solution)/shard_map/ppermute | solution.py:279
  3.2 6.4 %collective-permute-start.1 = (bf16[64,2048]{1,0:T(8,128)(2,1)S(1)}, bf16[64,2048]{1,0:T(8,128)(2,1)S(1)}, u32[]{:S(2)}, u32[]{:S(2)}) collective-permute-start(bf16[64,2048]{1,0:T(8,128)(2,1)S(1)} %shard_map.74.refs_0_), channel_id=1, source_target_pairs={{2,0},{9,1},{4,2},{11,3},{6,4},{13,5},{0,6},{15,7},{10,8},{17,9},{... | collective-permute-start | bytes 786440 | tf_op jit(solution)/shard_map/ppermute | solution.py:35
  5.1 8.2 %collective-permute-start.2 = (bf16[64,2048]{1,0:T(8,128)(2,1)S(1)}, bf16[64,2048]{1,0:T(8,128)(2,1)S(1)}, u32[]{:S(2)}, u32[]{:S(2)}) collective-permute-start(bf16[64,2048]{1,0:T(8,128)(2,1)S(1)} %shard_map.74.refs_0_), channel_id=1, source_target_pairs={{4,0},{17,1},{6,2},{19,3},{0,4},{21,5},{2,6},{23,7},{12,8},{25,9},... | collective-permute-start | bytes 786440 | tf_op jit(solution)/shard_map/ppermute | solution.py:35
  6.1 8.3 %collective-permute-start.3 = (bf16[64,2048]{1,0:T(8,128)(2,1)S(1)}, bf16[64,2048]{1,0:T(8,128)(2,1)S(1)}, u32[]{:S(2)}, u32[]{:S(2)}) collective-permute-start(bf16[64,2048]{1,0:T(8,128)(2,1)S(1)} %shard_map.74.refs_0_), channel_id=1, source_target_pairs={{6,0},{25,1},{0,2},{27,3},{2,4},{29,5},{4,6},{31,7},{14,8},{1,9},{... | collective-permute-start | bytes 786440 | tf_op jit(solution)/shard_map/ppermute | solution.py:35
  7.9 20.1 %copy-start.1 = (bf16[1,4096,448]{1,2,0:T(8,128)(2,1)S(1)}, bf16[1,4096,448]{1,2,0:T(8,128)(2,1)}, u32[]{:S(2)}) copy-start(bf16[1,4096,448]{1,2,0:T(8,128)(2,1)} %param.11) | copy-start | bytes 11010052
  7.9 20.1 %copy-start.2 = (bf16[1,4096,448]{1,2,0:T(8,128)(2,1)S(1)}, bf16[1,4096,448]{1,2,0:T(8,128)(2,1)}, u32[]{:S(2)}) copy-start(bf16[1,4096,448]{1,2,0:T(8,128)(2,1)} %param.12) | copy-start | bytes 11010052
  14.5 9.8 %collective-permute-start.6 = (bf16[256,1024]{1,0:T(8,128)(2,1)S(1)}, bf16[256,1024]{1,0:T(8,128)(2,1)S(1)}, u32[]{:S(2)}, u32[]{:S(2)}) collective-permute-start(bf16[256,1024]{1,0:T(8,128)(2,1)S(1)} %get-tuple-element.43.refs_4_), channel_id=1, source_target_pairs={{8,0},{3,1},{10,2},{5,3},{12,4},{7,5},{14,6},{1,7},{16,8},{11,9},{... | collective-permute-start | bytes 1572872 | tf_op jit(solution)/shard_map/ppermute | solution.py:44
  17.6 10.4 %collective-permute-start.5 = (bf16[256,1024]{1,0:T(8,128)(2,1)S(1)}, bf16[256,1024]{1,0:T(8,128)(2,1)S(1)}, u32[]{:S(2)}, u32[]{:S(2)}) collective-permute-start(bf16[256,1024]{1,0:T(8,128)(2,1)S(1)} %get-tuple-element.42.refs_1_), channel_id=1, source_target_pairs={{0,8},{1,3},{2,10},{3,5},{4,12},{5,7},{6,14},{7,1},{8,16},{9,11},{... | collective-permute-start | bytes 1572872 | tf_op jit(solution)/shard_map/ppermute | solution.py:44
  17.6 15.6 %collective-permute-start.4 = (bf16[256,1024]{1,0:T(8,128)(2,1)S(1)}, bf16[256,1024]{1,0:T(8,128)(2,1)S(1)}, u32[]{:S(2)}, u32[]{:S(2)}) collective-permute-start(bf16[256,1024]{1,0:T(8,128)(2,1)S(1)} %get-tuple-element.42.refs_1_), channel_id=1, source_target_pairs={{8,0},{3,1},{10,2},{5,3},{12,4},{7,5},{14,6},{1,7},{16,8},{11,9},{... | collective-permute-start | bytes 1572872 | tf_op jit(solution)/shard_map/ppermute | solution.py:44
  20.9 12.8 %collective-permute-start.7 = (bf16[256,1024]{1,0:T(8,128)(2,1)S(1)}, bf16[256,1024]{1,0:T(8,128)(2,1)S(1)}, u32[]{:S(2)}, u32[]{:S(2)}) collective-permute-start(bf16[256,1024]{1,0:T(8,128)(2,1)S(1)} %get-tuple-element.43.refs_4_), channel_id=1, source_target_pairs={{0,8},{1,3},{2,10},{3,5},{4,12},{5,7},{6,14},{7,1},{8,16},{9,11},{... | collective-permute-start | bytes 1572872 | tf_op jit(solution)/shard_map/ppermute | solution.py:44
  24.3 11.2 %collective-permute-start.10 = (bf16[256,1024]{1,0:T(8,128)(2,1)S(1)}, bf16[256,1024]{1,0:T(8,128)(2,1)S(1)}, u32[]{:S(2)}, u32[]{:S(2)}) collective-permute-start(bf16[256,1024]{1,0:T(8,128)(2,1)S(1)} %collective-permute-done.6.refs_5_), channel_id=1, source_target_pairs={{8,0},{3,1},{10,2},{5,3},{12,4},{7,5},{14,6},{1,7},{16,8},{11,9},{... | collective-permute-start | bytes 1572872 | tf_op jit(solution)/shard_map/ppermute | solution.py:44
  28.0 11.2 %collective-permute-start.8 = (bf16[256,1024]{1,0:T(8,128)(2,1)S(1)}, bf16[256,1024]{1,0:T(8,128)(2,1)S(1)}, u32[]{:S(2)}, u32[]{:S(2)}) collective-permute-start(bf16[256,1024]{1,0:T(8,128)(2,1)S(1)} %collective-permute-done.5.refs_3_), channel_id=1, source_target_pairs={{0,8},{1,3},{2,10},{3,5},{4,12},{5,7},{6,14},{7,1},{8,16},{9,11},{... | collective-permute-start | bytes 1572872 | tf_op jit(solution)/shard_map/ppermute | solution.py:44
  36.0 6.9 %collective-permute-start.11 = (bf16[512,1024]{1,0:T(8,128)(2,1)S(1)}, bf16[512,1024]{1,0:T(8,128)(2,1)S(1)}, u32[]{:S(2)}, u32[]{:S(2)}) collective-permute-start(bf16[512,1024]{1,0:T(8,128)(2,1)S(1)} %shard_map.80.right), channel_id=1, source_target_pairs={{0,1},{1,0},{2,3},{3,2},{4,5},{5,4},{6,7},{7,6},{8,9},{9,8},{10,11... | collective-permute-start | bytes 3145736 | tf_op jit(solution)/shard_map/ppermute | solution.py:309
  39.7 3.2 %collective-permute-start.9 = (bf16[512,1024]{1,0:T(8,128)(2,1)S(1)}, bf16[512,1024]{1,0:T(8,128)(2,1)S(1)}, u32[]{:S(2)}, u32[]{:S(2)}) collective-permute-start(bf16[512,1024]{1,0:T(8,128)(2,1)S(1)} %shard_map.79.left), channel_id=1, source_target_pairs={{0,1},{1,0},{2,3},{3,2},{4,5},{5,4},{6,7},{7,6},{8,9},{9,8},{10,11... | collective-permute-start | bytes 3145736 | tf_op jit(solution)/shard_map/ppermute | solution.py:309
  45.4 3.1 %collective-permute-start.12 = (bf16[256,448]{1,0:T(8,128)(2,1)S(1)}, bf16[256,448]{1,0:T(8,128)(2,1)S(1)}, u32[]{:S(2)}, u32[]{:S(2)}) collective-permute-start(bf16[256,448]{1,0:T(8,128)(2,1)S(1)} %shard_map.83), channel_id=1, source_target_pairs={{0,1},{1,0},{2,3},{3,2},{4,5},{5,4},{6,7},{7,6},{8,9},{9,8},{10,11... | collective-permute-start | bytes 688136 | tf_op jit(solution)/shard_map/ppermute | solution.py:329
  49.3 10.9 %collective-permute-start.15 = (bf16[256,1024]{1,0:T(8,128)(2,1)S(1)}, bf16[256,1024]{1,0:T(8,128)(2,1)S(1)}, u32[]{:S(2)}, u32[]{:S(2)}) collective-permute-start(bf16[256,1024]{1,0:T(8,128)(2,1)S(1)} %shard_map.86), channel_id=1, source_target_pairs={{0,4},{1,17},{2,6},{3,19},{4,0},{5,21},{6,2},{7,23},{8,12},{9,25},... | collective-permute-start | bytes 1572872 | tf_op jit(solution)/shard_map/ppermute | solution.py:35
  52.9 12.9 %collective-permute-start.14 = (bf16[256,1024]{1,0:T(8,128)(2,1)S(1)}, bf16[256,1024]{1,0:T(8,128)(2,1)S(1)}, u32[]{:S(2)}, u32[]{:S(2)}) collective-permute-start(bf16[256,1024]{1,0:T(8,128)(2,1)S(1)} %get-tuple-element.49), channel_id=1, source_target_pairs={{0,2},{1,9},{2,4},{3,11},{4,6},{5,13},{6,0},{7,15},{8,10},{9,17},{... | collective-permute-start | bytes 1572872 | tf_op jit(solution)/shard_map/ppermute | solution.py:35
  55.0 10.8 %collective-permute-start.16 = (bf16[256,1024]{1,0:T(8,128)(2,1)S(1)}, bf16[256,1024]{1,0:T(8,128)(2,1)S(1)}, u32[]{:S(2)}, u32[]{:S(2)}) collective-permute-start(bf16[256,1024]{1,0:T(8,128)(2,1)S(1)} %get-tuple-element.50), channel_id=1, source_target_pairs={{0,6},{1,25},{2,0},{3,27},{4,2},{5,29},{6,4},{7,31},{8,14},{9,1},{... | collective-permute-start | bytes 1572872 | tf_op jit(solution)/shard_map/ppermute | solution.py:35
  65.8 6.7 %collective-permute-start.18 = (bf16[256,256]{1,0:T(8,128)(2,1)S(1)}, bf16[256,256]{1,0:T(8,128)(2,1)S(1)}, u32[]{:S(2)}, u32[]{:S(2)}) collective-permute-start(bf16[256,256]{1,0:T(8,128)(2,1)S(1)} %shard_map.89), channel_id=1, source_target_pairs={{0,16},{1,5},{2,18},{3,7},{4,20},{5,1},{6,22},{7,3},{8,24},{9,13},... | collective-permute-start | bytes 393224 | tf_op jit(solution)/shard_map/ppermute | solution.py:35
  66.1 7.7 %collective-permute-start.17 = (bf16[256,256]{1,0:T(8,128)(2,1)S(1)}, bf16[256,256]{1,0:T(8,128)(2,1)S(1)}, u32[]{:S(2)}, u32[]{:S(2)}) collective-permute-start(bf16[256,256]{1,0:T(8,128)(2,1)S(1)} %get-tuple-element.51), channel_id=1, source_target_pairs={{0,8},{1,3},{2,10},{3,5},{4,12},{5,7},{6,14},{7,1},{8,16},{9,11},{... | collective-permute-start | bytes 393224 | tf_op jit(solution)/shard_map/ppermute | solution.py:35
  67.7 6.1 %collective-permute-start.19 = (bf16[256,256]{1,0:T(8,128)(2,1)S(1)}, bf16[256,256]{1,0:T(8,128)(2,1)S(1)}, u32[]{:S(2)}, u32[]{:S(2)}) collective-permute-start(bf16[256,256]{1,0:T(8,128)(2,1)S(1)} %get-tuple-element.52), channel_id=1, source_target_pairs={{0,24},{1,7},{2,26},{3,1},{4,28},{5,3},{6,30},{7,5},{8,0},{9,15},{... | collective-permute-start | bytes 393224 | tf_op jit(solution)/shard_map/ppermute | solution.py:35
  73.8 1.4 %collective-permute-start.20 = (bf16[256,256]{1,0:T(8,128)(2,1)S(1)}, bf16[256,256]{1,0:T(8,128)(2,1)S(1)}, u32[]{:S(2)}, u32[]{:S(2)}) collective-permute-start(bf16[256,256]{1,0:T(8,128)(2,1)S(1)} %shard_map.90.refs_1_), channel_id=1, source_target_pairs={{0,1},{1,0},{2,3},{3,2},{4,5},{5,4},{6,7},{7,6},{8,9},{9,8},{10,11... | collective-permute-start | bytes 393224 | tf_op jit(solution)/shard_map/ppermute | solution.py:348
  (4 other events, 13.3 us)
